TPU v7x, 512 devices: a whole 4x4x16 slice. The times are simulated.
512 devices in a mesh: gz: 4 (over z_lo), gy: 16 (over z_hi, y), gx: 8 (over x, core).
Axes of the slice: x: 4, y: 4, z: 16 (z_hi: 4, z_lo: 4; z = z_hi * 4 + z_lo), core: 2. Of those that a mesh axis runs over, the one named last changes fastest.
Arguments:
- fine_now: float32 [3, 16, 256, 2048], P(None, 'gz', 'gy', 'gx'), may hold values from -6 to 6
- fine_prev: float32 [3, 16, 256, 2048], P(None, 'gz', 'gy', 'gx'), may hold values from -6 to 6
- stiffness: float32 [9, 16, 256, 2048], P(None, 'gz', 'gy', 'gx'), may hold values from 0 to 6, as said below
- metric: float32 [16, 256, 2048], P('gz', 'gy', 'gx'), may hold values from 0.7 to 1.4
- density: float32 [16, 256, 2048], P('gz', 'gy', 'gx'), may hold values from 1 to 2
- coarse_now: float32 [3, 32, 128, 1024], P(None, 'gz', 'gy', 'gx'), may hold values from -6 to 6
- coarse_prev: float32 [3, 32, 128, 1024], P(None, 'gz', 'gy', 'gx'), may hold values from -6 to 6
- coarse_stiffness: float32 [9, 32, 128, 1024], P(None, 'gz', 'gy', 'gx'), may hold values from 0 to 24, as said below
- coarse_density: float32 [32, 128, 1024], P('gz', 'gy', 'gx'), may hold values from 1.5 to 3
Outputs:
- fine_next: float32 [3, 16, 256, 2048], P(None, 'gz', 'gy', 'gx')
- coarse_next: float32 [3, 32, 128, 1024], P(None, 'gz', 'gy', 'gx')
Inputs may be any that keep to these rules, and one draw needn't show every extreme that they name: `stiffness`: channels 0 to 5 lie in [2, 6] and channels 6 to 8 in [0, 0.9]. `coarse_stiffness`: channels 0 to 5 lie in [8, 24] and channels 6 to 8 in [0, 3.6].
All inputs are finite; a program needn't handle non-finite values.
Results may differ from a plain program's by a relative error of at most 0.00002.
Values sent between devices are 32-bit elements; how exact they have to be, the bound alone decides.
A program may use at most 64 MiB of HBM per device.

v0:
```python
import jax
import jax.numpy as jnp
from jax import lax
from jax.sharding import PartitionSpec as P

ITERS = 3


TIME_STEP = 0.2


def with_halo(shard, sides, width):
    edges = {}
    for axis, dim in sides:
        size, length = (lax.axis_size(axis), shard.shape[dim])
        up = [(i, (i + 1) % size) for i in range(size - 1)]
        last = lax.slice_in_dim(shard, length - width, length, axis=dim)
        first = lax.slice_in_dim(shard, 0, width, axis=dim)
        edges[dim] = (
            lax.ppermute(last, axis, up),
            lax.ppermute(first, axis, [(b, a) for a, b in up]),
        )
    done = []
    for _, dim in sides:
        low, high = edges[dim]
        around = [(width, width) if d in done else (0, 0) for d in range(shard.ndim)]
        shard = jnp.concatenate([jnp.pad(low, around), shard, jnp.pad(high, around)], axis=dim)
        done.append(dim)
    return shard


def passed_along(shard, axis, by):
    length = lax.axis_size(axis)
    pairs = [(i, i + by) for i in range(length) if 0 <= i + by < length]
    return lax.ppermute(shard, axis, pairs)


def with_halo_2(cells, sides, width):
    for axis, dim in sides:
        count = lax.axis_size(axis)
        ends = count - 1
        head = lax.slice_in_dim(cells, 0, width, axis=dim)
        tail = lax.slice_in_dim(cells, cells.shape[dim] - width, cells.shape[dim], axis=dim)
        cells = jnp.concatenate(
            [
                lax.ppermute(tail, axis, [(i, (i + 1) % count) for i in range(ends)]),
                cells,
                lax.ppermute(head, axis, [((i + 1) % count, i) for i in range(ends)]),
            ],
            axis=dim,
        )
    return cells


def along_x(volume, inverse_step):
    return (volume[..., 1:-1, 1:-1, 2:] - volume[..., 1:-1, 1:-1, :-2]) * inverse_step


def along_y(volume, inverse_step):
    return (volume[..., 1:-1, 2:, 1:-1] - volume[..., 1:-1, :-2, 1:-1]) * inverse_step


def along_z(volume, inverse_step, stretch):
    return (volume[..., 2:, 1:-1, 1:-1] - volume[..., :-2, 1:-1, 1:-1]) * inverse_step * stretch


def stresses(padded, stiffness, stretch, inverse_step):
    disp_x, disp_y, disp_z = (padded[0], padded[1], padded[2])
    normal_x = along_x(disp_x, inverse_step)
    normal_y = along_y(disp_y, inverse_step)
    normal_z = along_z(disp_z, inverse_step, stretch)
    stress_xx = stiffness[0] * normal_x + stiffness[6] * normal_y + stiffness[7] * normal_z
    stress_yy = stiffness[6] * normal_x + stiffness[1] * normal_y + stiffness[8] * normal_z
    stress_zz = stiffness[7] * normal_x + stiffness[8] * normal_y + stiffness[2] * normal_z
    stress_yz = stiffness[3] * (
        along_z(disp_y, inverse_step, stretch) + along_y(disp_z, inverse_step)
    )
    stress_xz = stiffness[4] * (
        along_z(disp_x, inverse_step, stretch) + along_x(disp_z, inverse_step)
    )
    stress_xy = stiffness[5] * (along_y(disp_x, inverse_step) + along_x(disp_y, inverse_step))
    return jnp.stack([stress_xx, stress_yy, stress_zz, stress_yz, stress_xz, stress_xy])


def divergence(stress, stretch, inverse_step):
    total_x = (
        along_x(stress[0], inverse_step)
        + along_y(stress[5], inverse_step)
        + along_z(stress[4], inverse_step, stretch)
    )
    total_y = (
        along_x(stress[5], inverse_step)
        + along_y(stress[1], inverse_step)
        + along_z(stress[3], inverse_step, stretch)
    )
    total_z = (
        along_x(stress[4], inverse_step)
        + along_y(stress[3], inverse_step)
        + along_z(stress[2], inverse_step, stretch)
    )
    return jnp.stack([total_x, total_y, total_z])


def prolong_axis(padded, axis):
    length = padded.shape[axis] - 2
    centre = lax.slice_in_dim(padded, 1, length + 1, axis=axis)
    before = lax.slice_in_dim(padded, 0, length, axis=axis)
    behind = lax.slice_in_dim(padded, 2, length + 2, axis=axis)
    even_cells = 0.75 * centre + 0.25 * before
    odd_cells = 0.75 * centre + 0.25 * behind
    new_shape = list(centre.shape)
    new_shape[axis] = 2 * length
    return jnp.stack([even_cells, odd_cells], axis + 1).reshape(new_shape)


def prolong(padded):
    return prolong_axis(prolong_axis(padded, 1), 2)


def restrict(surface):
    row_pairs = surface.reshape(surface.shape[0], surface.shape[1] // 2, 2, surface.shape[2])
    summed = row_pairs[:, :, 0] + row_pairs[:, :, 1]
    col_pairs = summed.reshape(summed.shape[0], summed.shape[1], summed.shape[2] // 2, 2)
    return (col_pairs[..., 0] + col_pairs[..., 1]) * 0.25


def extend_edges(padded):
    plane_y = lax.axis_index("gy")
    plane_x = lax.axis_index("gx")
    upper_rim = jnp.where(plane_y == 0, padded[:, 1:2], padded[:, 0:1])
    bottom = jnp.where(plane_y == lax.axis_size("gy") - 1, padded[:, -2:-1], padded[:, -1:])
    row_fixed = jnp.concatenate([upper_rim, padded[:, 1:-1], bottom], 1)
    left_rim = jnp.where(plane_x == 0, row_fixed[:, :, 1:2], row_fixed[:, :, 0:1])
    right_rim = jnp.where(
        plane_x == lax.axis_size("gx") - 1, row_fixed[:, :, -2:-1], row_fixed[:, :, -1:]
    )
    return jnp.concatenate([left_rim, row_fixed[:, :, 1:-1], right_rim], 2)


def advance(now, prev, stiffness, density, stretch_own, inverse_step, is_fine):
    if is_fine:
        padded = with_halo(now, (("gz", 1), ("gy", 2), ("gx", 3)), 1)
        stress = with_halo(
            stresses(padded, stiffness, stretch_own, inverse_step),
            (("gz", 1), ("gy", 2), ("gx", 3)),
            1,
        )
    else:
        padded = with_halo(now, (("gz", 1), ("gy", 2), ("gx", 3)), 1)
        stress = with_halo(
            stresses(padded, stiffness, stretch_own, inverse_step),
            (("gz", 1), ("gy", 2), ("gx", 3)),
            1,
        )
    internal = divergence(stress, stretch_own, inverse_step)
    return 2.0 * now - prev + TIME_STEP * TIME_STEP * internal / density


def per_device(
    fine_now,
    fine_prev,
    stiffness,
    metric,
    density,
    coarse_now,
    coarse_prev,
    coarse_stiffness,
    coarse_density,
):
    plane_z = lax.axis_index("gz")
    count_z = lax.axis_size("gz")
    layers = fine_now.shape[1]
    layer_index = plane_z * layers + jnp.arange(layers)
    stretch_own = jnp.where((layer_index < count_z * layers // 2)[:, None, None], metric, 1.0)
    fine_step = advance(fine_now, fine_prev, stiffness, density, stretch_own, 0.5, True)
    coarse_step = advance(
        coarse_now, coarse_prev, coarse_stiffness, coarse_density, 1.0, 0.25, False
    )
    fine_start = fine_step[:, -1]
    above = fine_step[:, -2]
    fine_coef = jnp.stack([stiffness[4, -1], stiffness[3, -1], stiffness[2, -1]])
    coarse_start = coarse_step[:, 0]
    below = coarse_step[:, 1]
    coarse_coef = jnp.stack(
        [coarse_stiffness[4, 0], coarse_stiffness[3, 0], coarse_stiffness[2, 0]]
    )
    coarse_iter = coarse_start
    bundle = jnp.concatenate([fine_start, above, fine_coef], 0)
    lowered = passed_along(bundle, "gz", -3)
    slot_fine = lowered[:3]
    slot_above = lowered[3:6]
    slot_coef = jnp.where(plane_z == 0, lowered[6:], 1.0)
    for repeat in range(ITERS):
        traction = coarse_coef * (below - coarse_iter) * 0.25
        padded = with_halo_2(traction, (("gy", 1), ("gx", 2)), 1)
        fine_later = slot_above + prolong(extend_edges(padded)) / slot_coef
        coarse_iter = 0.5 * (coarse_start + restrict(slot_fine))
        slot_fine = fine_later
    fine_iter = passed_along(slot_fine, "gz", 3)
    fine_next = fine_step.at[:, -1].set(
        jnp.where(plane_z == count_z - 1, fine_iter, fine_step[:, -1])
    )
    coarse_next = coarse_step.at[:, 0].set(jnp.where(plane_z == 0, coarse_iter, coarse_step[:, 0]))
    return (fine_next, coarse_next)


def solution(mesh):
    placed = (
        P(None, "gz", "gy", "gx"),
        P(None, "gz", "gy", "gx"),
        P(None, "gz", "gy", "gx"),
        P("gz", "gy", "gx"),
        P("gz", "gy", "gx"),
        P(None, "gz", "gy", "gx"),
        P(None, "gz", "gy", "gx"),
        P(None, "gz", "gy", "gx"),
        P("gz", "gy", "gx"),
    )
    return jax.shard_map(
        per_device,
        mesh=mesh,
        in_specs=placed,
        out_specs=(P(None, "gz", "gy", "gx"), P(None, "gz", "gy", "gx")),
        check_vma=False,
    )
```

profile of v0, /device:TPU:482, one launch (start us, length us, event | category | flops | bytes accessed | tf_op | source)
XLA Modules:
  0.0 181.6 jit_solution(4530791302180147863)
XLA Ops:
  4.8 7.9 %collective-permute-start.17 = (f32[3,8,1,128]{3,1,2,0:T(8,128)S(1)}, f32[3,8,1,128]{3,1,2,0:T(8,128)S(1)}, u32[]{:S(2)}, u32[]{:S(2)}) collective-permute-start(f32[3,8,1,128]{3,1,2,0:T(8,128)S(1)} %bitcast.309), channel_id=1, source_target_pairs={{8,0},{16,8},{24,16},{32,24},{40,32},{48,40},{56,48},{64,56},{72,6... | collective-permute-start | bytes 36872 | tf_op jit(solution)/shard_map/ppermute | solution.py:21
  15.3 2.9 %collective-permute-start.16 = (f32[3,1,8,128]{3,2,1,0:T(8,128)S(1)}, f32[3,1,8,128]{3,2,1,0:T(8,128)S(1)}, u32[]{:S(2)}, u32[]{:S(2)}) collective-permute-start(f32[3,1,8,128]{3,2,1,0:T(8,128)S(1)} %get-tuple-element.95), channel_id=1, source_target_pairs={{128,0},{256,128},{384,256},{129,1},{257,129},{385,257},{130,2},{2... | collective-permute-start | bytes 36872 | tf_op jit(solution)/shard_map/ppermute | solution.py:21
  24.3 3.5 %collective-permute-done.13 = f32[3,8,8,1]{3,0,2,1:T(4,128)S(1)} collective-permute-done((f32[3,8,8,1]{3,0,2,1:T(4,128)S(1)}, f32[3,8,8,1]{3,0,2,1:T(4,128)S(1)}, u32[]{:S(2)}, u32[]{:S(2)}) %collective-permute-start.13) | collective-permute-done | bytes 800 | tf_op jit(solution)/shard_map/ppermute | solution.py:20
  31.2 9.9 %collective-permute-start.23 = (f32[6,8,1,128]{3,1,2,0:T(8,128)S(1)}, f32[6,8,1,128]{3,1,2,0:T(8,128)S(1)}, u32[]{:S(2)}, u32[]{:S(2)}) collective-permute-start(f32[6,8,1,128]{3,1,2,0:T(8,128)S(1)} %bitcast.305), channel_id=1, source_target_pairs={{8,0},{16,8},{24,16},{32,24},{40,32},{48,40},{56,48},{64,56},{72,6... | collective-permute-start | bytes 73736 | tf_op jit(solution)/shard_map/ppermute | solution.py:21
  43.1 2.1 %collective-permute-start.19 = (f32[6,8,8,1]{3,2,1,0:T(8,128)S(1)}, f32[6,8,8,1]{3,2,1,0:T(8,128)S(1)}, u32[]{:S(2)}, u32[]{:S(2)}) collective-permute-start(f32[6,8,8,1]{3,2,1,0:T(8,128)S(1)} %get-tuple-element.75), channel_id=1, source_target_pairs={{0,1},{1,2},{2,3},{3,4},{4,5},{5,6},{6,7},{8,9},{9,10},{10,11},{11... | collective-permute-start | bytes 4616 | tf_op jit(solution)/shard_map/ppermute | solution.py:20
  45.2 4.5 %collective-permute-start.22 = (f32[6,1,8,128]{3,2,1,0:T(8,128)S(1)}, f32[6,1,8,128]{3,2,1,0:T(8,128)S(1)}, u32[]{:S(2)}, u32[]{:S(2)}) collective-permute-start(f32[6,1,8,128]{3,2,1,0:T(8,128)S(1)} %get-tuple-element.74), channel_id=1, source_target_pairs={{128,0},{256,128},{384,256},{129,1},{257,129},{385,257},{130,2},{2... | collective-permute-start | bytes 73736 | tf_op jit(solution)/shard_map/ppermute | solution.py:21
  51.2 3.2 %collective-permute-start.5 = (f32[3,4,16,1]{3,2,1,0:T(8,128)S(1)}, f32[3,4,16,1]{3,2,1,0:T(8,128)S(1)}, u32[]{:S(2)}, u32[]{:S(2)}) collective-permute-start(f32[3,4,16,1]{3,2,1,0:T(8,128)S(1)} %get-tuple-element.82), channel_id=1, source_target_pairs={{1,0},{2,1},{3,2},{4,3},{5,4},{6,5},{7,6},{9,8},{10,9},{11,10},{12... | collective-permute-start | bytes 2312 | tf_op jit(solution)/shard_map/ppermute | solution.py:21
  54.3 9.9 %collective-permute-start.4 = (f32[3,4,1,256]{3,1,2,0:T(4,128)S(1)}, f32[3,4,1,256]{3,1,2,0:T(4,128)S(1)}, u32[]{:S(2)}, u32[]{:S(2)}) collective-permute-start(f32[3,4,1,256]{3,1,2,0:T(4,128)S(1)} %copy.445), channel_id=1, source_target_pairs={{8,0},{16,8},{24,16},{32,24},{40,32},{48,40},{56,48},{64,56},{72,6... | collective-permute-start | bytes 36872 | tf_op jit(solution)/shard_map/ppermute | solution.py:21
  71.7 4.3 %collective-permute-start.3 = (f32[3,1,16,256]{3,2,1,0:T(8,128)S(1)}, f32[3,1,16,256]{3,2,1,0:T(8,128)S(1)}, u32[]{:S(2)}, u32[]{:S(2)}) collective-permute-start(f32[3,1,16,256]{3,2,1,0:T(8,128)S(1)} %get-tuple-element.80), channel_id=1, source_target_pairs={{128,0},{256,128},{384,256},{129,1},{257,129},{385,257},{130,2},{2... | collective-permute-start | bytes 147464 | tf_op jit(solution)/shard_map/ppermute | solution.py:21
  76.1 9.9 %collective-permute-start.26 = (f32[3,1,128]{2,1,0:T(1,128)S(1)}, f32[3,1,128]{2,1,0:T(1,128)S(1)}, u32[]{:S(2)}, u32[]{:S(2)}) collective-permute-start(f32[3,1,128]{2,1,0:T(1,128)S(1)} %get-tuple-element.134), channel_id=1, source_target_pairs={{8,0},{16,8},{24,16},{32,24},{40,32},{48,40},{56,48},{64,56},{72,6... | collective-permute-start | bytes 4616 | tf_op jit(solution)/shard_map/ppermute | solution.py:48
  87.4 2.5 %collective-permute-start.28 = (f32[3,10,1]{2,0,1:T(4,128)S(1)}, f32[3,10,1]{2,0,1:T(4,128)S(1)}, u32[]{:S(2)}, u32[]{:S(2)}) collective-permute-start(f32[3,10,1]{2,0,1:T(4,128)S(1)} %get-tuple-element.129), channel_id=1, source_target_pairs={{1,0},{2,1},{3,2},{4,3},{5,4},{6,5},{7,6},{9,8},{10,9},{11,10},{12... | collective-permute-start | bytes 368 | tf_op jit(solution)/shard_map/ppermute | solution.py:48
  95.8 2.0 %collective-permute-done.2 = f32[3,1,16,256]{3,2,1,0:T(8,128)S(1)} collective-permute-done((f32[3,1,16,256]{3,2,1,0:T(8,128)S(1)}, f32[3,1,16,256]{3,2,1,0:T(8,128)S(1)}, u32[]{:S(2)}, u32[]{:S(2)}) %collective-permute-start.2) | collective-permute-done | bytes 49184 | tf_op jit(solution)/shard_map/ppermute | solution.py:20
  99.3 10.2 %collective-permute-start.10 = (f32[6,4,1,256]{3,1,2,0:T(4,128)S(1)}, f32[6,4,1,256]{3,1,2,0:T(4,128)S(1)}, u32[]{:S(2)}, u32[]{:S(2)}) collective-permute-start(f32[6,4,1,256]{3,1,2,0:T(4,128)S(1)} %copy.447), channel_id=1, source_target_pairs={{8,0},{16,8},{24,16},{32,24},{40,32},{48,40},{56,48},{64,56},{72,6... | collective-permute-start | bytes 73736 | tf_op jit(solution)/shard_map/ppermute | solution.py:21
  113.4 2.4 %collective-permute-start.6 = (f32[6,4,16,1]{3,2,1,0:T(8,128)S(1)}, f32[6,4,16,1]{3,2,1,0:T(8,128)S(1)}, u32[]{:S(2)}, u32[]{:S(2)}) collective-permute-start(f32[6,4,16,1]{3,2,1,0:T(8,128)S(1)} %get-tuple-element.64), channel_id=1, source_target_pairs={{0,1},{1,2},{2,3},{3,4},{4,5},{5,6},{6,7},{8,9},{9,10},{10,11},{11... | collective-permute-start | bytes 4616 | tf_op jit(solution)/shard_map/ppermute | solution.py:20
  115.8 2.9 %collective-permute-start.9 = (f32[6,1,16,256]{3,2,1,0:T(8,128)S(1)}, f32[6,1,16,256]{3,2,1,0:T(8,128)S(1)}, u32[]{:S(2)}, u32[]{:S(2)}) collective-permute-start(f32[6,1,16,256]{3,2,1,0:T(8,128)S(1)} %get-tuple-element.63), channel_id=1, source_target_pairs={{128,0},{256,128},{384,256},{129,1},{257,129},{385,257},{130,2},{2... | collective-permute-start | bytes 294920 | tf_op jit(solution)/shard_map/ppermute | solution.py:21
  120.5 3.1 %collective-permute-done.7 = f32[6,4,1,256]{3,1,2,0:T(4,128)S(1)} collective-permute-done((f32[6,4,1,256]{3,1,2,0:T(4,128)S(1)}, f32[6,4,1,256]{3,1,2,0:T(4,128)S(1)}, u32[]{:S(2)}, u32[]{:S(2)}) %collective-permute-start.7) | collective-permute-done | bytes 24608 | tf_op jit(solution)/shard_map/ppermute | solution.py:20
  123.7 2.6 %collective-permute-done.8 = f32[6,1,16,256]{3,2,1,0:T(8,128)S(1)} collective-permute-done((f32[6,1,16,256]{3,2,1,0:T(8,128)S(1)}, f32[6,1,16,256]{3,2,1,0:T(8,128)S(1)}, u32[]{:S(2)}, u32[]{:S(2)}) %collective-permute-start.8) | collective-permute-done | bytes 98336 | tf_op jit(solution)/shard_map/ppermute | solution.py:20
  129.5 3.6 %collective-permute-done.12 = f32[9,16,256]{2,1,0:T(8,128)S(1)} collective-permute-done((f32[9,16,256]{2,1,0:T(8,128)S(1)}, f32[9,16,256]{2,1,0:T(8,128)S(1)}, u32[]{:S(2)}, u32[]{:S(2)}) %collective-permute-start.12) | collective-permute-done | bytes 147488 | tf_op jit(solution)/shard_map/ppermute | solution.py:35
  136.6 9.9 %collective-permute-start.35 = (f32[3,1,128]{2,1,0:T(1,128)S(1)}, f32[3,1,128]{2,1,0:T(1,128)S(1)}, u32[]{:S(2)}, u32[]{:S(2)}) collective-permute-start(f32[3,1,128]{2,1,0:T(1,128)S(1)} %get-tuple-element.130), channel_id=1, source_target_pairs={{8,0},{16,8},{24,16},{32,24},{40,32},{48,40},{56,48},{64,56},{72,6... | collective-permute-start | bytes 4616 | tf_op jit(solution)/shard_map/ppermute | solution.py:48
  148.5 9.9 %collective-permute-start.30 = (f32[3,1,128]{2,1,0:T(1,128)S(1)}, f32[3,1,128]{2,1,0:T(1,128)S(1)}, u32[]{:S(2)}, u32[]{:S(2)}) collective-permute-start(f32[3,1,128]{2,1,0:T(1,128)S(1)} %get-tuple-element.132), channel_id=1, source_target_pairs={{8,0},{16,8},{24,16},{32,24},{40,32},{48,40},{56,48},{64,56},{72,6... | collective-permute-start | bytes 4616 | tf_op jit(solution)/shard_map/ppermute | solution.py:48
  160.5 2.4 %collective-permute-start.36 = (f32[3,10,1]{2,0,1:T(4,128)S(1)}, f32[3,10,1]{2,0,1:T(4,128)S(1)}, u32[]{:S(2)}, u32[]{:S(2)}) collective-permute-start(f32[3,10,1]{2,0,1:T(4,128)S(1)} %get-tuple-element.124), channel_id=1, source_target_pairs={{0,1},{1,2},{2,3},{3,4},{4,5},{5,6},{6,7},{8,9},{9,10},{10,11},{11... | collective-permute-start | bytes 368 | tf_op jit(solution)/shard_map/ppermute | solution.py:46
  163.0 3.1 %collective-permute-start.32 = (f32[3,10,1]{2,0,1:T(4,128)S(1)}, f32[3,10,1]{2,0,1:T(4,128)S(1)}, u32[]{:S(2)}, u32[]{:S(2)}) collective-permute-start(f32[3,10,1]{2,0,1:T(4,128)S(1)} %get-tuple-element.127), channel_id=1, source_target_pairs={{1,0},{2,1},{3,2},{4,3},{5,4},{6,5},{7,6},{9,8},{10,9},{11,10},{12... | collective-permute-start | bytes 368 | tf_op jit(solution)/shard_map/ppermute | solution.py:48
  168.5 2.8 %collective-permute-done.31 = f32[3,10,1]{2,0,1:T(4,128)S(1)} collective-permute-done((f32[3,10,1]{2,0,1:T(4,128)S(1)}, f32[3,10,1]{2,0,1:T(4,128)S(1)}, u32[]{:S(2)}, u32[]{:S(2)}) %collective-permute-start.31) | collective-permute-done | bytes 152 | tf_op jit(solution)/shard_map/ppermute | solution.py:46
  175.2 5.7 %collective-permute-done.33 = f32[3,16,256]{2,1,0:T(8,128)S(1)} collective-permute-done((f32[3,16,256]{2,1,0:T(8,128)S(1)}, f32[3,16,256]{2,1,0:T(8,128)S(1)}, u32[]{:S(2)}, u32[]{:S(2)}) %collective-permute-start.33) | collective-permute-done | bytes 49184 | tf_op jit(solution)/shard_map/ppermute | solution.py:35
  (219 shorter events, 57.9 us)
Async XLA Ops:
  1.8 22.5 %collective-permute-start.18 = (f32[3,8,8,1]{3,0,2,1:T(4,128)S(1)}, f32[3,8,8,1]{3,0,2,1:T(4,128)S(1)}, u32[]{:S(2)}, u32[]{:S(2)}) collective-permute-start(f32[3,8,8,1]{3,0,2,1:T(4,128)S(1)} %copy.443), channel_id=1, source_target_pairs={{1,0},{2,1},{3,2},{4,3},{5,4},{6,5},{7,6},{9,8},{10,9},{11,10},{12... | collective-permute-start | bytes 2312 | tf_op jit(solution)/shard_map/ppermute | solution.py:21
  4.8 19.2 %collective-permute-start.17 = (f32[3,8,1,128]{3,1,2,0:T(8,128)S(1)}, f32[3,8,1,128]{3,1,2,0:T(8,128)S(1)}, u32[]{:S(2)}, u32[]{:S(2)}) collective-permute-start(f32[3,8,1,128]{3,1,2,0:T(8,128)S(1)} %bitcast.309), channel_id=1, source_target_pairs={{8,0},{16,8},{24,16},{32,24},{40,32},{48,40},{56,48},{64,56},{72,6... | collective-permute-start | bytes 36872 | tf_op jit(solution)/shard_map/ppermute | solution.py:21
  12.7 11.6 %collective-permute-start.14 = (f32[3,8,1,128]{3,1,2,0:T(8,128)S(1)}, f32[3,8,1,128]{3,1,2,0:T(8,128)S(1)}, u32[]{:S(2)}, u32[]{:S(2)}) collective-permute-start(f32[3,8,1,128]{3,1,2,0:T(8,128)S(1)} %bitcast.308), channel_id=1, source_target_pairs={{0,8},{8,16},{16,24},{24,32},{32,40},{40,48},{48,56},{56,64},{64,7... | collective-permute-start | bytes 36872 | tf_op jit(solution)/shard_map/ppermute | solution.py:20
  29.3 20.5 %collective-permute-start.24 = (f32[6,8,8,1]{3,2,1,0:T(8,128)S(1)}, f32[6,8,8,1]{3,2,1,0:T(8,128)S(1)}, u32[]{:S(2)}, u32[]{:S(2)}) collective-permute-start(f32[6,8,8,1]{3,2,1,0:T(8,128)S(1)} %get-tuple-element.76), channel_id=1, source_target_pairs={{1,0},{2,1},{3,2},{4,3},{5,4},{6,5},{7,6},{9,8},{10,9},{11,10},{12... | collective-permute-start | bytes 4616 | tf_op jit(solution)/shard_map/ppermute | solution.py:21
  31.2 23.1 %collective-permute-start.23 = (f32[6,8,1,128]{3,1,2,0:T(8,128)S(1)}, f32[6,8,1,128]{3,1,2,0:T(8,128)S(1)}, u32[]{:S(2)}, u32[]{:S(2)}) collective-permute-start(f32[6,8,1,128]{3,1,2,0:T(8,128)S(1)} %bitcast.305), channel_id=1, source_target_pairs={{8,0},{16,8},{24,16},{32,24},{40,32},{48,40},{56,48},{64,56},{72,6... | collective-permute-start | bytes 73736 | tf_op jit(solution)/shard_map/ppermute | solution.py:21
  41.2 23.1 %collective-permute-start.20 = (f32[6,8,1,128]{3,1,2,0:T(8,128)S(1)}, f32[6,8,1,128]{3,1,2,0:T(8,128)S(1)}, u32[]{:S(2)}, u32[]{:S(2)}) collective-permute-start(f32[6,8,1,128]{3,1,2,0:T(8,128)S(1)} %bitcast.304), channel_id=1, source_target_pairs={{0,8},{8,16},{16,24},{24,32},{32,40},{40,48},{48,56},{56,64},{64,7... | collective-permute-start | bytes 73736 | tf_op jit(solution)/shard_map/ppermute | solution.py:20
  45.2 21.0 %collective-permute-start.22 = (f32[6,1,8,128]{3,2,1,0:T(8,128)S(1)}, f32[6,1,8,128]{3,2,1,0:T(8,128)S(1)}, u32[]{:S(2)}, u32[]{:S(2)}) collective-permute-start(f32[6,1,8,128]{3,2,1,0:T(8,128)S(1)} %get-tuple-element.74), channel_id=1, source_target_pairs={{128,0},{256,128},{384,256},{129,1},{257,129},{385,257},{130,2},{2... | collective-permute-start | bytes 73736 | tf_op jit(solution)/shard_map/ppermute | solution.py:21
  49.8 18.4 %collective-permute-start.21 = (f32[6,1,8,128]{3,2,1,0:T(8,128)S(1)}, f32[6,1,8,128]{3,2,1,0:T(8,128)S(1)}, u32[]{:S(2)}, u32[]{:S(2)}) collective-permute-start(f32[6,1,8,128]{3,2,1,0:T(8,128)S(1)} %get-tuple-element.73), channel_id=1, source_target_pairs={{0,128},{128,256},{256,384},{1,129},{129,257},{257,385},{2,130},{1... | collective-permute-start | bytes 73736 | tf_op jit(solution)/shard_map/ppermute | solution.py:20
  51.2 44.6 %collective-permute-start.5 = (f32[3,4,16,1]{3,2,1,0:T(8,128)S(1)}, f32[3,4,16,1]{3,2,1,0:T(8,128)S(1)}, u32[]{:S(2)}, u32[]{:S(2)}) collective-permute-start(f32[3,4,16,1]{3,2,1,0:T(8,128)S(1)} %get-tuple-element.82), channel_id=1, source_target_pairs={{1,0},{2,1},{3,2},{4,3},{5,4},{6,5},{7,6},{9,8},{10,9},{11,10},{12... | collective-permute-start | bytes 2312 | tf_op jit(solution)/shard_map/ppermute | solution.py:21
  54.3 17.4 %collective-permute-start.4 = (f32[3,4,1,256]{3,1,2,0:T(4,128)S(1)}, f32[3,4,1,256]{3,1,2,0:T(4,128)S(1)}, u32[]{:S(2)}, u32[]{:S(2)}) collective-permute-start(f32[3,4,1,256]{3,1,2,0:T(4,128)S(1)} %copy.445), channel_id=1, source_target_pairs={{8,0},{16,8},{24,16},{32,24},{40,32},{48,40},{56,48},{64,56},{72,6... | collective-permute-start | bytes 36872 | tf_op jit(solution)/shard_map/ppermute | solution.py:21
  64.3 11.7 %collective-permute-start.1 = (f32[3,4,1,256]{3,1,2,0:T(4,128)S(1)}, f32[3,4,1,256]{3,1,2,0:T(4,128)S(1)}, u32[]{:S(2)}, u32[]{:S(2)}) collective-permute-start(f32[3,4,1,256]{3,1,2,0:T(4,128)S(1)} %copy.444), channel_id=1, source_target_pairs={{0,8},{8,16},{16,24},{24,32},{32,40},{40,48},{48,56},{56,64},{64,7... | collective-permute-start | bytes 36872 | tf_op jit(solution)/shard_map/ppermute | solution.py:20
  66.2 29.5 %collective-permute-start = (f32[3,4,16,1]{3,2,1,0:T(8,128)S(1)}, f32[3,4,16,1]{3,2,1,0:T(8,128)S(1)}, u32[]{:S(2)}, u32[]{:S(2)}) collective-permute-start(f32[3,4,16,1]{3,2,1,0:T(8,128)S(1)} %get-tuple-element.81), channel_id=1, source_target_pairs={{0,1},{1,2},{2,3},{3,4},{4,5},{5,6},{6,7},{8,9},{9,10},{10,11},{11... | collective-permute-start | bytes 2312 | tf_op jit(solution)/shard_map/ppermute | solution.py:20
  69.8 16.3 %collective-permute-start.25 = (f32[3,1,128]{2,1,0:T(1,128)S(1)}, f32[3,1,128]{2,1,0:T(1,128)S(1)}, u32[]{:S(2)}, u32[]{:S(2)}) collective-permute-start(f32[3,1,128]{2,1,0:T(1,128)S(1)} %get-tuple-element.135), channel_id=1, source_target_pairs={{0,8},{8,16},{16,24},{24,32},{32,40},{40,48},{48,56},{56,64},{64,7... | collective-permute-start | bytes 4616 | tf_op jit(solution)/shard_map/ppermute | solution.py:46
  71.7 24.0 %collective-permute-start.3 = (f32[3,1,16,256]{3,2,1,0:T(8,128)S(1)}, f32[3,1,16,256]{3,2,1,0:T(8,128)S(1)}, u32[]{:S(2)}, u32[]{:S(2)}) collective-permute-start(f32[3,1,16,256]{3,2,1,0:T(8,128)S(1)} %get-tuple-element.80), channel_id=1, source_target_pairs={{128,0},{256,128},{384,256},{129,1},{257,129},{385,257},{130,2},{2... | collective-permute-start | bytes 147464 | tf_op jit(solution)/shard_map/ppermute | solution.py:21
  76.1 11.2 %collective-permute-start.26 = (f32[3,1,128]{2,1,0:T(1,128)S(1)}, f32[3,1,128]{2,1,0:T(1,128)S(1)}, u32[]{:S(2)}, u32[]{:S(2)}) collective-permute-start(f32[3,1,128]{2,1,0:T(1,128)S(1)} %get-tuple-element.134), channel_id=1, source_target_pairs={{8,0},{16,8},{24,16},{32,24},{40,32},{48,40},{56,48},{64,56},{72,6... | collective-permute-start | bytes 4616 | tf_op jit(solution)/shard_map/ppermute | solution.py:48
  99.3 19.4 %collective-permute-start.10 = (f32[6,4,1,256]{3,1,2,0:T(4,128)S(1)}, f32[6,4,1,256]{3,1,2,0:T(4,128)S(1)}, u32[]{:S(2)}, u32[]{:S(2)}) collective-permute-start(f32[6,4,1,256]{3,1,2,0:T(4,128)S(1)} %copy.447), channel_id=1, source_target_pairs={{8,0},{16,8},{24,16},{32,24},{40,32},{48,40},{56,48},{64,56},{72,6... | collective-permute-start | bytes 73736 | tf_op jit(solution)/shard_map/ppermute | solution.py:21
  109.5 14.1 %collective-permute-start.11 = (f32[6,4,16,1]{3,2,1,0:T(8,128)S(1)}, f32[6,4,16,1]{3,2,1,0:T(8,128)S(1)}, u32[]{:S(2)}, u32[]{:S(2)}) collective-permute-start(f32[6,4,16,1]{3,2,1,0:T(8,128)S(1)} %get-tuple-element.65), channel_id=1, source_target_pairs={{1,0},{2,1},{3,2},{4,3},{5,4},{6,5},{7,6},{9,8},{10,9},{11,10},{12... | collective-permute-start | bytes 4616 | tf_op jit(solution)/shard_map/ppermute | solution.py:21
  111.5 12.1 %collective-permute-start.7 = (f32[6,4,1,256]{3,1,2,0:T(4,128)S(1)}, f32[6,4,1,256]{3,1,2,0:T(4,128)S(1)}, u32[]{:S(2)}, u32[]{:S(2)}) collective-permute-start(f32[6,4,1,256]{3,1,2,0:T(4,128)S(1)} %copy.446), channel_id=1, source_target_pairs={{0,8},{8,16},{16,24},{24,32},{32,40},{40,48},{48,56},{56,64},{64,7... | collective-permute-start | bytes 73736 | tf_op jit(solution)/shard_map/ppermute | solution.py:20
  113.4 10.2 %collective-permute-start.6 = (f32[6,4,16,1]{3,2,1,0:T(8,128)S(1)}, f32[6,4,16,1]{3,2,1,0:T(8,128)S(1)}, u32[]{:S(2)}, u32[]{:S(2)}) collective-permute-start(f32[6,4,16,1]{3,2,1,0:T(8,128)S(1)} %get-tuple-element.64), channel_id=1, source_target_pairs={{0,1},{1,2},{2,3},{3,4},{4,5},{5,6},{6,7},{8,9},{9,10},{10,11},{11... | collective-permute-start | bytes 4616 | tf_op jit(solution)/shard_map/ppermute | solution.py:20
  134.6 23.8 %collective-permute-start.34 = (f32[3,1,128]{2,1,0:T(1,128)S(1)}, f32[3,1,128]{2,1,0:T(1,128)S(1)}, u32[]{:S(2)}, u32[]{:S(2)}) collective-permute-start(f32[3,1,128]{2,1,0:T(1,128)S(1)} %get-tuple-element.131), channel_id=1, source_target_pairs={{0,8},{8,16},{16,24},{24,32},{32,40},{40,48},{48,56},{56,64},{64,7... | collective-permute-start | bytes 4616 | tf_op jit(solution)/shard_map/ppermute | solution.py:46
  136.6 21.9 %collective-permute-start.35 = (f32[3,1,128]{2,1,0:T(1,128)S(1)}, f32[3,1,128]{2,1,0:T(1,128)S(1)}, u32[]{:S(2)}, u32[]{:S(2)}) collective-permute-start(f32[3,1,128]{2,1,0:T(1,128)S(1)} %get-tuple-element.130), channel_id=1, source_target_pairs={{8,0},{16,8},{24,16},{32,24},{40,32},{48,40},{56,48},{64,56},{72,6... | collective-permute-start | bytes 4616 | tf_op jit(solution)/shard_map/ppermute | solution.py:48
  146.5 16.4 %collective-permute-start.29 = (f32[3,1,128]{2,1,0:T(1,128)S(1)}, f32[3,1,128]{2,1,0:T(1,128)S(1)}, u32[]{:S(2)}, u32[]{:S(2)}) collective-permute-start(f32[3,1,128]{2,1,0:T(1,128)S(1)} %get-tuple-element.133), channel_id=1, source_target_pairs={{0,8},{8,16},{16,24},{24,32},{32,40},{40,48},{48,56},{56,64},{64,7... | collective-permute-start | bytes 4616 | tf_op jit(solution)/shard_map/ppermute | solution.py:46
  148.5 14.5 %collective-permute-start.30 = (f32[3,1,128]{2,1,0:T(1,128)S(1)}, f32[3,1,128]{2,1,0:T(1,128)S(1)}, u32[]{:S(2)}, u32[]{:S(2)}) collective-permute-start(f32[3,1,128]{2,1,0:T(1,128)S(1)} %get-tuple-element.132), channel_id=1, source_target_pairs={{8,0},{16,8},{24,16},{32,24},{40,32},{48,40},{56,48},{64,56},{72,6... | collective-permute-start | bytes 4616 | tf_op jit(solution)/shard_map/ppermute | solution.py:48
  158.5 9.6 %collective-permute-start.37 = (f32[3,10,1]{2,0,1:T(4,128)S(1)}, f32[3,10,1]{2,0,1:T(4,128)S(1)}, u32[]{:S(2)}, u32[]{:S(2)}) collective-permute-start(f32[3,10,1]{2,0,1:T(4,128)S(1)} %get-tuple-element.125), channel_id=1, source_target_pairs={{1,0},{2,1},{3,2},{4,3},{5,4},{6,5},{7,6},{9,8},{10,9},{11,10},{12... | collective-permute-start | bytes 368 | tf_op jit(solution)/shard_map/ppermute | solution.py:48
  (25 other events, 151.8 us)
where the time goes:
time: 183 us; the launch traced here: 182 us
  starting transfers between devices  135 us (74%)
  waiting for transfers between devices  27.2 us (15%)
  local copies, waits for them, and re-layouts  11.5 us (6%)
  other arithmetic  5.91 us (3%)
  between operations  2.15 us (1%)
    ppermute x12, starting transfers between devices, with_halo(): lax.ppermute(first, axis, [(b, a) for a, b in up])  61.5 us
    ppermute x6, starting transfers between devices, with_halo_2(): lax.ppermute(head, axis, [((i + 1) % count, i) for i in range(ends)])  37.4 us
    ppermute x12, starting transfers between devices, with_halo(): lax.ppermute(last, axis, up)  21.2 us
    ppermute x12, waiting for transfers between devices, with_halo(): lax.ppermute(last, axis, up)  12 us
    ppermute x6, starting transfers between devices, with_halo_2(): lax.ppermute(tail, axis, [(i, (i + 1) % count) for i in range(ends)])  12 us
    ppermute x2, waiting for transfers between devices, passed_along(): return lax.ppermute(shard, axis, pairs)  9.29 us
    slice x12, local copies, waits for them, and re-layouts, with_halo(): last = lax.slice_in_dim(shard, length - width, length, axis=dim)  5.02 us
    ppermute x6, waiting for transfers between devices, with_halo_2(): lax.ppermute(tail, axis, [(i, (i + 1) % count) for i in range(ends)])  4.63 us
  transfers between devices with their start and end apart: 38, of which 11 were waited for; matrix products, arithmetic and copies ran while one was open for 4% of the time, Pallas kernels for 0%

commit v1 on v0

v1 whole, which is shorter than its diff:
```python
import functools

import jax
import jax.numpy as jnp
from jax import lax
from jax.experimental import pallas as pl
from jax.experimental.pallas import tpu as pltpu
from jax.sharding import PartitionSpec as P

TIME_STEP = 0.2
ITERS = 3
F32 = jnp.float32
XX, XY, YY, XZ, YZ, ZZ = range(6)
FACE_X = (XX, XY, XZ)
FACE_Y = (XY, YY, YZ)
CH = (4, 3, 2)
PAD = 8
LANES = 128


def lanes_of(rows):
    return lax.broadcasted_iota(jnp.int32, (rows, LANES), 1)


def pack_x(ref, comps, z_count, y_count, width):
    lane = lanes_of(y_count)
    packed = jnp.zeros((y_count, LANES), F32)
    k = 0
    for c in comps:
        for z in range(z_count):
            rows = pl.ds(PAD, y_count)
            tile = ref[c, z + 1, rows, 0:LANES]
            if width > LANES:
                last = ref[c, z + 1, rows, width - LANES : width]
                tile = jnp.where(lane >= LANES // 2, last, tile)
            packed = jnp.where(lane // 2 == k, pltpu.roll(tile, 2 * k + 1, 1), packed)
            k += 1
    return packed


def unpack_x(ref, comps, z_count, y_count, width, from_left, from_right):
    lane = lanes_of(y_count)
    both = jnp.where(lane % 2 == 0, from_left, from_right)
    k = 0
    for c in comps:
        for z in range(z_count):
            ref[c, z + 1, pl.ds(PAD, y_count), width : width + LANES] = pltpu.roll(
                both, LANES - 1 - 2 * k, 1
            )
            k += 1


def diff_x(ref, c, z0, zn, y_count, width, scale):
    v = ref[c, z0 : z0 + zn, PAD : PAD + y_count, :]
    span = width + LANES
    return (pltpu.roll(v, span - 1, 2) - pltpu.roll(v, 1, 2))[:, :, :width] * scale


def diff_y(ref, c, z0, zn, y_count, width, scale):
    after = ref[c, z0 : z0 + zn, PAD + 1 : PAD + 1 + y_count, 0:width]
    before = ref[c, z0 : z0 + zn, PAD - 1 : PAD - 1 + y_count, 0:width]
    return (after - before) * scale


def diff_z(ref, c, z0, zn, y_count, width, scale):
    after = ref[c, z0 + 1 : z0 + 1 + zn, PAD : PAD + y_count, 0:width]
    before = ref[c, z0 - 1 : z0 - 1 + zn, PAD : PAD + y_count, 0:width]
    return (after - before) * scale


def stress_block(u, stiff, s, z, zn, y_count, width, inv, stretch):
    args = (z + 1, zn, y_count, width, inv)
    own = (slice(z + 1, z + 1 + zn), slice(PAD, PAD + y_count), slice(0, width))
    c = [stiff[i, z : z + zn] for i in range(9)]
    nx = diff_x(u, 0, *args)
    ny = diff_y(u, 1, *args)
    nz = diff_z(u, 2, *args) * stretch
    s[(XX,) + own] = c[0] * nx + c[6] * ny + c[7] * nz
    s[(YY,) + own] = c[6] * nx + c[1] * ny + c[8] * nz
    s[(ZZ,) + own] = c[7] * nx + c[8] * ny + c[2] * nz
    s[(YZ,) + own] = c[3] * (diff_z(u, 1, *args) * stretch + diff_y(u, 2, *args))
    s[(XZ,) + own] = c[4] * (diff_z(u, 0, *args) * stretch + diff_x(u, 2, *args))
    s[(XY,) + own] = c[5] * (diff_y(u, 0, *args) + diff_x(u, 1, *args))


def step_block(u, s, prev, dens, out, z, zn, y_count, width, inv, stretch):
    args = (z + 1, zn, y_count, width, inv)
    gain = (TIME_STEP * TIME_STEP) / dens[z : z + zn]
    for c, (sx, sy, sz) in enumerate(((XX, XY, XZ), (XY, YY, YZ), (XZ, YZ, ZZ))):
        total = diff_x(s, sx, *args) + diff_y(s, sy, *args) + diff_z(s, sz, *args) * stretch
        now = u[c, z + 1 : z + 1 + zn, PAD : PAD + y_count, 0:width]
        out[c, z : z + zn] = (2.0 * now - prev[c, z : z + zn]) + gain * total


def pick(x, index):
    return jnp.take_along_axis(x, index, axis=1, mode="promise_in_bounds")


def kernel(
    counts,
    fn, fp, st, me, de, cn, cp, cst, cde,
    fo_hbm, co_hbm,
    u, uc, s, sc, fprev, stiff, metric, dens, cprev, cstiff, cdens, fout, cout,
    xs, xr, yfs, yfr, ycs, ycr,
    tiles, own, own_opp, ikf_opp, ys3, yr3, yo3, xs3, xr3, xo3, ext,
    load_sem, out_sem, send_sem, recv_sem,
):
    n_z, n_y, n_x = counts
    zf, yf, xf = me.shape
    zc, yc, xc = cde.shape
    gz, gy, gx = lax.axis_index("gz"), lax.axis_index("gy"), lax.axis_index("gx")
    opp = n_z - 1 - gz
    is_c, is_f = gz == 0, gz == n_z - 1
    active = jnp.logical_or(is_c, is_f)
    has_y = {-1: gy > 0, 0: gy >= 0, 1: gy < n_y - 1}
    has_x = {-1: gx > 0, 0: gx >= 0, 1: gx < n_x - 1}
    has = (gz > 0, gz < n_z - 1, has_y[-1], has_y[1], has_x[-1], has_x[1])
    near = (
        (gz - 1, gy, gx), (gz + 1, gy, gx),
        (gz, gy - 1, gx), (gz, gy + 1, gx),
        (gz, gy, gx - 1), (gz, gy, gx + 1),
    )
    own_f = (slice(1, zf + 1), slice(PAD, PAD + yf), slice(0, xf))
    own_c = (slice(1, zc + 1), slice(PAD, PAD + yc), slice(0, xc))

    loads = [
        pltpu.make_async_copy(src, dst, load_sem.at[i])
        for i, (src, dst) in enumerate((
            (fn, u.at[(slice(None),) + own_f]),
            (cn, uc.at[(slice(None),) + own_c]),
            (st, stiff), (cst, cstiff), (me, metric),
            (fp, fprev), (cp, cprev), (de, dens), (cde, cdens),
        ))
    ]
    for load in loads:
        load.start()

    barrier = pltpu.get_barrier_semaphore()
    expected = jnp.int32(0)

    def greet(there, device):
        @pl.when(there)
        def _():
            pl.semaphore_signal(barrier, 1, device_id=device, device_id_type=pl.DeviceIdType.MESH)

        return there.astype(jnp.int32)

    for d in range(6):
        expected += greet(has[d], near[d])
    diagonals = [(a, b) for a in (-1, 1) for b in (-1, 1)]
    for a, b in diagonals:
        there = jnp.logical_and(active, jnp.logical_and(has_y[a], has_x[b]))
        expected += greet(there, (gz, gy + a, gx + b))
    expected += greet(active, (opp, gy, gx))

    for d in range(6):
        @pl.when(jnp.logical_not(has[d]))
        def _(d=d):
            side = d % 2
            if d < 2:
                plane_f, plane_c = (0, 0) if side == 0 else (zf + 1, zc + 1)
                for ref, plane, (_, rows, cols) in (
                    (u, plane_f, own_f), (uc, plane_c, own_c), (s, plane_f, own_f), (sc, plane_c, own_c),
                ):
                    part = ref.at[:, plane, rows, cols]
                    part[...] = jnp.zeros(part.shape, F32)
            elif d < 4:
                for r in range(2):
                    for ref in (yfr, ycr):
                        ref[r, side] = jnp.zeros(ref.shape[2:], F32)
            else:
                for r in range(2):
                    xr[r, side] = jnp.zeros(xr.shape[2:], F32)

    def rdma(src, dst, slot, device):
        return pltpu.make_async_remote_copy(
            src_ref=src, dst_ref=dst, send_sem=send_sem.at[slot], recv_sem=recv_sem.at[slot],
            device_id=device, device_id_type=pl.DeviceIdType.MESH,
        )

    def round_copies(r, d):
        side = d % 2
        arrival = 1 - side
        slot = (r * 6 + d) * 2
        if d < 2:
            fine, coarse = ((u, uc), (s, sc))[r]
            comps = (slice(0, 3), slice(3, 6))[r]
            made = []
            for g, (ref, z_count, (_, rows, cols)) in enumerate(((fine, zf, own_f), (coarse, zc, own_c))):
                sent, landed = (1, z_count + 1) if side == 0 else (z_count, 0)
                made.append(rdma(ref.at[comps, sent, rows, cols], ref.at[comps, landed, rows, cols], slot + g, near[d]))
            return made
        if d < 4:
            return [
                rdma(yfs.at[r, side], yfr.at[r, arrival], slot, near[d]),
                rdma(ycs.at[r, side], ycr.at[r, arrival], slot + 1, near[d]),
            ]
        return [rdma(xs.at[r], xr.at[r, arrival], slot, near[d])]

    def start_round(r):
        for d in (2, 3, 4, 5, 0, 1):
            @pl.when(has[d])
            def _(d=d):
                for copy in round_copies(r, d):
                    copy.start()

    def end_round(r, directions):
        for d in directions:
            @pl.when(has[d ^ 1])
            def _(d=d):
                for copy in round_copies(r, d):
                    copy.wait_recv()

    def pack(r, fine, coarse, face_x, face_y):
        for i, c in enumerate(face_y):
            yfs[r, 0, i] = fine[c, 1 : zf + 1, PAD : PAD + 1, 0:xf]
            yfs[r, 1, i] = fine[c, 1 : zf + 1, PAD + yf - 1 : PAD + yf, 0:xf]
            ycs[r, 0, i] = coarse[c, 1 : zc + 1, PAD : PAD + 1, 0:xc]
            ycs[r, 1, i] = coarse[c, 1 : zc + 1, PAD + yc - 1 : PAD + yc, 0:xc]
        xs[r, 0:yf] = pack_x(fine, face_x, zf, yf, xf)
        xs[r, yf : yf + yc] = pack_x(coarse, face_x, zc, yc, xc)

    def unpack(r, fine, coarse, face_x, face_y):
        for i, c in enumerate(face_y):
            fine[c, 1 : zf + 1, PAD - 1 : PAD, 0:xf] = yfr[r, 0, i]
            fine[c, 1 : zf + 1, PAD + yf : PAD + yf + 1, 0:xf] = yfr[r, 1, i]
            coarse[c, 1 : zc + 1, PAD - 1 : PAD, 0:xc] = ycr[r, 0, i]
            coarse[c, 1 : zc + 1, PAD + yc : PAD + yc + 1, 0:xc] = ycr[r, 1, i]
        unpack_x(fine, face_x, zf, yf, xf, xr[r, 0, 0:yf], xr[r, 1, 0:yf])
        unpack_x(coarse, face_x, zc, yc, xc, xr[r, 0, yf : yf + yc], xr[r, 1, yf : yf + yc])

    loads[0].wait()
    loads[1].wait()
    pack(0, u, uc, (0, 1, 2), (0, 1, 2))
    pl.semaphore_wait(barrier, expected)
    start_round(0)
    for load in loads[2:]:
        load.wait()

    lane = lanes_of(yc)
    even = (2 * lane) % LANES

    def squeeze(left, right, odd):
        return jnp.where(lane < LANES // 2, pick(left, even + odd), pick(right, even + odd))

    ikf_copy = rdma(own.at[6:18], ikf_opp, 24, (opp, gy, gx))

    @pl.when(is_f)
    def _():
        for c in range(3):
            inverse = 1.0 / stiff[CH[c], zf - 1]
            for t in range(2):
                tiles[t] = inverse[:, t * LANES : (t + 1) * LANES]
            for py in range(2):
                rows = pl.ds(py, yc, stride=2)
                left, right = tiles[0, rows, :], tiles[1, rows, :]
                for px in range(2):
                    own[6 + c * 4 + py * 2 + px] = squeeze(left, right, px)
        ikf_copy.start()

    def stretch_of(z):
        return jnp.where(gz * zf + z < n_z * zf // 2, metric[z : z + 1], 1.0)

    zb = min(4, zc)
    fine_order = tuple(range(zf - 1, -1, -1))
    coarse_order = tuple(range(0, zc, zb))

    end_round(0, (0, 1, 4, 5, 2, 3))
    unpack(0, u, uc, (0, 1, 2), (0, 1, 2))
    for z in fine_order:
        stress_block(u, stiff, s, z, 1, yf, xf, 0.5, stretch_of(z))
    for z in coarse_order:
        stress_block(uc, cstiff, sc, z, zb, yc, xc, 0.25, 1.0)
    pack(1, s, sc, FACE_X, FACE_Y)
    start_round(1)
    end_round(1, (0, 1, 4, 5, 2, 3))
    unpack(1, s, sc, FACE_X, FACE_Y)

    def fine_step(z):
        step_block(u, s, fprev, dens, fout, z, 1, yf, xf, 0.5, stretch_of(z))

    def coarse_step(z):
        step_block(uc, sc, cprev, cdens, cout, z, zb, yc, xc, 0.25, 1.0)

    fine_step(zf - 1)
    fine_step(zf - 2)
    coarse_step(0)

    @pl.when(is_c)
    def _():
        for c in range(3):
            start, below = cout[c, 0], cout[c, 1]
            k = cstiff[CH[c], 0] * 0.25
            own[c] = k * (below - start)
            own[3 + c] = below - 0.5 * start
            own[6 + c] = k

    @pl.when(is_f)
    def _():
        for c in range(3):
            for i, z in enumerate((zf - 2, zf - 1)):
                plane = fout[c, z]
                sums = []
                for t in range(2):
                    tiles[t] = plane[:, t * LANES : (t + 1) * LANES]
                    pair = tiles[t, pl.ds(0, yc, stride=2), :] + tiles[t, pl.ds(1, yc, stride=2), :]
                    sums.append(pair + pltpu.roll(pair, LANES - 1, 1))
                own[3 * i + c] = squeeze(sums[0], sums[1], 0) * 0.25

    fields = 18
    lane4 = lane // 4
    own_copy = rdma(own.at[0:9], own_opp, 25, (opp, gy, gx))
    strips = []
    for i, a in enumerate((-1, 1)):
        strips.append((
            jnp.logical_and(active, has_y[a]), jnp.logical_and(active, has_y[-a]),
            rdma(ys3.at[i], yr3.at[1 - i], 26 + i, (gz, gy + a, gx)),
        ))
    for i, b in enumerate((-1, 1)):
        for a in (-1, 0, 1):
            strips.append((
                jnp.logical_and(active, jnp.logical_and(has_y[a], has_x[b])),
                jnp.logical_and(active, jnp.logical_and(has_y[-a], has_x[-b])),
                rdma(xs3, xr3.at[1 - i, pl.ds((1 - a) * 8, 8)], 28 + i * 3 + (a + 1), (gz, gy + a, gx + b)),
            ))

    @pl.when(active)
    def _():
        own_copy.start()
        ys3[0] = own[:, 0:2, :]
        ys3[1] = own[:, yc - 2 : yc, :]
        packed = jnp.zeros((yc, LANES), F32)
        for k in range(fields):
            packed = jnp.where(lane4 == k, pltpu.roll(own[k], 4 * k + 2, 1), packed)
        xs3[...] = packed

    for there, _, copy in strips:
        @pl.when(there)
        def _(copy=copy):
            copy.start()

    for z in fine_order[2:]:
        fine_step(z)
    for z in coarse_order[1:]:
        coarse_step(z)

    early = [
        pltpu.make_async_copy(fout.at[:, 0 : zf - 1], fo_hbm.at[:, 0 : zf - 1], out_sem.at[0]),
        pltpu.make_async_copy(cout.at[:, 1:zc], co_hbm.at[:, 1:zc], out_sem.at[1]),
    ]
    late = [
        pltpu.make_async_copy(fout.at[:, zf - 1], fo_hbm.at[:, zf - 1], out_sem.at[2]),
        pltpu.make_async_copy(cout.at[:, 0], co_hbm.at[:, 0], out_sem.at[3]),
    ]
    for copy in early:
        copy.start()

    for _, comes, copy in strips:
        @pl.when(comes)
        def _(copy=copy):
            copy.wait_recv()

    forward = [
        rdma(yr3.at[:, 0:9], yo3, 34, (opp, gy, gx)),
        rdma(xr3, xo3, 35, (opp, gy, gx)),
    ]
    lane24 = lax.broadcasted_iota(jnp.int32, (24, LANES), 1)
    wide_row = lax.broadcasted_iota(jnp.int32, (24, 2 * LANES), 0)
    wide_lane = lax.broadcasted_iota(jnp.int32, (24, 2 * LANES), 1)

    def extend(k, field, centre, rims, sides):
        ext[k, 8:16, 0:LANES] = centre
        ext[k, 6:8, 0:LANES] = rims[0, field]
        ext[k, 16:18, 0:LANES] = rims[1, field]
        ext[k, :, LANES : 2 * LANES] = pltpu.roll(sides, LANES - (4 * field + 2), 1)

    def clamp(t):
        t = jnp.where(jnp.logical_and(wide_row == 7, gy == 0), pltpu.roll(t, 23, 0), t)
        t = jnp.where(jnp.logical_and(wide_row == 16, gy == n_y - 1), pltpu.roll(t, 1, 0), t)
        t = jnp.where(jnp.logical_and(wide_lane == 2 * LANES - 1, gx == 0), pltpu.roll(t, 2 * LANES - 1, 1), t)
        return jnp.where(jnp.logical_and(wide_lane == LANES, gx == n_x - 1), pltpu.roll(t, 1, 1), t)

    def along_y(t):
        return (0.75 * t + 0.25 * pltpu.roll(t, 1, 0), 0.75 * t + 0.25 * pltpu.roll(t, 23, 0))

    def along_x(t):
        return (0.75 * t + 0.25 * pltpu.roll(t, 1, 1), 0.75 * t + 0.25 * pltpu.roll(t, 2 * LANES - 1, 1))

    @pl.when(active)
    def _():
        for copy in forward:
            copy.start()
        own_copy.wait_recv()

    @pl.when(is_c)
    def _():
        ikf_copy.wait_recv()
        sides = jnp.where(lane24 % 4 < 2, xr3[0], xr3[1])
        for k in range(3, 9):
            extend(k, k, own[k], yr3, sides)

    @pl.when(is_f)
    def _():
        sides = jnp.where(lane24 % 4 < 2, xr3[0], xr3[1])
        for k in range(3):
            extend(9 + k, k, own[k], yr3, sides)
        for k in range(12):
            extend(12 + k, 6 + k, own[6 + k], yr3, sides)

    @pl.when(active)
    def _():
        for copy in forward:
            copy.wait_recv()

    @pl.when(is_c)
    def _():
        sides = jnp.where(lane24 % 4 < 2, xo3[0], xo3[1])
        for c in range(3):
            extend(9 + c, 3 + c, own_opp[3 + c], yo3, sides)
            t1 = clamp(ext[6 + c] * (ext[3 + c] - 0.5 * ext[9 + c]))
            total = jnp.zeros((yc, LANES), F32)
            for py, part in enumerate(along_y(t1)):
                for px, full in enumerate(along_x(part[8:16])):
                    total += full[:, 0:LANES] * ikf_opp[c * 4 + py * 2 + px]
            cout[c, 0] = 0.5 * (cout[c, 0] + own_opp[c] + 0.25 * total)

    @pl.when(is_f)
    def _():
        sides = jnp.where(lane24 % 4 < 2, xo3[0], xo3[1])
        half = lane // 2
        for c in range(3):
            for k in (c, 3 + c, 6 + c):
                extend(k, k, own_opp[k], yo3, sides)
            total = jnp.zeros((24, 2 * LANES), F32)
            for py, part in enumerate(along_y(clamp(ext[c]))):
                for px, full in enumerate(along_x(part)):
                    total += full * ext[12 + c * 4 + py * 2 + px]
            t2 = clamp(ext[6 + c] * (ext[3 + c] - 0.5 * (ext[9 + c] + 0.25 * total)))
            for py, part in enumerate(along_y(t2)):
                evens, odds = along_x(part[8:16])
                evens, odds = evens[:, 0:LANES], odds[:, 0:LANES]
                for t in range(2):
                    index = half + t * (LANES // 2)
                    tiles[t, pl.ds(py, yc, stride=2), :] = jnp.where(
                        lane % 2 == 0, pick(evens, index), pick(odds, index)
                    )
            for t in range(2):
                cols = slice(t * LANES, (t + 1) * LANES)
                fout[c, zf - 1, :, cols] = fout[c, zf - 2, :, cols] + tiles[t] / stiff[CH[c], zf - 1, :, cols]

    for copy in late:
        copy.start()
    for r in range(2):
        for d in range(6):
            @pl.when(has[d])
            def _(r=r, d=d):
                for copy in round_copies(r, d):
                    copy.wait_send()
    for there, _, copy in strips:
        @pl.when(there)
        def _(copy=copy):
            copy.wait_send()

    @pl.when(is_f)
    def _():
        ikf_copy.wait_send()

    @pl.when(active)
    def _():
        own_copy.wait_send()
        for copy in forward:
            copy.wait_send()

    for copy in early + late:
        copy.wait()


def per_device(counts, *args):
    fine, coarse = args[0].shape, args[5].shape
    _, zf, yf, xf = fine
    _, zc, yc, xc = coarse
    vmem = lambda *shape: pltpu.VMEM(shape, F32)
    anywhere = pl.BlockSpec(memory_space=pl.ANY)
    return pl.pallas_call(
        functools.partial(kernel, counts),
        out_shape=(jax.ShapeDtypeStruct(fine, F32), jax.ShapeDtypeStruct(coarse, F32)),
        in_specs=[anywhere] * 9,
        out_specs=(anywhere, anywhere),
        scratch_shapes=[
            vmem(3, zf + 2, yf + 2 * PAD, xf + LANES),
            vmem(3, zc + 2, yc + 2 * PAD, xc + LANES),
            vmem(6, zf + 2, yf + 2 * PAD, xf + LANES),
            vmem(6, zc + 2, yc + 2 * PAD, xc + LANES),
            vmem(3, zf, yf, xf), vmem(9, zf, yf, xf), vmem(zf, yf, xf), vmem(zf, yf, xf),
            vmem(3, zc, yc, xc), vmem(9, zc, yc, xc), vmem(zc, yc, xc),
            vmem(3, zf, yf, xf), vmem(3, zc, yc, xc),
            vmem(2, yf + yc, LANES), vmem(2, 2, yf + yc, LANES),
            vmem(2, 2, 3, zf, 1, xf), vmem(2, 2, 3, zf, 1, xf),
            vmem(2, 2, 3, zc, 1, xc), vmem(2, 2, 3, zc, 1, xc),
            vmem(2, yf, LANES), vmem(18, yc, LANES), vmem(9, yc, LANES), vmem(12, yc, LANES),
            vmem(2, 18, 2, LANES), vmem(2, 18, 2, LANES), vmem(2, 9, 2, LANES),
            vmem(yc, LANES), vmem(2, 24, LANES), vmem(2, 24, LANES),
            vmem(24, 24, 2 * LANES),
            pltpu.SemaphoreType.DMA((9,)),
            pltpu.SemaphoreType.DMA((4,)),
            pltpu.SemaphoreType.DMA((36,)),
            pltpu.SemaphoreType.DMA((36,)),
        ],
        compiler_params=pltpu.CompilerParams(
            collective_id=0, has_side_effects=True, vmem_limit_bytes=60 * 1024 * 1024
        ),
        name="elastic_step",
    )(*args)


def solution(mesh):
    counts = tuple(mesh.shape[name] for name in ("gz", "gy", "gx"))
    volume, field = P(None, "gz", "gy", "gx"), P("gz", "gy", "gx")
    return jax.shard_map(
        functools.partial(per_device, counts),
        mesh=mesh,
        in_specs=(volume, volume, volume, field, field, volume, volume, volume, field),
        out_specs=(volume, volume),
        check_vma=False,
    )
```

time: 183 us -> 37.4 us (0.20)
  the two profiles are of different devices: /device:TPU:482 before, /device:TPU:25 now
where the time goes in v1:
time: 37.4 us; the launch traced here: 37.3 us
  Pallas kernels  34.3 us (92%)
  local copies, waits for them, and re-layouts  2.29 us (6%)
  between operations  0.65 us (2%)
    pallas_call x1, Pallas kernels, per_device(): pl.pallas_call(functools.partial(kernel, counts), out_shape=(jax.ShapeDty...  34.3 us
    unnamed x4, local copies, waits for them, and re-layouts  2.29 us

profile of v1, /device:TPU:25, one launch (start us, length us, event | category | flops | bytes accessed | tf_op | source)
XLA Modules:
  0.0 37.3 jit_solution(16113457301347377153)
XLA Ops:
  0.6 34.3 %elastic_step.1 = (f32[3,4,16,256]{3,2,1,0:T(8,128)}, f32[3,8,8,128]{3,2,1,0:T(8,128)}) custom-call(f32[3,4,16,256]{3,2,1,0:T(8,128)} %fn.1, f32[3,4,16,256]{3,2,1,0:T(8,128)} %fp.1, f32[9,4,16,256]{3,2,1,0:T(8,128)} %st.1, f32[4,16,256]{2,1,0:T(8,128)} %me.1, f32[4,16,256]{2,1,0:T(8,128)} %de.1, f32[3,8,8,128]{3,2,1,0:T(8,128)} %cn.1, f32[3,8,8,128]{3,2,1,0:T(8,128)} %cp.1, ...), custom_call_target="tpu_custom_call" | custom-call | tf_op jit(solution)/shard_map/elastic_step/pallas_call | solution.py:484
  35.0 0.0 copy-start
  35.0 1.6 %copy.13 = f32[3,4,16,256]{3,2,1,0:T(8,128)} copy(f32[3,4,16,256]{3,2,1,0:T(8,128)} %get-tuple-element.4) | data formatting | bytes 393216
  36.6 0.0 copy-done
  36.6 0.6 %copy.14 = f32[3,8,8,128]{3,2,1,0:T(8,128)} copy(f32[3,8,8,128]{3,2,1,0:T(8,128)S(1)} %copy-done) | data formatting | bytes 196608
Async XLA Ops:
  35.0 1.7 %copy-start = (f32[3,8,8,128]{3,2,1,0:T(8,128)S(1)}, f32[3,8,8,128]{3,2,1,0:T(8,128)}, u32[]{:S(2)}) copy-start(f32[3,8,8,128]{3,2,1,0:T(8,128)} %get-tuple-element.5) | copy-start | bytes 294916

commit v2 on v1

v2 whole, which is shorter than its diff:
```python
import functools

import jax
import jax.numpy as jnp
from jax import lax
from jax.experimental import pallas as pl
from jax.experimental.pallas import tpu as pltpu
from jax.sharding import PartitionSpec as P

TIME_STEP = 0.2
ITERS = 3
F32 = jnp.float32
XX, XY, YY, XZ, YZ, ZZ = range(6)
FACE_X = (XX, XY, XZ)
FACE_Y = (XY, YY, YZ)
WIDE_Y = (1, 3, 5, 6, 8)
WIDE_X = (0, 4, 5, 6, 7)
CH = (4, 3, 2)
PAD = 8
LANES = 128


def lanes_of(rows):
    return lax.broadcasted_iota(jnp.int32, (rows, LANES), 1)


def pack_x(ref, comps, z_count, y_count, width):
    lane = lanes_of(y_count)
    packed = jnp.zeros((y_count, LANES), F32)
    k = 0
    for c in comps:
        for z in range(z_count):
            rows = pl.ds(PAD, y_count)
            tile = ref[c, z + 1, rows, 0:LANES]
            if width > LANES:
                last = ref[c, z + 1, rows, width - LANES : width]
                tile = jnp.where(lane >= LANES // 2, last, tile)
            packed = jnp.where(lane // 2 == k, pltpu.roll(tile, 2 * k + 1, 1), packed)
            k += 1
    return packed


def unpack_x(ref, comps, z_count, y_count, width, from_left, from_right):
    lane = lanes_of(y_count)
    both = jnp.where(lane % 2 == 0, from_left, from_right)
    k = 0
    for c in comps:
        for z in range(z_count):
            ref[c, z + 1, pl.ds(PAD, y_count), width : width + LANES] = pltpu.roll(
                both, LANES - 1 - 2 * k, 1
            )
            k += 1


def diff_x(ref, c, z0, zn, y_count, width, scale):
    v = ref[c, z0 : z0 + zn, PAD : PAD + y_count, :]
    span = width + LANES
    return (pltpu.roll(v, span - 1, 2) - pltpu.roll(v, 1, 2))[:, :, :width] * scale


def diff_y(ref, c, z0, zn, y_count, width, scale):
    after = ref[c, z0 : z0 + zn, PAD + 1 : PAD + 1 + y_count, 0:width]
    before = ref[c, z0 : z0 + zn, PAD - 1 : PAD - 1 + y_count, 0:width]
    return (after - before) * scale


def diff_z(ref, c, z0, zn, y_count, width, scale):
    after = ref[c, z0 + 1 : z0 + 1 + zn, PAD : PAD + y_count, 0:width]
    before = ref[c, z0 - 1 : z0 - 1 + zn, PAD : PAD + y_count, 0:width]
    return (after - before) * scale


def stress_block(u, stiff, s, z, zn, y_count, width, inv, stretch):
    args = (z + 1, zn, y_count, width, inv)
    own = (slice(z + 1, z + 1 + zn), slice(PAD, PAD + y_count), slice(0, width))
    c = [stiff[i, z : z + zn] for i in range(9)]
    nx = diff_x(u, 0, *args)
    ny = diff_y(u, 1, *args)
    nz = diff_z(u, 2, *args) * stretch
    s[(XX,) + own] = c[0] * nx + c[6] * ny + c[7] * nz
    s[(YY,) + own] = c[6] * nx + c[1] * ny + c[8] * nz
    s[(ZZ,) + own] = c[7] * nx + c[8] * ny + c[2] * nz
    s[(YZ,) + own] = c[3] * (diff_z(u, 1, *args) * stretch + diff_y(u, 2, *args))
    s[(XZ,) + own] = c[4] * (diff_z(u, 0, *args) * stretch + diff_x(u, 2, *args))
    s[(XY,) + own] = c[5] * (diff_y(u, 0, *args) + diff_x(u, 1, *args))


def step_block(u, s, prev, dens, out, z, zn, y_count, width, inv, stretch):
    args = (z + 1, zn, y_count, width, inv)
    gain = (TIME_STEP * TIME_STEP) / dens[z : z + zn]
    for c, (sx, sy, sz) in enumerate(((XX, XY, XZ), (XY, YY, YZ), (XZ, YZ, ZZ))):
        total = diff_x(s, sx, *args) + diff_y(s, sy, *args) + diff_z(s, sz, *args) * stretch
        now = u[c, z + 1 : z + 1 + zn, PAD : PAD + y_count, 0:width]
        out[c, z : z + zn] = (2.0 * now - prev[c, z : z + zn]) + gain * total


def stress_ext(u, stiff, s, layer, slab, y_count, width, inv):
    z, first, rows, span = layer + 1, PAD - 1, y_count + 2, width + LANES

    def at(c, dz, dr):
        return u[c, z + dz, first + dr : first + dr + rows, :]

    def dx(c):
        v = at(c, 0, 0)
        return (pltpu.roll(v, span - 1, 1) - pltpu.roll(v, 1, 1)) * inv

    def dy(c):
        return (at(c, 0, 1) - at(c, 0, -1)) * inv

    def dz(c):
        return (at(c, 1, 0) - at(c, -1, 0)) * inv

    c = [stiff[i, slab, first : first + rows, :] for i in range(9)]
    nx, ny, nz = dx(0), dy(1), dz(2)
    values = {
        XX: c[0] * nx + c[6] * ny + c[7] * nz,
        YY: c[6] * nx + c[1] * ny + c[8] * nz,
        ZZ: c[7] * nx + c[8] * ny + c[2] * nz,
        YZ: c[3] * (dz(1) + dy(2)),
        XZ: c[4] * (dz(0) + dx(2)),
        XY: c[5] * (dy(0) + dx(1)),
    }
    for component, value in values.items():
        s[component, z, first : first + rows, :] = value


def pick(x, index):
    return jnp.take_along_axis(x, index, axis=1, mode="promise_in_bounds")


class Grid:
    def __init__(self, **fields):
        self.__dict__.update(fields)
        self.own = (slice(1, self.z + 1), slice(PAD, PAD + self.y), slice(0, self.x))


def kernel(
    counts,
    fn, fp, st, me, de, cn, cp, cst, cde,
    fout, cout,
    u, uc, s, sc, fprev, stiff, metric, dens, cprev, cstiff, cdens,
    xs, xr, yfs, yfr, ycs, ycr,
    fwide, cwide, yef_s, yef_r, yec_s, yec_r, xef_s, xef_r, xec_s, xec_r,
    tiles, own, own_opp, ikf_opp, yi_s, yi_r, ys3, yr3, yo3, xs3, xr3, xo3, ext,
    load_sem, send_sem, recv_sem,
):
    n_z, n_y, n_x = counts
    zf, yf, xf = me.shape
    zc, yc, xc = cde.shape
    fine = Grid(
        z=zf, y=yf, x=xf, u=u, s=s, wide=fwide, source=st, stiff=stiff, third=zf - 3, prev=fprev, dens=dens, out=fout, inv=0.5,
        layers=(zf - 2, zf - 1), near=(zf - 3, zf - 2, zf - 1), ye_s=yef_s, ye_r=yef_r, xe_s=xef_s, xe_r=xef_r,
    )
    coarse = Grid(
        z=zc, y=yc, x=xc, u=uc, s=sc, wide=cwide, source=cst, stiff=cstiff, third=2, prev=cprev, dens=cdens, out=cout, inv=0.25,
        layers=(0, 1), near=(0, 1, 2), ye_s=yec_s, ye_r=yec_r, xe_s=xec_s, xe_r=xec_r,
    )
    gz, gy, gx = lax.axis_index("gz"), lax.axis_index("gy"), lax.axis_index("gx")
    opp = n_z - 1 - gz
    is_c, is_f = gz == 0, gz == n_z - 1
    active = jnp.logical_or(is_c, is_f)
    has_y = {-1: gy > 0, 0: gy >= 0, 1: gy < n_y - 1}
    has_x = {-1: gx > 0, 0: gx >= 0, 1: gx < n_x - 1}
    has = (gz > 0, gz < n_z - 1, has_y[-1], has_y[1], has_x[-1], has_x[1])
    near = (
        (gz - 1, gy, gx), (gz + 1, gy, gx),
        (gz, gy - 1, gx), (gz, gy + 1, gx),
        (gz, gy, gx - 1), (gz, gy, gx + 1),
    )

    barrier = pltpu.get_barrier_semaphore()
    expected = jnp.int32(0)

    def greet(there, device):
        @pl.when(there)
        def _():
            pl.semaphore_signal(barrier, 1, device_id=device, device_id_type=pl.DeviceIdType.MESH)

        return there.astype(jnp.int32)

    for d in (2, 3, 4, 5, 0, 1):
        expected += greet(has[d], near[d])
    for a in (-1, 1):
        for b in (-1, 1):
            there = jnp.logical_and(active, jnp.logical_and(has_y[a], has_x[b]))
            expected += greet(there, (gz, gy + a, gx + b))
    expected += greet(active, (opp, gy, gx))

    loads = [
        pltpu.make_async_copy(src, dst, load_sem.at[i])
        for i, (src, dst) in enumerate((
            (fn, u.at[(slice(None),) + fine.own]),
            (cn, uc.at[(slice(None),) + coarse.own]),
            (st, stiff), (cst, cstiff), (me, metric),
            (fp, fprev), (cp, cprev), (de, dens), (cde, cdens),
        ))
    ]

    def wide_load(g):
        return pltpu.make_async_copy(
            g.source.at[:, g.layers[0] : g.layers[1] + 1], g.wide.at[(slice(None), slice(None)) + g.own[1:]], load_sem.at[9]
        )

    sides = ((is_f, fine), (is_c, coarse))
    for load in loads[:2]:
        load.start()
    for there, g in sides:
        @pl.when(there)
        def _(g=g):
            wide_load(g).start()
    for load in loads[2:]:
        load.start()

    def clear(part):
        part[...] = jnp.zeros(part.shape, F32)

    for d in range(6):
        @pl.when(jnp.logical_not(has[d]))
        def _(d=d):
            side = d % 2
            if d < 2:
                for g in (fine, coarse):
                    plane = 0 if side == 0 else g.z + 1
                    clear(g.u.at[:, plane])
                    clear(g.s.at[3:6, plane, g.own[1], g.own[2]])
            elif d < 4:
                for r in range(2):
                    for ref in (yfr, ycr):
                        clear(ref.at[r, side])
                for g in (fine, coarse):
                    clear(g.ye_r.at[side])
                    for b in range(2):
                        rows = pl.ds(0 if side == 0 else PAD + g.y, PAD)
                        clear(g.xe_r.at[b, rows])
            else:
                for r in range(2):
                    clear(xr.at[r, side])
                for g in (fine, coarse):
                    clear(g.xe_r.at[side])

    def rdma(src, dst, slot, device):
        return pltpu.make_async_remote_copy(
            src_ref=src, dst_ref=dst, send_sem=send_sem.at[slot], recv_sem=recv_sem.at[slot],
            device_id=device, device_id_type=pl.DeviceIdType.MESH,
        )

    def round_copies(r, d):
        side = d % 2
        arrival = 1 - side
        slot = (r * 6 + d) * 2
        if d < 2:
            comps = (slice(0, 3), slice(3, 6))[r]
            made = []
            for i, g in enumerate((fine, coarse)):
                ref = (g.u, g.s)[r]
                sent, landed = (1, g.z + 1) if side == 0 else (g.z, 0)
                made.append(rdma(
                    ref.at[comps, sent, g.own[1], g.own[2]], ref.at[comps, landed, g.own[1], g.own[2]], slot + i, near[d]
                ))
            return made
        if d < 4:
            return [
                rdma(yfs.at[r, side], yfr.at[r, arrival], slot, near[d]),
                rdma(ycs.at[r, side], ycr.at[r, arrival], slot + 1, near[d]),
            ]
        return [rdma(xs.at[r], xr.at[r, arrival], slot, near[d])]

    def start_round(r, directions):
        for d in directions:
            @pl.when(has[d])
            def _(d=d):
                for copy in round_copies(r, d):
                    copy.start()

    def end_round(r, directions):
        for d in directions:
            @pl.when(has[d ^ 1])
            def _(d=d):
                for copy in round_copies(r, d):
                    copy.wait_recv()

    def pack_rows(r, refs, face_y):
        for g, ref, out in ((fine, refs[0], yfs), (coarse, refs[1], ycs)):
            for i, c in enumerate(face_y):
                out[r, 0, i] = ref[c, 1 : g.z + 1, PAD : PAD + 1, 0 : g.x]
                out[r, 1, i] = ref[c, 1 : g.z + 1, PAD + g.y - 1 : PAD + g.y, 0 : g.x]

    def pack_columns(r, refs, face_x):
        xs[r, 0:yf] = pack_x(refs[0], face_x, zf, yf, xf)
        xs[r, yf : yf + yc] = pack_x(refs[1], face_x, zc, yc, xc)

    def unpack_rows(r, g, ref, landed, face_y):
        for i, c in enumerate(face_y):
            ref[c, 1 : g.z + 1, PAD - 1 : PAD, 0 : g.x] = landed[r, 0, i]
            ref[c, 1 : g.z + 1, PAD + g.y : PAD + g.y + 1, 0 : g.x] = landed[r, 1, i]

    def unpack(r, refs, face_x, face_y):
        unpack_rows(r, fine, refs[0], yfr, face_y)
        unpack_rows(r, coarse, refs[1], ycr, face_y)
        unpack_x(refs[0], face_x, zf, yf, xf, xr[r, 0, 0:yf], xr[r, 1, 0:yf])
        unpack_x(refs[1], face_x, zc, yc, xc, xr[r, 0, yf : yf + yc], xr[r, 1, yf : yf + yc])

    def pack_wide(g):
        first = g.layers[0]
        for side, (edge, second) in enumerate(((PAD, PAD + 1), (PAD + g.y - 1, PAD + g.y - 2))):
            for c in range(3):
                g.ye_s[side, c] = g.u[c, first + 1 : first + 3, second : second + 1, 0 : g.x]
            for i, c in enumerate(WIDE_Y):
                g.ye_s[side, 3 + i] = g.wide[c, :, edge : edge + 1, 0 : g.x]
        lane = lanes_of(g.y)
        packed = jnp.zeros((g.y, LANES), F32)
        for k, (ref, index) in enumerate(wide_blocks(g)):
            tile = ref[index + (g.own[1], slice(0, LANES))]
            if g.x > LANES:
                last = ref[index + (g.own[1], slice(g.x - LANES, g.x))]
                tile = jnp.where(lane >= LANES // 2, last, tile)
            packed = jnp.where(lane // 4 == k, pltpu.roll(tile, 4 * k + 2, 1), packed)
        g.xe_s[...] = packed

    def wide_blocks(g):
        blocks = [(g.u, (c, z + 1)) for c in range(3) for z in g.near]
        return blocks + [(g.wide, (c, l)) for c in WIDE_X for l in range(2)]

    def wide_rows(g):
        return [
            (has_y[a], has_y[-a], rdma(g.ye_s.at[i], g.ye_r.at[1 - i], 26 + i, (gz, gy + a, gx)))
            for i, a in enumerate((-1, 1))
        ]

    def wide_columns(g):
        made = []
        for i, b in enumerate((-1, 1)):
            for a in (-1, 0, 1):
                src, dst = {
                    -1: (slice(0, PAD), slice(PAD + g.y, 2 * PAD + g.y)),
                    0: (slice(0, g.y), slice(PAD, PAD + g.y)),
                    1: (slice(g.y - PAD, g.y), slice(0, PAD)),
                }[a]
                made.append((
                    jnp.logical_and(has_y[a], has_x[b]), jnp.logical_and(has_y[-a], has_x[-b]),
                    rdma(g.xe_s.at[src], g.xe_r.at[1 - i, dst], 28 + i * 3 + (a + 1), (gz, gy + a, gx + b)),
                ))
        return made

    def unpack_wide(g):
        first = g.layers[0]
        unpack_rows(0, g, g.u, yfr if g is fine else ycr, (0, 1, 2))
        for side, (edge, second) in enumerate(((PAD - 1, PAD - 2), (PAD + g.y, PAD + g.y + 1))):
            for c in range(3):
                g.u[c, first + 1 : first + 3, second : second + 1, 0 : g.x] = g.ye_r[side, c]
            for i, c in enumerate(WIDE_Y):
                g.wide[c, :, edge : edge + 1, 0 : g.x] = g.ye_r[side, 3 + i]
        rows = g.y + 2 * PAD
        both = jnp.where(lanes_of(rows) % 4 < 2, g.xe_r[0], g.xe_r[1])
        for k, (ref, index) in enumerate(wide_blocks(g)):
            ref[index + (slice(0, rows), slice(g.x, g.x + LANES))] = pltpu.roll(both, LANES - (4 * k + 2), 1)

    def start_all(copies):
        for there, _, copy in copies:
            @pl.when(there)
            def _(copy=copy):
                copy.start()

    def receive_all(copies):
        for _, comes, copy in copies:
            @pl.when(comes)
            def _(copy=copy):
                copy.wait_recv()

    def sent_all(copies):
        for there, _, copy in copies:
            @pl.when(there)
            def _(copy=copy):
                copy.wait_send()

    with jax.named_scope("load_pack"):
        loads[0].wait()
        loads[1].wait()
        pack_rows(0, (u, uc), (0, 1, 2))
        for there, g in sides:
            @pl.when(there)
            def _(g=g):
                wide_load(g).wait()
                pack_wide(g)
        pack_columns(0, (u, uc), (0, 1, 2))
    with jax.named_scope("barrier"):
        pl.semaphore_wait(barrier, expected)
    with jax.named_scope("send_0"):
        start_round(0, (2, 3))
        for there, g in sides:
            @pl.when(there)
            def _(g=g):
                start_all(wide_rows(g))
                start_all(wide_columns(g))
        start_round(0, (4, 5, 0, 1))
        for load in loads[2:]:
            load.wait()

    lane = lanes_of(yc)
    even = (2 * lane) % LANES

    def squeeze(left, right, odd):
        return jnp.where(lane < LANES // 2, pick(left, even + odd), pick(right, even + odd))

    ikf_copy = rdma(own.at[6:18], ikf_opp, 24, (opp, gy, gx))
    ikf_rows = [
        (has_y[a], has_y[-a], rdma(yi_s.at[i], yi_r.at[1 - i], 34 + i, (gz, gy + a, gx))) for i, a in enumerate((-1, 1))
    ]

    @pl.when(is_f)
    def _():
        for c in range(3):
            inverse = 1.0 / stiff[CH[c], zf - 1]
            for t in range(2):
                tiles[t] = inverse[:, t * LANES : (t + 1) * LANES]
            for py in range(2):
                rows = pl.ds(py, yc, stride=2)
                left, right = tiles[0, rows, :], tiles[1, rows, :]
                for px in range(2):
                    own[6 + c * 4 + py * 2 + px] = squeeze(left, right, px)
        yi_s[0] = own[6:18, 0:2, :]
        yi_s[1] = own[6:18, yc - 2 : yc, :]
        ikf_copy.start()
        start_all(ikf_rows)

    with jax.named_scope("wait_wide"):
        for there, g in sides:
            @pl.when(there)
            def _(g=g):
                receive_all(wide_rows(g))
                receive_all(wide_columns(g))
                for d in (2, 3):
                    @pl.when(has[d ^ 1])
                    def _(d=d):
                        round_copies(0, d)[0 if g is fine else 1].wait_recv()

    for there, g in sides:
        @pl.when(there)
        def _(g=g):
            unpack_wide(g)
            stress_block(g.u, g.stiff, g.s, g.third, 1, g.y, g.x, g.inv, 1.0)
            for l, z in enumerate(g.layers):
                stress_ext(g.u, g.wide, g.s, z, l, g.y, g.x, g.inv)
            for z in g.layers:
                step_block(g.u, g.s, g.prev, g.dens, g.out, z, 1, g.y, g.x, g.inv, 1.0)

    @pl.when(is_c)
    def _():
        for c in range(3):
            start, below = cout[c, 0], cout[c, 1]
            k = cstiff[CH[c], 0] * 0.25
            own[c] = k * (below - start)
            own[3 + c] = below - 0.5 * start
            own[6 + c] = k

    @pl.when(is_f)
    def _():
        for c in range(3):
            for i, z in enumerate((zf - 2, zf - 1)):
                plane = fout[c, z]
                sums = []
                for t in range(2):
                    tiles[t] = plane[:, t * LANES : (t + 1) * LANES]
                    pair = tiles[t, pl.ds(0, yc, stride=2), :] + tiles[t, pl.ds(1, yc, stride=2), :]
                    sums.append(pair + pltpu.roll(pair, LANES - 1, 1))
                own[3 * i + c] = squeeze(sums[0], sums[1], 0) * 0.25

    fields = 18
    lane4 = lane // 4
    own_copy = rdma(own.at[0:9], own_opp, 25, (opp, gy, gx))
    strips = []
    for level, rows_to, tile_to, slot in ((opp, yo3, xo3, 36), (gz, yr3, xr3, 44)):
        for i, a in enumerate((-1, 1)):
            strips.append((
                jnp.logical_and(active, has_y[a]), jnp.logical_and(active, has_y[-a]),
                rdma(ys3.at[i], rows_to.at[1 - i], slot + i, (level, gy + a, gx)),
            ))
        for i, b in enumerate((-1, 1)):
            for a in (-1, 0, 1):
                strips.append((
                    jnp.logical_and(active, jnp.logical_and(has_y[a], has_x[b])),
                    jnp.logical_and(active, jnp.logical_and(has_y[-a], has_x[-b])),
                    rdma(xs3, tile_to.at[1 - i, pl.ds((1 - a) * 8, 8)], slot + 2 + i * 3 + (a + 1), (level, gy + a, gx + b)),
                ))
    opp_strips, level_strips = strips[:8], strips[8:]

    @pl.when(active)
    def _():
        ys3[0] = own[0:9, 0:2, :]
        ys3[1] = own[0:9, yc - 2 : yc, :]
        packed = jnp.zeros((yc, LANES), F32)
        for k in range(fields):
            packed = jnp.where(lane4 == k, pltpu.roll(own[k], 4 * k + 2, 1), packed)
        xs3[...] = packed
        own_copy.start()

    start_all(strips)

    def stretch_of(z):
        return jnp.where(gz * zf + z < n_z * zf // 2, metric[z : z + 1], 1.0)

    zb = min(4, zc)

    with jax.named_scope("wait_0"):
        @pl.when(jnp.logical_not(is_f))
        def _():
            for d in (2, 3):
                @pl.when(has[d ^ 1])
                def _(d=d):
                    round_copies(0, d)[0].wait_recv()

        @pl.when(jnp.logical_not(is_c))
        def _():
            for d in (2, 3):
                @pl.when(has[d ^ 1])
                def _(d=d):
                    round_copies(0, d)[1].wait_recv()

        end_round(0, (0, 1, 4, 5))
    with jax.named_scope("stress"):
        unpack(0, (u, uc), (0, 1, 2), (0, 1, 2))
        for z in range(zf):
            stress_block(u, stiff, s, z, 1, yf, xf, 0.5, stretch_of(z))
        for z in range(0, zc, zb):
            stress_block(uc, cstiff, sc, z, zb, yc, xc, 0.25, 1.0)
    with jax.named_scope("pack_1"):
        pack_rows(1, (s, sc), FACE_Y)
        start_round(1, (2, 3))
        pack_columns(1, (s, sc), FACE_X)
        start_round(1, (4, 5, 0, 1))
    with jax.named_scope("wait_1"):
        end_round(1, (0, 1, 4, 5, 2, 3))
    with jax.named_scope("step"):
        unpack(1, (s, sc), FACE_X, FACE_Y)
        for z in range(zf):
            step_block(u, s, fprev, dens, fout, z, 1, yf, xf, 0.5, stretch_of(z))
        for z in range(0, zc, zb):
            step_block(uc, sc, cprev, cdens, cout, z, zb, yc, xc, 0.25, 1.0)

    lane24 = lax.broadcasted_iota(jnp.int32, (24, LANES), 1)
    wide_row = lax.broadcasted_iota(jnp.int32, (24, 2 * LANES), 0)
    wide_lane = lax.broadcasted_iota(jnp.int32, (24, 2 * LANES), 1)

    def extend(k, field, centre, rims, row, edges):
        ext[k, 8:16, 0:LANES] = centre
        ext[k, 6:8, 0:LANES] = rims[0, row]
        ext[k, 16:18, 0:LANES] = rims[1, row]
        ext[k, :, LANES : 2 * LANES] = pltpu.roll(edges, LANES - (4 * field + 2), 1)

    def clamp(t):
        t = jnp.where(jnp.logical_and(wide_row == 7, gy == 0), pltpu.roll(t, 23, 0), t)
        t = jnp.where(jnp.logical_and(wide_row == 16, gy == n_y - 1), pltpu.roll(t, 1, 0), t)
        t = jnp.where(jnp.logical_and(wide_lane == 2 * LANES - 1, gx == 0), pltpu.roll(t, 2 * LANES - 1, 1), t)
        return jnp.where(jnp.logical_and(wide_lane == LANES, gx == n_x - 1), pltpu.roll(t, 1, 1), t)

    def along_y(t):
        return (0.75 * t + 0.25 * pltpu.roll(t, 1, 0), 0.75 * t + 0.25 * pltpu.roll(t, 23, 0))

    def along_x(t):
        return (0.75 * t + 0.25 * pltpu.roll(t, 1, 1), 0.75 * t + 0.25 * pltpu.roll(t, 2 * LANES - 1, 1))

    with jax.named_scope("wait_level"):
        receive_all(level_strips)

        @pl.when(is_f)
        def _():
            receive_all(ikf_rows)

    @pl.when(is_c)
    def _():
        edges = jnp.where(lane24 % 4 < 2, xr3[0], xr3[1])
        for k in range(3, 9):
            extend(k, k, own[k], yr3, k, edges)
        ikf_copy.wait_recv()

    @pl.when(is_f)
    def _():
        edges = jnp.where(lane24 % 4 < 2, xr3[0], xr3[1])
        for k in range(3):
            extend(9 + k, k, own[k], yr3, k, edges)
        for k in range(12):
            extend(12 + k, 6 + k, own[6 + k], yi_r, k, edges)

    with jax.named_scope("wait_opp"):
        @pl.when(active)
        def _():
            own_copy.wait_recv()

        receive_all(opp_strips)

    @pl.when(is_c)
    def _():
        edges = jnp.where(lane24 % 4 < 2, xo3[0], xo3[1])
        for c in range(3):
            extend(9 + c, 3 + c, own_opp[3 + c], yo3, 3 + c, edges)
            t1 = clamp(ext[6 + c] * (ext[3 + c] - 0.5 * ext[9 + c]))
            total = jnp.zeros((yc, LANES), F32)
            for py, part in enumerate(along_y(t1)):
                for px, full in enumerate(along_x(part[8:16])):
                    total += full[:, 0:LANES] * ikf_opp[c * 4 + py * 2 + px]
            cout[c, 0] = 0.5 * (cout[c, 0] + own_opp[c] + 0.25 * total)

    @pl.when(is_f)
    def _():
        edges = jnp.where(lane24 % 4 < 2, xo3[0], xo3[1])
        half = lane // 2
        for c in range(3):
            for k in (c, 3 + c, 6 + c):
                extend(k, k, own_opp[k], yo3, k, edges)
            total = jnp.zeros((24, 2 * LANES), F32)
            for py, part in enumerate(along_y(clamp(ext[c]))):
                for px, full in enumerate(along_x(part)):
                    total += full * ext[12 + c * 4 + py * 2 + px]
            t2 = clamp(ext[6 + c] * (ext[3 + c] - 0.5 * (ext[9 + c] + 0.25 * total)))
            for py, part in enumerate(along_y(t2)):
                evens, odds = along_x(part[8:16])
                evens, odds = evens[:, 0:LANES], odds[:, 0:LANES]
                for t in range(2):
                    index = half + t * (LANES // 2)
                    tiles[t, pl.ds(py, yc, stride=2), :] = jnp.where(
                        lane % 2 == 0, pick(evens, index), pick(odds, index)
                    )
            for t in range(2):
                cols = slice(t * LANES, (t + 1) * LANES)
                fout[c, zf - 1, :, cols] = fout[c, zf - 2, :, cols] + tiles[t] / stiff[CH[c], zf - 1, :, cols]

    with jax.named_scope("drain"):
        for r in range(2):
            for d in range(6):
                @pl.when(has[d])
                def _(r=r, d=d):
                    for copy in round_copies(r, d):
                        copy.wait_send()
        sent_all(strips)
        for there, g in sides:
            @pl.when(there)
            def _(g=g):
                sent_all(wide_rows(g))
                sent_all(wide_columns(g))

        @pl.when(is_f)
        def _():
            ikf_copy.wait_send()
            sent_all(ikf_rows)

        @pl.when(active)
        def _():
            own_copy.wait_send()


def per_device(counts, *args):
    fine, coarse = args[0].shape, args[5].shape
    _, zf, yf, xf = fine
    _, zc, yc, xc = coarse
    vmem = lambda *shape: pltpu.VMEM(shape, F32)
    anywhere = pl.BlockSpec(memory_space=pl.ANY)
    in_vmem = pl.BlockSpec(memory_space=pltpu.VMEM)
    return pl.pallas_call(
        functools.partial(kernel, counts),
        out_shape=(pltpu.VMEM(fine, F32), pltpu.VMEM(coarse, F32)),
        in_specs=[anywhere] * 9,
        out_specs=(in_vmem, in_vmem),
        scratch_shapes=[
            vmem(3, zf + 2, yf + 2 * PAD, xf + LANES),
            vmem(3, zc + 2, yc + 2 * PAD, xc + LANES),
            vmem(6, zf + 2, yf + 2 * PAD, xf + LANES),
            vmem(6, zc + 2, yc + 2 * PAD, xc + LANES),
            vmem(3, zf, yf, xf), vmem(9, zf, yf, xf), vmem(zf, yf, xf), vmem(zf, yf, xf),
            vmem(3, zc, yc, xc), vmem(9, zc, yc, xc), vmem(zc, yc, xc),
            vmem(2, yf + yc, LANES), vmem(2, 2, yf + yc, LANES),
            vmem(2, 2, 3, zf, 1, xf), vmem(2, 2, 3, zf, 1, xf),
            vmem(2, 2, 3, zc, 1, xc), vmem(2, 2, 3, zc, 1, xc),
            vmem(9, 2, yf + 2 * PAD, xf + LANES), vmem(9, 2, yc + 2 * PAD, xc + LANES),
            vmem(2, 8, 2, 1, xf), vmem(2, 8, 2, 1, xf), vmem(2, 8, 2, 1, xc), vmem(2, 8, 2, 1, xc),
            vmem(yf, LANES), vmem(2, yf + 2 * PAD, LANES), vmem(yc, LANES), vmem(2, yc + 2 * PAD, LANES),
            vmem(2, yf, LANES), vmem(18, yc, LANES), vmem(9, yc, LANES), vmem(12, yc, LANES),
            vmem(2, 12, 2, LANES), vmem(2, 12, 2, LANES),
            vmem(2, 9, 2, LANES), vmem(2, 9, 2, LANES), vmem(2, 9, 2, LANES),
            vmem(yc, LANES), vmem(2, 24, LANES), vmem(2, 24, LANES),
            vmem(24, 24, 2 * LANES),
            pltpu.SemaphoreType.DMA((10,)),
            pltpu.SemaphoreType.DMA((52,)),
            pltpu.SemaphoreType.DMA((52,)),
        ],
        compiler_params=pltpu.CompilerParams(
            collective_id=0, has_side_effects=True, vmem_limit_bytes=56 * 1024 * 1024
        ),
        name="elastic_step",
    )(*args)


def solution(mesh):
    counts = tuple(mesh.shape[name] for name in ("gz", "gy", "gx"))
    volume, field = P(None, "gz", "gy", "gx"), P("gz", "gy", "gx")
    return jax.shard_map(
        functools.partial(per_device, counts),
        mesh=mesh,
        in_specs=(volume, volume, volume, field, field, volume, volume, volume, field),
        out_specs=(volume, volume),
        check_vma=False,
    )
```

time: 37.4 us -> 31 us (0.83)
  Pallas kernels: 34.3 us -> 28.8 us
  local copies, waits for them, and re-layouts: 2.29 us -> 1.32 us
    pallas_call x1, Pallas kernels: 34.3 us -> 28.8 us  [per_device(): pl.pallas_call(functools.partial(kernel, counts), out_shape=(pltpu.VMEM(f...]
    unnamed x4 -> x2, local copies, waits for them, and re-layouts: 2.29 us -> 1.32 us
where the time goes in v2:
time: 31 us; the launch traced here: 30.7 us
  Pallas kernels  28.8 us (93%)
  local copies, waits for them, and re-layouts  1.32 us (4%)
  between operations  0.64 us (2%)
    pallas_call x1, Pallas kernels, per_device(): pl.pallas_call(functools.partial(kernel, counts), out_shape=(pltpu.VMEM(f...  28.8 us
    unnamed x2, local copies, waits for them, and re-layouts  1.32 us

profile of v2, /device:TPU:25, one launch (start us, length us, event | category | flops | bytes accessed | tf_op | source)
XLA Modules:
  0.0 30.7 jit_solution(6514623868588098558)
XLA Ops:
  0.6 28.8 %elastic_step.1 = (f32[3,4,16,256]{3,2,1,0:T(8,128)S(1)}, f32[3,8,8,128]{3,2,1,0:T(8,128)S(1)}) custom-call(f32[3,4,16,256]{3,2,1,0:T(8,128)} %fn.1, f32[3,4,16,256]{3,2,1,0:T(8,128)} %fp.1, f32[9,4,16,256]{3,2,1,0:T(8,128)} %st.1, f32[4,16,256]{2,1,0:T(8,128)} %me.1, f32[4,16,256]{2,1,0:T(8,128)} %de.1, f32[3,8,8,128]{3,2,1,0:T(8,128)} %cn.1, ...), custom_call_target="tpu_custom_call" | custom-call | tf_op jit(solution)/shard_map/elastic_step/pallas_call | solution.py:658
  29.4 0.7 %copy.13 = f32[3,4,16,256]{3,2,1,0:T(8,128)} copy(f32[3,4,16,256]{3,2,1,0:T(8,128)S(1)} %get-tuple-element.2) | data formatting | bytes 393216
  30.1 0.6 %copy.14 = f32[3,8,8,128]{3,2,1,0:T(8,128)} copy(f32[3,8,8,128]{3,2,1,0:T(8,128)S(1)} %get-tuple-element.3) | data formatting | bytes 196608

commit v3 on v2

--- a/solution.py
+++ b/solution.py
@@ -139,21 +139,22 @@
     fn, fp, st, me, de, cn, cp, cst, cde,
     fout, cout,
     u, uc, s, sc, fprev, stiff, metric, dens, cprev, cstiff, cdens,
-    xs, xr, yfs, yfr, ycs, ycr,
+    xs, xr, ys, yr,
     fwide, cwide, yef_s, yef_r, yec_s, yec_r, xef_s, xef_r, xec_s, xec_r,
-    tiles, own, own_opp, ikf_opp, yi_s, yi_r, ys3, yr3, yo3, xs3, xr3, xo3, ext,
+    npf_s, npf_r, npc_s, npc_r,
+    tiles, sums, own, own_opp, ikf_opp, yi_s, yi_r, ys3, yo3, xs3, xr3, xo3, ext,
     load_sem, send_sem, recv_sem,
 ):
     n_z, n_y, n_x = counts
     zf, yf, xf = me.shape
     zc, yc, xc = cde.shape
     fine = Grid(
-        z=zf, y=yf, x=xf, u=u, s=s, wide=fwide, source=st, stiff=stiff, third=zf - 3, prev=fprev, dens=dens, out=fout, inv=0.5,
-        layers=(zf - 2, zf - 1), near=(zf - 3, zf - 2, zf - 1), ye_s=yef_s, ye_r=yef_r, xe_s=xef_s, xe_r=xef_r,
+        z=zf, y=yf, x=xf, u=u, s=s, wide=fwide, source=st, stiff=stiff, third=0, prev=fprev, dens=dens, out=fout, inv=0.5,
+        slabs=(1, 2), near=zf - 3, np_s=npf_s, np_r=npf_r, ye_s=yef_s, ye_r=yef_r, xe_s=xef_s, xe_r=xef_r,
     )
     coarse = Grid(
         z=zc, y=yc, x=xc, u=uc, s=sc, wide=cwide, source=cst, stiff=cstiff, third=2, prev=cprev, dens=cdens, out=cout, inv=0.25,
-        layers=(0, 1), near=(0, 1, 2), ye_s=yec_s, ye_r=yec_r, xe_s=xec_s, xe_r=xec_r,
+        slabs=(0, 1), near=0, np_s=npc_s, np_r=npc_r, ye_s=yec_s, ye_r=yec_r, xe_s=xec_s, xe_r=xec_r,
     )
     gz, gy, gx = lax.axis_index("gz"), lax.axis_index("gy"), lax.axis_index("gx")
     opp = n_z - 1 - gz
@@ -191,14 +192,14 @@
         for i, (src, dst) in enumerate((
             (fn, u.at[(slice(None),) + fine.own]),
             (cn, uc.at[(slice(None),) + coarse.own]),
+            (de, dens), (cde, cdens), (fp, fprev), (cp, cprev),
             (st, stiff), (cst, cstiff), (me, metric),
-            (fp, fprev), (cp, cprev), (de, dens), (cde, cdens),
         ))
     ]
 
     def wide_load(g):
         return pltpu.make_async_copy(
-            g.source.at[:, g.layers[0] : g.layers[1] + 1], g.wide.at[(slice(None), slice(None)) + g.own[1:]], load_sem.at[9]
+            g.source.at[:, g.near : g.near + 3], g.wide.at[(slice(None), slice(None)) + g.own[1:]], load_sem.at[9]
         )
 
     sides = ((is_f, fine), (is_c, coarse))
@@ -213,6 +214,13 @@
 
     def clear(part):
         part[...] = jnp.zeros(part.shape, F32)
+
+    for there, g in sides:
+        @pl.when(there)
+        def _(g=g):
+            for rows in (pl.ds(0, PAD), pl.ds(PAD + g.y, PAD)):
+                clear(g.u.at[:, g.near + 1 : g.near + 4, rows])
+                clear(g.wide.at[:, :, rows])
 
     for d in range(6):
         @pl.when(jnp.logical_not(has[d]))
@@ -225,29 +233,27 @@
                     clear(g.s.at[3:6, plane, g.own[1], g.own[2]])
             elif d < 4:
                 for r in range(2):
-                    for ref in (yfr, ycr):
-                        clear(ref.at[r, side])
+                    clear(yr.at[r, side])
                 for g in (fine, coarse):
                     clear(g.ye_r.at[side])
+                    clear(g.np_r.at[side])
                     for b in range(2):
-                        rows = pl.ds(0 if side == 0 else PAD + g.y, PAD)
-                        clear(g.xe_r.at[b, rows])
+                        clear(g.xe_r.at[b, pl.ds(0 if side == 0 else PAD + g.y, PAD)])
             else:
                 for r in range(2):
                     clear(xr.at[r, side])
                 for g in (fine, coarse):
                     clear(g.xe_r.at[side])
 
-    def rdma(src, dst, slot, device):
+    def rdma(src, dst, out, into, device):
         return pltpu.make_async_remote_copy(
-            src_ref=src, dst_ref=dst, send_sem=send_sem.at[slot], recv_sem=recv_sem.at[slot],
+            src_ref=src, dst_ref=dst, send_sem=send_sem.at[out], recv_sem=recv_sem.at[into],
             device_id=device, device_id_type=pl.DeviceIdType.MESH,
         )
 
     def round_copies(r, d):
         side = d % 2
         arrival = 1 - side
-        slot = (r * 6 + d) * 2
         if d < 2:
             comps = (slice(0, 3), slice(3, 6))[r]
             made = []
@@ -255,15 +261,13 @@
                 ref = (g.u, g.s)[r]
                 sent, landed = (1, g.z + 1) if side == 0 else (g.z, 0)
                 made.append(rdma(
-                    ref.at[comps, sent, g.own[1], g.own[2]], ref.at[comps, landed, g.own[1], g.own[2]], slot + i, near[d]
+                    ref.at[comps, sent, g.own[1], g.own[2]], ref.at[comps, landed, g.own[1], g.own[2]],
+                    2 * d + i, 8 * r + 2 * d + i, near[d],
                 ))
             return made
         if d < 4:
-            return [
-                rdma(yfs.at[r, side], yfr.at[r, arrival], slot, near[d]),
-                rdma(ycs.at[r, side], ycr.at[r, arrival], slot + 1, near[d]),
-            ]
-        return [rdma(xs.at[r], xr.at[r, arrival], slot, near[d])]
+            return [rdma(ys.at[r, side], yr.at[r, arrival], d + 2, 8 * r + d + 2, near[d])]
+        return [rdma(xs.at[r], xr.at[r, arrival], d + 2, 8 * r + d + 2, near[d])]
 
     def start_round(r, directions):
         for d in directions:
@@ -279,34 +283,56 @@
                 for copy in round_copies(r, d):
                     copy.wait_recv()
 
+    def row_parts(g, ref, c, row):
+        if g is fine:
+            return [(ref.at[c, 1 : zf + 1, row : row + 1, 0:xf], (c, slice(0, zf), slice(None), slice(0, xf)))]
+        half = zc // 2
+        return [
+            (
+                ref.at[c, 1 + i * half : 1 + (i + 1) * half, row : row + 1, 0:xc],
+                (c, slice(zf, zf + half), slice(None), slice(i * xc, (i + 1) * xc)),
+            )
+            for i in range(2)
+        ]
+
     def pack_rows(r, refs, face_y):
-        for g, ref, out in ((fine, refs[0], yfs), (coarse, refs[1], ycs)):
-            for i, c in enumerate(face_y):
-                out[r, 0, i] = ref[c, 1 : g.z + 1, PAD : PAD + 1, 0 : g.x]
-                out[r, 1, i] = ref[c, 1 : g.z + 1, PAD + g.y - 1 : PAD + g.y, 0 : g.x]
+        for g, ref in ((fine, refs[0]), (coarse, refs[1])):
+            for side, row in enumerate((PAD, PAD + g.y - 1)):
+                for i, c in enumerate(face_y):
+                    for part, place in row_parts(g, ref, c, row):
+                        ys[(r, side, i) + place[1:]] = part[...]
 
     def pack_columns(r, refs, face_x):
         xs[r, 0:yf] = pack_x(refs[0], face_x, zf, yf, xf)
         xs[r, yf : yf + yc] = pack_x(refs[1], face_x, zc, yc, xc)
 
-    def unpack_rows(r, g, ref, landed, face_y):
-        for i, c in enumerate(face_y):
-            ref[c, 1 : g.z + 1, PAD - 1 : PAD, 0 : g.x] = landed[r, 0, i]
-            ref[c, 1 : g.z + 1, PAD + g.y : PAD + g.y + 1, 0 : g.x] = landed[r, 1, i]
+    def unpack_rows(r, g, ref, face_y):
+        for side, row in enumerate((PAD - 1, PAD + g.y)):
+            for i, c in enumerate(face_y):
+                for part, place in row_parts(g, ref, c, row):
+                    part[...] = yr[(r, side, i) + place[1:]]
 
     def unpack(r, refs, face_x, face_y):
-        unpack_rows(r, fine, refs[0], yfr, face_y)
-        unpack_rows(r, coarse, refs[1], ycr, face_y)
+        unpack_rows(r, fine, refs[0], face_y)
+        unpack_rows(r, coarse, refs[1], face_y)
         unpack_x(refs[0], face_x, zf, yf, xf, xr[r, 0, 0:yf], xr[r, 1, 0:yf])
         unpack_x(refs[1], face_x, zc, yc, xc, xr[r, 0, yf : yf + yc], xr[r, 1, yf : yf + yc])
 
-    def pack_wide(g):
-        first = g.layers[0]
+    def pack_wide_rows(g):
+        first = g.near + g.slabs[0]
         for side, (edge, second) in enumerate(((PAD, PAD + 1), (PAD + g.y - 1, PAD + g.y - 2))):
+            out = g.ye_s.at[side]
             for c in range(3):
-                g.ye_s[side, c] = g.u[c, first + 1 : first + 3, second : second + 1, 0 : g.x]
+                out[2 * c : 2 * c + 2] = g.u[c, first + 1 : first + 3, second : second + 1, 0 : g.x]
             for i, c in enumerate(WIDE_Y):
-                g.ye_s[side, 3 + i] = g.wide[c, :, edge : edge + 1, 0 : g.x]
+                out[6 + 3 * i : 9 + 3 * i] = g.wide[c, :, edge : edge + 1, 0 : g.x]
+            for i, row in enumerate((edge, second)):
+                out[21 + 2 * i : 23 + 2 * i] = g.dens[first : first + 2, row - PAD : row - PAD + 1, :]
+                if g is coarse:
+                    for c in range(3):
+                        out[25 + 3 * i + c] = g.wide[CH[c], 0, row : row + 1, 0 : g.x]
+
+    def pack_wide_columns(g):
         lane = lanes_of(g.y)
         packed = jnp.zeros((g.y, LANES), F32)
         for k, (ref, index) in enumerate(wide_blocks(g)):
@@ -318,19 +344,19 @@
         g.xe_s[...] = packed
 
     def wide_blocks(g):
-        blocks = [(g.u, (c, z + 1)) for c in range(3) for z in g.near]
-        return blocks + [(g.wide, (c, l)) for c in WIDE_X for l in range(2)]
+        blocks = [(g.u, (c, g.near + l + 1)) for c in range(3) for l in range(3)]
+        return blocks + [(g.wide, (c, l)) for c in WIDE_X for l in g.slabs]
 
     def wide_rows(g):
         return [
-            (has_y[a], has_y[-a], rdma(g.ye_s.at[i], g.ye_r.at[1 - i], 26 + i, (gz, gy + a, gx)))
+            (has_y[a], has_y[-a], rdma(g.ye_s.at[i], g.ye_r.at[1 - i], 11 + i, 19 + i, (gz, gy + a, gx)))
             for i, a in enumerate((-1, 1))
         ]
 
-    def wide_columns(g):
+    def wide_columns(g, ups):
         made = []
         for i, b in enumerate((-1, 1)):
-            for a in (-1, 0, 1):
+            for a in ups:
                 src, dst = {
                     -1: (slice(0, PAD), slice(PAD + g.y, 2 * PAD + g.y)),
                     0: (slice(0, g.y), slice(PAD, PAD + g.y)),
@@ -338,22 +364,84 @@
                 }[a]
                 made.append((
                     jnp.logical_and(has_y[a], has_x[b]), jnp.logical_and(has_y[-a], has_x[-b]),
-                    rdma(g.xe_s.at[src], g.xe_r.at[1 - i, dst], 28 + i * 3 + (a + 1), (gz, gy + a, gx + b)),
+                    rdma(
+                        g.xe_s.at[src], g.xe_r.at[1 - i, dst], 13 + i * 3 + (a + 1), 21 + i * 3 + (a + 1),
+                        (gz, gy + a, gx + b),
+                    ),
                 ))
         return made
 
-    def unpack_wide(g):
-        first = g.layers[0]
-        unpack_rows(0, g, g.u, yfr if g is fine else ycr, (0, 1, 2))
+    def part_rows(g):
+        return [
+            (has_y[a], has_y[-a], rdma(g.np_s.at[i], g.np_r.at[1 - i], 19 + i, 27 + i, (gz, gy + a, gx)))
+            for i, a in enumerate((-1, 1))
+        ]
+
+    def unpack_wide_rows(g):
+        first = g.near + g.slabs[0]
+        unpack_rows(0, g, g.u, (0, 1, 2))
         for side, (edge, second) in enumerate(((PAD - 1, PAD - 2), (PAD + g.y, PAD + g.y + 1))):
+            landed = g.ye_r.at[side]
             for c in range(3):
-                g.u[c, first + 1 : first + 3, second : second + 1, 0 : g.x] = g.ye_r[side, c]
+                g.u[c, first + 1 : first + 3, second : second + 1, 0 : g.x] = landed[2 * c : 2 * c + 2]
             for i, c in enumerate(WIDE_Y):
-                g.wide[c, :, edge : edge + 1, 0 : g.x] = g.ye_r[side, 3 + i]
-        rows = g.y + 2 * PAD
-        both = jnp.where(lanes_of(rows) % 4 < 2, g.xe_r[0], g.xe_r[1])
+                g.wide[c, :, edge : edge + 1, 0 : g.x] = landed[6 + 3 * i : 9 + 3 * i]
+
+    def unpack_wide_columns(g, row, count):
+        rows = slice(row, row + count)
+        both = jnp.where(lanes_of(count) % 4 < 2, g.xe_r[0, rows], g.xe_r[1, rows])
         for k, (ref, index) in enumerate(wide_blocks(g)):
-            ref[index + (slice(0, rows), slice(g.x, g.x + LANES))] = pltpu.roll(both, LANES - (4 * k + 2), 1)
+            ref[index + (rows, slice(g.x, g.x + LANES))] = pltpu.roll(both, LANES - (4 * k + 2), 1)
+
+    def interface_step(g):
+        stress_block(g.u, g.stiff, g.s, g.near + g.third, 1, g.y, g.x, g.inv, 1.0)
+        for l in g.slabs:
+            stress_ext(g.u, g.wide, g.s, g.near + l, l, g.y, g.x, g.inv)
+        for l in g.slabs:
+            step_block(g.u, g.s, g.prev, g.dens, g.out, g.near + l, 1, g.y, g.x, g.inv, 1.0)
+
+    def beyond_edges(g):
+        first = g.near + g.slabs[0]
+        span = g.x + LANES
+        result = []
+        for side, (sign, edge, adjacent) in enumerate(((1.0, PAD, PAD - 1), (-1.0, PAD + g.y - 1, PAD + g.y))):
+            scale = sign * g.inv
+            d = [g.u[c, g.near + 1 : g.near + 4, edge : edge + 1, :] * scale for c in range(3)]
+            w = {c: g.wide[c, :, adjacent : adjacent + 1, :] for c in WIDE_Y}
+            s_xx, s_yy, s_zz, s_yz, s_xy = w[6] * d[1], w[1] * d[1], w[8] * d[1], w[3] * d[2], w[5] * d[0]
+
+            def two(v):
+                return v[g.slabs[0] : g.slabs[0] + 2, :, 0 : g.x]
+
+            def along_x_of(v):
+                v = v[g.slabs[0] : g.slabs[0] + 2]
+                return (pltpu.roll(v, span - 1, 2) - pltpu.roll(v, 1, 2))[:, :, 0 : g.x] * g.inv
+
+            def along_z_of(v):
+                v = v[:, :, 0 : g.x]
+                parts = []
+                for l in g.slabs:
+                    parts.append((v[l + 1 : l + 2] if l < 2 else 0.0) - (v[l - 1 : l] if l > 0 else 0.0))
+                return jnp.concatenate(parts, 0) * g.inv
+
+            def edge_stress(component):
+                return g.s[component, first + 1 : first + 3, edge : edge + 1, 0 : g.x] * scale
+
+            totals = (
+                (
+                    along_x_of(s_xx) + edge_stress(XY),
+                    along_x_of(s_xy) + edge_stress(YY) + along_z_of(s_yz),
+                    edge_stress(YZ) + along_z_of(s_zz),
+                ),
+                (two(s_xy) * scale, two(s_yy) * scale, two(s_yz) * scale),
+            )
+            rows = []
+            for i in range(2):
+                gain = (TIME_STEP * TIME_STEP) / g.ye_r[side, 21 + 2 * i : 23 + 2 * i]
+                index = 1 - i if side == 0 else i
+                rows.append([g.np_r[side, index, c] + gain * totals[i][c] for c in range(3)])
+            result.append(rows)
+        return result
 
     def start_all(copies):
         for there, _, copy in copies:
@@ -376,24 +464,34 @@
     with jax.named_scope("load_pack"):
         loads[0].wait()
         loads[1].wait()
-        pack_rows(0, (u, uc), (0, 1, 2))
         for there, g in sides:
             @pl.when(there)
             def _(g=g):
                 wide_load(g).wait()
-                pack_wide(g)
+                pack_wide_columns(g)
+        pack_rows(0, (u, uc), (0, 1, 2))
+        loads[2].wait()
+        loads[3].wait()
+        for there, g in sides:
+            @pl.when(there)
+            def _(g=g):
+                pack_wide_rows(g)
         pack_columns(0, (u, uc), (0, 1, 2))
     with jax.named_scope("barrier"):
         pl.semaphore_wait(barrier, expected)
     with jax.named_scope("send_0"):
+        for there, g in sides:
+            @pl.when(there)
+            def _(g=g):
+                start_all(wide_columns(g, (0,)))
         start_round(0, (2, 3))
         for there, g in sides:
             @pl.when(there)
             def _(g=g):
                 start_all(wide_rows(g))
-                start_all(wide_columns(g))
+                start_all(wide_columns(g, (-1, 1)))
         start_round(0, (4, 5, 0, 1))
-        for load in loads[2:]:
+        for load in loads[4:]:
             load.wait()
 
     lane = lanes_of(yc)
@@ -402,9 +500,9 @@
     def squeeze(left, right, odd):
         return jnp.where(lane < LANES // 2, pick(left, even + odd), pick(right, even + odd))
 
-    ikf_copy = rdma(own.at[6:18], ikf_opp, 24, (opp, gy, gx))
+    ikf_copy = rdma(own.at[6:18, 8:16], ikf_opp, 8, 16, (opp, gy, gx))
     ikf_rows = [
-        (has_y[a], has_y[-a], rdma(yi_s.at[i], yi_r.at[1 - i], 34 + i, (gz, gy + a, gx))) for i, a in enumerate((-1, 1))
+        (has_y[a], has_y[-a], rdma(yi_s.at[i], yi_r.at[1 - i], 9 + i, 17 + i, (gz, gy + a, gx))) for i, a in enumerate((-1, 1))
     ]
 
     @pl.when(is_f)
@@ -417,82 +515,134 @@
                 rows = pl.ds(py, yc, stride=2)
                 left, right = tiles[0, rows, :], tiles[1, rows, :]
                 for px in range(2):
-                    own[6 + c * 4 + py * 2 + px] = squeeze(left, right, px)
-        yi_s[0] = own[6:18, 0:2, :]
-        yi_s[1] = own[6:18, yc - 2 : yc, :]
+                    own[6 + c * 4 + py * 2 + px, 8:16] = squeeze(left, right, px)
+        yi_s[0] = own[6:18, 8:9, :]
+        yi_s[1] = own[6:18, yc + 7 : yc + 8, :]
         ikf_copy.start()
         start_all(ikf_rows)
 
-    with jax.named_scope("wait_wide"):
+    with jax.named_scope("wait_part"):
         for there, g in sides:
             @pl.when(there)
             def _(g=g):
-                receive_all(wide_rows(g))
-                receive_all(wide_columns(g))
-                for d in (2, 3):
-                    @pl.when(has[d ^ 1])
-                    def _(d=d):
-                        round_copies(0, d)[0 if g is fine else 1].wait_recv()
+                receive_all(wide_columns(g, (0,)))
 
     for there, g in sides:
         @pl.when(there)
         def _(g=g):
-            unpack_wide(g)
-            stress_block(g.u, g.stiff, g.s, g.third, 1, g.y, g.x, g.inv, 1.0)
-            for l, z in enumerate(g.layers):
-                stress_ext(g.u, g.wide, g.s, z, l, g.y, g.x, g.inv)
-            for z in g.layers:
-                step_block(g.u, g.s, g.prev, g.dens, g.out, z, 1, g.y, g.x, g.inv, 1.0)
+            unpack_wide_columns(g, PAD, g.y)
+            interface_step(g)
+            first = g.near + g.slabs[0]
+            for side, row in enumerate((0, g.y - 2)):
+                for i in range(2):
+                    for c in range(3):
+                        g.np_s[side, i, c] = g.out[c, first : first + 2, row + i : row + i + 1, :]
+            start_all(part_rows(g))
+
+    with jax.named_scope("wait_wide"):
+        for there, g in sides:
+            @pl.when(there)
+            def _(g=g):
+                end_round(0, (2, 3))
+                receive_all(wide_rows(g))
+                receive_all(wide_columns(g, (-1, 1)))
+
+    for there, g in sides:
+        @pl.when(there)
+        def _(g=g):
+            unpack_wide_rows(g)
+            unpack_wide_columns(g, 0, PAD)
+            unpack_wide_columns(g, PAD + g.y, PAD)
+            interface_step(g)
 
     @pl.when(is_c)
     def _():
         for c in range(3):
             start, below = cout[c, 0], cout[c, 1]
             k = cstiff[CH[c], 0] * 0.25
-            own[c] = k * (below - start)
-            own[3 + c] = below - 0.5 * start
-            own[6 + c] = k
+            own[c, 8:16] = k * (below - start)
+            own[3 + c, 8:16] = below - 0.5 * start
+            own[6 + c, 8:16] = k
 
     @pl.when(is_f)
     def _():
         for c in range(3):
             for i, z in enumerate((zf - 2, zf - 1)):
                 plane = fout[c, z]
-                sums = []
+                pairs = []
                 for t in range(2):
                     tiles[t] = plane[:, t * LANES : (t + 1) * LANES]
                     pair = tiles[t, pl.ds(0, yc, stride=2), :] + tiles[t, pl.ds(1, yc, stride=2), :]
-                    sums.append(pair + pltpu.roll(pair, LANES - 1, 1))
-                own[3 * i + c] = squeeze(sums[0], sums[1], 0) * 0.25
+                    pairs.append(pair + pltpu.roll(pair, LANES - 1, 1))
+                own[3 * i + c, 8:16] = squeeze(pairs[0], pairs[1], 0) * 0.25
+
+    with jax.named_scope("wait_beyond"):
+        for there, g in sides:
+            @pl.when(there)
+            def _(g=g):
+                receive_all(part_rows(g))
+
+        @pl.when(is_f)
+        def _():
+            receive_all(ikf_rows)
+
+    @pl.when(is_c)
+    def _():
+        for side, rows in enumerate(beyond_edges(coarse)):
+            for i in range(2):
+                place = (7 - i) if side == 0 else (16 + i)
+                for c in range(3):
+                    start, below = rows[i][c][0], rows[i][c][1]
+                    k = yec_r[side, 25 + 3 * i + c] * 0.25
+                    own[c, place : place + 1] = k * (below - start)
+                    own[3 + c, place : place + 1] = below - 0.5 * start
+                    own[6 + c, place : place + 1] = k
+
+    @pl.when(is_f)
+    def _():
+        for side, rows in enumerate(beyond_edges(fine)):
+            for c in range(3):
+                both = rows[0][c] + rows[1][c]
+                for i in range(2):
+                    k = side * 6 + 3 * i + c
+                    for t in range(2):
+                        sums[t, k : k + 1] = both[i, :, t * LANES : (t + 1) * LANES]
+        pairs = [sums[t] + pltpu.roll(sums[t], LANES - 1, 1) for t in range(2)]
+        lane16 = lanes_of(16)
+        index = (2 * lane16) % LANES
+        tiles[0] = jnp.where(lane16 < LANES // 2, pick(pairs[0], index), pick(pairs[1], index)) * 0.25
+        for side, place in enumerate((7, 16)):
+            for k in range(6):
+                own[k, place : place + 1] = tiles[0, side * 6 + k : side * 6 + k + 1]
+            own[6:18, place : place + 1] = yi_r[side]
 
     fields = 18
-    lane4 = lane // 4
-    own_copy = rdma(own.at[0:9], own_opp, 25, (opp, gy, gx))
-    strips = []
-    for level, rows_to, tile_to, slot in ((opp, yo3, xo3, 36), (gz, yr3, xr3, 44)):
-        for i, a in enumerate((-1, 1)):
+    strips = [
+        (active, active, rdma(own.at[0:9, 8:16], own_opp, 13, 29, (opp, gy, gx))),
+        (active, active, rdma(ys3, yo3, 14, 30, (opp, gy, gx))),
+    ]
+    for level, tile_to, out, into in ((opp, xo3, 15, 33), (gz, xr3, 17, 31)):
+        for i, b in enumerate((-1, 1)):
             strips.append((
-                jnp.logical_and(active, has_y[a]), jnp.logical_and(active, has_y[-a]),
-                rdma(ys3.at[i], rows_to.at[1 - i], slot + i, (level, gy + a, gx)),
+                jnp.logical_and(active, has_x[b]), jnp.logical_and(active, has_x[-b]),
+                rdma(xs3, tile_to.at[1 - i], out + i, into + i, (level, gy, gx + b)),
             ))
-        for i, b in enumerate((-1, 1)):
-            for a in (-1, 0, 1):
-                strips.append((
-                    jnp.logical_and(active, jnp.logical_and(has_y[a], has_x[b])),
-                    jnp.logical_and(active, jnp.logical_and(has_y[-a], has_x[-b])),
-                    rdma(xs3, tile_to.at[1 - i, pl.ds((1 - a) * 8, 8)], slot + 2 + i * 3 + (a + 1), (level, gy + a, gx + b)),
-                ))
-    opp_strips, level_strips = strips[:8], strips[8:]
+    opp_strips, level_strips = strips[:4], strips[4:]
 
     @pl.when(active)
     def _():
-        ys3[0] = own[0:9, 0:2, :]
-        ys3[1] = own[0:9, yc - 2 : yc, :]
-        packed = jnp.zeros((yc, LANES), F32)
+        ys3[0] = own[0:9, 6:8, :]
+        ys3[1] = own[0:9, 16:18, :]
+        packed = jnp.zeros((24, LANES), F32)
+        lane4 = lanes_of(24) // 4
         for k in range(fields):
             packed = jnp.where(lane4 == k, pltpu.roll(own[k], 4 * k + 2, 1), packed)
         xs3[...] = packed
-        own_copy.start()
+
+    for there, g in sides:
+        @pl.when(there)
+        def _(g=g):
+            sent_all(wide_columns(g, (-1, 0, 1)))
 
     start_all(strips)
 
@@ -502,19 +652,9 @@
     zb = min(4, zc)
 
     with jax.named_scope("wait_0"):
-        @pl.when(jnp.logical_not(is_f))
+        @pl.when(jnp.logical_not(active))
         def _():
-            for d in (2, 3):
-                @pl.when(has[d ^ 1])
-                def _(d=d):
-                    round_copies(0, d)[0].wait_recv()
-
-        @pl.when(jnp.logical_not(is_c))
-        def _():
-            for d in (2, 3):
-                @pl.when(has[d ^ 1])
-                def _(d=d):
-                    round_copies(0, d)[1].wait_recv()
+            end_round(0, (2, 3))
 
         end_round(0, (0, 1, 4, 5))
     with jax.named_scope("stress"):
@@ -525,6 +665,11 @@
             stress_block(uc, cstiff, sc, z, zb, yc, xc, 0.25, 1.0)
     with jax.named_scope("pack_1"):
         pack_rows(1, (s, sc), FACE_Y)
+        for d in range(6):
+            @pl.when(has[d])
+            def _(d=d):
+                for copy in round_copies(0, d):
+                    copy.wait_send()
         start_round(1, (2, 3))
         pack_columns(1, (s, sc), FACE_X)
         start_round(1, (4, 5, 0, 1))
@@ -559,33 +704,29 @@
     def along_x(t):
         return (0.75 * t + 0.25 * pltpu.roll(t, 1, 1), 0.75 * t + 0.25 * pltpu.roll(t, 2 * LANES - 1, 1))
 
+    def extend_own(k, field, edges):
+        ext[k, :, 0:LANES] = own[field]
+        ext[k, :, LANES : 2 * LANES] = pltpu.roll(edges, LANES - (4 * field + 2), 1)
+
     with jax.named_scope("wait_level"):
         receive_all(level_strips)
 
-        @pl.when(is_f)
-        def _():
-            receive_all(ikf_rows)
-
     @pl.when(is_c)
     def _():
         edges = jnp.where(lane24 % 4 < 2, xr3[0], xr3[1])
         for k in range(3, 9):
-            extend(k, k, own[k], yr3, k, edges)
+            extend_own(k, k, edges)
         ikf_copy.wait_recv()
 
     @pl.when(is_f)
     def _():
         edges = jnp.where(lane24 % 4 < 2, xr3[0], xr3[1])
         for k in range(3):
-            extend(9 + k, k, own[k], yr3, k, edges)
+            extend_own(9 + k, k, edges)
         for k in range(12):
-            extend(12 + k, 6 + k, own[6 + k], yi_r, k, edges)
+            extend_own(12 + k, 6 + k, edges)
 
     with jax.named_scope("wait_opp"):
-        @pl.when(active)
-        def _():
-            own_copy.wait_recv()
-
         receive_all(opp_strips)
 
     @pl.when(is_c)
@@ -625,27 +766,22 @@
                 fout[c, zf - 1, :, cols] = fout[c, zf - 2, :, cols] + tiles[t] / stiff[CH[c], zf - 1, :, cols]
 
     with jax.named_scope("drain"):
-        for r in range(2):
-            for d in range(6):
-                @pl.when(has[d])
-                def _(r=r, d=d):
-                    for copy in round_copies(r, d):
-                        copy.wait_send()
+        for d in range(6):
+            @pl.when(has[d])
+            def _(d=d):
+                for copy in round_copies(1, d):
+                    copy.wait_send()
         sent_all(strips)
         for there, g in sides:
             @pl.when(there)
             def _(g=g):
                 sent_all(wide_rows(g))
-                sent_all(wide_columns(g))
+                sent_all(part_rows(g))
 
         @pl.when(is_f)
         def _():
             ikf_copy.wait_send()
             sent_all(ikf_rows)
-
-        @pl.when(active)
-        def _():
-            own_copy.wait_send()
 
 
 def per_device(counts, *args):
@@ -668,19 +804,19 @@
             vmem(3, zf, yf, xf), vmem(9, zf, yf, xf), vmem(zf, yf, xf), vmem(zf, yf, xf),
             vmem(3, zc, yc, xc), vmem(9, zc, yc, xc), vmem(zc, yc, xc),
             vmem(2, yf + yc, LANES), vmem(2, 2, yf + yc, LANES),
-            vmem(2, 2, 3, zf, 1, xf), vmem(2, 2, 3, zf, 1, xf),
-            vmem(2, 2, 3, zc, 1, xc), vmem(2, 2, 3, zc, 1, xc),
-            vmem(9, 2, yf + 2 * PAD, xf + LANES), vmem(9, 2, yc + 2 * PAD, xc + LANES),
-            vmem(2, 8, 2, 1, xf), vmem(2, 8, 2, 1, xf), vmem(2, 8, 2, 1, xc), vmem(2, 8, 2, 1, xc),
+            vmem(2, 2, 3, zf + zc // 2, 1, xf), vmem(2, 2, 3, zf + zc // 2, 1, xf),
+            vmem(9, 3, yf + 2 * PAD, xf + LANES), vmem(9, 3, yc + 2 * PAD, xc + LANES),
+            vmem(2, 31, 1, xf), vmem(2, 31, 1, xf), vmem(2, 31, 1, xc), vmem(2, 31, 1, xc),
             vmem(yf, LANES), vmem(2, yf + 2 * PAD, LANES), vmem(yc, LANES), vmem(2, yc + 2 * PAD, LANES),
-            vmem(2, yf, LANES), vmem(18, yc, LANES), vmem(9, yc, LANES), vmem(12, yc, LANES),
-            vmem(2, 12, 2, LANES), vmem(2, 12, 2, LANES),
-            vmem(2, 9, 2, LANES), vmem(2, 9, 2, LANES), vmem(2, 9, 2, LANES),
-            vmem(yc, LANES), vmem(2, 24, LANES), vmem(2, 24, LANES),
+            vmem(2, 2, 3, 2, 1, xf), vmem(2, 2, 3, 2, 1, xf), vmem(2, 2, 3, 2, 1, xc), vmem(2, 2, 3, 2, 1, xc),
+            vmem(2, yf, LANES), vmem(2, yf, LANES), vmem(18, 24, LANES), vmem(9, yc, LANES), vmem(12, yc, LANES),
+            vmem(2, 12, 1, LANES), vmem(2, 12, 1, LANES),
+            vmem(2, 9, 2, LANES), vmem(2, 9, 2, LANES),
+            vmem(24, LANES), vmem(2, 24, LANES), vmem(2, 24, LANES),
             vmem(24, 24, 2 * LANES),
             pltpu.SemaphoreType.DMA((10,)),
-            pltpu.SemaphoreType.DMA((52,)),
-            pltpu.SemaphoreType.DMA((52,)),
+            pltpu.SemaphoreType.DMA((21,)),
+            pltpu.SemaphoreType.DMA((35,)),
         ],
         compiler_params=pltpu.CompilerParams(
             collective_id=0, has_side_effects=True, vmem_limit_bytes=56 * 1024 * 1024

time: 31 us -> 29.6 us (0.955)
  the two profiles are of different devices: /device:TPU:25 before, /device:TPU:122 now
where the time goes in v3:
time: 29.6 us; the launch traced here: 29.5 us
  Pallas kernels  27.5 us (93%)
  local copies, waits for them, and re-layouts  1.32 us (4%)
  between operations  0.64 us (2%)
    pallas_call x1, Pallas kernels, per_device(): pl.pallas_call(functools.partial(kernel, counts), out_shape=(pltpu.VMEM(f...  27.5 us
    unnamed x2, local copies, waits for them, and re-layouts  1.32 us

profile of v3, /device:TPU:122, one launch (start us, length us, event | category | flops | bytes accessed | tf_op | source)
XLA Modules:
  0.0 29.5 jit_solution(7903333896541833461)
XLA Ops:
  0.6 27.5 %elastic_step.1 = (f32[3,4,16,256]{3,2,1,0:T(8,128)S(1)}, f32[3,8,8,128]{3,2,1,0:T(8,128)S(1)}) custom-call(f32[3,4,16,256]{3,2,1,0:T(8,128)} %fn.1, f32[3,4,16,256]{3,2,1,0:T(8,128)} %fp.1, f32[9,4,16,256]{3,2,1,0:T(8,128)} %st.1, f32[4,16,256]{2,1,0:T(8,128)} %me.1, f32[4,16,256]{2,1,0:T(8,128)} %de.1, f32[3,8,8,128]{3,2,1,0:T(8,128)} %cn.1, ...), custom_call_target="tpu_custom_call" | custom-call | tf_op jit(solution)/shard_map/elastic_step/pallas_call | solution.py:794
  28.2 0.7 %copy.13 = f32[3,4,16,256]{3,2,1,0:T(8,128)} copy(f32[3,4,16,256]{3,2,1,0:T(8,128)S(1)} %get-tuple-element.2) | data formatting | bytes 393216
  28.8 0.6 %copy.14 = f32[3,8,8,128]{3,2,1,0:T(8,128)} copy(f32[3,8,8,128]{3,2,1,0:T(8,128)S(1)} %get-tuple-element.3) | data formatting | bytes 196608

commit v4 on v3

--- a/solution.py
+++ b/solution.py
@@ -9,11 +9,13 @@
 
 TIME_STEP = 0.2
 ITERS = 3
+SPLIT = False
 F32 = jnp.float32
 XX, XY, YY, XZ, YZ, ZZ = range(6)
 FACE_X = (XX, XY, XZ)
 FACE_Y = (XY, YY, YZ)
 WIDE_Y = (1, 3, 5, 6, 8)
+EDGE_Y = (5, 1, 3)
 WIDE_X = (0, 4, 5, 6, 7)
 CH = (4, 3, 2)
 PAD = 8
@@ -141,8 +143,8 @@
     u, uc, s, sc, fprev, stiff, metric, dens, cprev, cstiff, cdens,
     xs, xr, ys, yr,
     fwide, cwide, yef_s, yef_r, yec_s, yec_r, xef_s, xef_r, xec_s, xec_r,
-    npf_s, npf_r, npc_s, npc_r,
-    tiles, sums, own, own_opp, ikf_opp, yi_s, yi_r, ys3, yo3, xs3, xr3, xo3, ext,
+    npf_s, npf_l, npf_o, npc_s, npc_l, npc_o, cs, cr,
+    tiles, sums, own, own_opp, ikf_opp, ys3, yo3, xs3, xr3, xo3, ext,
     load_sem, send_sem, recv_sem,
 ):
     n_z, n_y, n_x = counts
@@ -150,11 +152,11 @@
     zc, yc, xc = cde.shape
     fine = Grid(
         z=zf, y=yf, x=xf, u=u, s=s, wide=fwide, source=st, stiff=stiff, third=0, prev=fprev, dens=dens, out=fout, inv=0.5,
-        slabs=(1, 2), near=zf - 3, np_s=npf_s, np_r=npf_r, ye_s=yef_s, ye_r=yef_r, xe_s=xef_s, xe_r=xef_r,
+        slabs=(1, 2), near=zf - 3, np_s=npf_s, np_l=npf_l, np_o=npf_o, ye_s=yef_s, ye_r=yef_r, xe_s=xef_s, xe_r=xef_r,
     )
     coarse = Grid(
         z=zc, y=yc, x=xc, u=uc, s=sc, wide=cwide, source=cst, stiff=cstiff, third=2, prev=cprev, dens=cdens, out=cout, inv=0.25,
-        slabs=(0, 1), near=0, np_s=npc_s, np_r=npc_r, ye_s=yec_s, ye_r=yec_r, xe_s=xec_s, xe_r=xec_r,
+        slabs=(0, 1), near=0, np_s=npc_s, np_l=npc_l, np_o=npc_o, ye_s=yec_s, ye_r=yec_r, xe_s=xec_s, xe_r=xec_r,
     )
     gz, gy, gx = lax.axis_index("gz"), lax.axis_index("gy"), lax.axis_index("gx")
     opp = n_z - 1 - gz
@@ -209,7 +211,7 @@
         @pl.when(there)
         def _(g=g):
             wide_load(g).start()
-    for load in loads[2:]:
+    for load in loads[2:4]:
         load.start()
 
     def clear(part):
@@ -222,6 +224,9 @@
                 clear(g.u.at[:, g.near + 1 : g.near + 4, rows])
                 clear(g.wide.at[:, :, rows])
 
+    for g in (fine, coarse):
+        for row in (PAD - 1, PAD + g.y):
+            clear(g.u.at[:, 1 : g.z + 1, row : row + 1, 0 : g.x])
     for d in range(6):
         @pl.when(jnp.logical_not(has[d]))
         def _(d=d):
@@ -234,9 +239,9 @@
             elif d < 4:
                 for r in range(2):
                     clear(yr.at[r, side])
+                clear(cr.at[side])
                 for g in (fine, coarse):
                     clear(g.ye_r.at[side])
-                    clear(g.np_r.at[side])
                     for b in range(2):
                         clear(g.xe_r.at[b, pl.ds(0 if side == 0 else PAD + g.y, PAD)])
             else:
@@ -262,12 +267,12 @@
                 sent, landed = (1, g.z + 1) if side == 0 else (g.z, 0)
                 made.append(rdma(
                     ref.at[comps, sent, g.own[1], g.own[2]], ref.at[comps, landed, g.own[1], g.own[2]],
-                    2 * d + i, 8 * r + 2 * d + i, near[d],
+                    (0, 31)[r] + 2 * d + i, 8 * r + 2 * d + i, near[d],
                 ))
             return made
         if d < 4:
-            return [rdma(ys.at[r, side], yr.at[r, arrival], d + 2, 8 * r + d + 2, near[d])]
-        return [rdma(xs.at[r], xr.at[r, arrival], d + 2, 8 * r + d + 2, near[d])]
+            return [rdma(ys.at[r, side], yr.at[r, arrival], (d + 2, d + 19)[r], 8 * r + d + 2, near[d])]
+        return [rdma(xs.at[r], xr.at[r, arrival], (d + 2, d + 31)[r], 8 * r + d + 2, near[d])]
 
     def start_round(r, directions):
         for d in directions:
@@ -306,15 +311,34 @@
         xs[r, 0:yf] = pack_x(refs[0], face_x, zf, yf, xf)
         xs[r, yf : yf + yc] = pack_x(refs[1], face_x, zc, yc, xc)
 
+    stiff_rows = [
+        (has_y[a], has_y[-a], rdma(cs.at[i], cr.at[1 - i], 23 + i, 35 + i, (gz, gy + a, gx))) for i, a in enumerate((-1, 1))
+    ]
+
+    def pack_stiff_rows():
+        half = zc // 2
+        for i, c in enumerate(EDGE_Y):
+            for side in range(2):
+                row = (0, yf - 1)[side]
+                cs[side, i, 0:zf] = stiff[c, :, row : row + 1, :]
+                row = (0, yc - 1)[side]
+                for j in range(2):
+                    cs[side, i, zf : zf + half, :, j * xc : (j + 1) * xc] = cstiff[
+                        c, j * half : (j + 1) * half, row : row + 1, :
+                    ]
+
+    def complete_rows():
+        for side, sign in enumerate((1.0, -1.0)):
+            for g, part in ((fine, slice(0, zf)), (coarse, slice(zf, zf + zc // 2))):
+                yr[1, side, :, part] = yr[1, side, :, part] + cr[side, :, part] * ys[0, side, :, part] * (sign * g.inv)
+
     def unpack_rows(r, g, ref, face_y):
         for side, row in enumerate((PAD - 1, PAD + g.y)):
             for i, c in enumerate(face_y):
                 for part, place in row_parts(g, ref, c, row):
                     part[...] = yr[(r, side, i) + place[1:]]
 
-    def unpack(r, refs, face_x, face_y):
-        unpack_rows(r, fine, refs[0], face_y)
-        unpack_rows(r, coarse, refs[1], face_y)
+    def unpack_columns(r, refs, face_x):
         unpack_x(refs[0], face_x, zf, yf, xf, xr[r, 0, 0:yf], xr[r, 1, 0:yf])
         unpack_x(refs[1], face_x, zc, yc, xc, xr[r, 0, yf : yf + yc], xr[r, 1, yf : yf + yc])
 
@@ -372,14 +396,35 @@
         return made
 
     def part_rows(g):
-        return [
-            (has_y[a], has_y[-a], rdma(g.np_s.at[i], g.np_r.at[1 - i], 19 + i, 27 + i, (gz, gy + a, gx)))
-            for i, a in enumerate((-1, 1))
-        ]
+        made = []
+        for i, a in enumerate((-1, 1)):
+            for b in (-1, 0, 1):
+                k = 3 * i + b + 1
+                made.append((
+                    jnp.logical_and(has_y[a], has_x[b]), jnp.logical_and(has_y[-a], has_x[-b]),
+                    rdma(g.np_s.at[i], g.np_l.at[1 - i, 1 - b], 25 + k, 37 + k, (gz, gy + a, gx + b)),
+                ))
+        return made
+
+    def passed_parts(g):
+        source, target = (npf_l.at[:, :, 0:6], npc_o) if g is fine else (npc_l, npf_o)
+        return rdma(source, target, 9, 17, (opp, gy, gx))
+
+    def squeeze_rows(row_of):
+        for side in range(2):
+            for c in range(3):
+                both = row_of(side, c)
+                for i in range(2):
+                    k = side * 6 + 3 * i + c
+                    for t in range(2):
+                        sums[t, k : k + 1] = both[i, :, t * LANES : (t + 1) * LANES]
+        pairs = [sums[t] + pltpu.roll(sums[t], LANES - 1, 1) for t in range(2)]
+        lane16 = lanes_of(16)
+        index = (2 * lane16) % LANES
+        return jnp.where(lane16 < LANES // 2, pick(pairs[0], index), pick(pairs[1], index)) * 0.25
 
     def unpack_wide_rows(g):
         first = g.near + g.slabs[0]
-        unpack_rows(0, g, g.u, (0, 1, 2))
         for side, (edge, second) in enumerate(((PAD - 1, PAD - 2), (PAD + g.y, PAD + g.y + 1))):
             landed = g.ye_r.at[side]
             for c in range(3):
@@ -438,8 +483,7 @@
             rows = []
             for i in range(2):
                 gain = (TIME_STEP * TIME_STEP) / g.ye_r[side, 21 + 2 * i : 23 + 2 * i]
-                index = 1 - i if side == 0 else i
-                rows.append([g.np_r[side, index, c] + gain * totals[i][c] for c in range(3)])
+                rows.append([gain * totals[i][c] for c in range(3)])
             result.append(rows)
         return result
 
@@ -464,6 +508,8 @@
     with jax.named_scope("load_pack"):
         loads[0].wait()
         loads[1].wait()
+        for load in loads[4:]:
+            load.start()
         for there, g in sides:
             @pl.when(there)
             def _(g=g):
@@ -493,6 +539,8 @@
         start_round(0, (4, 5, 0, 1))
         for load in loads[4:]:
             load.wait()
+        if SPLIT:
+            pack_stiff_rows()
 
     lane = lanes_of(yc)
     even = (2 * lane) % LANES
@@ -501,10 +549,6 @@
         return jnp.where(lane < LANES // 2, pick(left, even + odd), pick(right, even + odd))
 
     ikf_copy = rdma(own.at[6:18, 8:16], ikf_opp, 8, 16, (opp, gy, gx))
-    ikf_rows = [
-        (has_y[a], has_y[-a], rdma(yi_s.at[i], yi_r.at[1 - i], 9 + i, 17 + i, (gz, gy + a, gx))) for i, a in enumerate((-1, 1))
-    ]
-
     @pl.when(is_f)
     def _():
         for c in range(3):
@@ -516,10 +560,13 @@
                 left, right = tiles[0, rows, :], tiles[1, rows, :]
                 for px in range(2):
                     own[6 + c * 4 + py * 2 + px, 8:16] = squeeze(left, right, px)
-        yi_s[0] = own[6:18, 8:9, :]
-        yi_s[1] = own[6:18, yc + 7 : yc + 8, :]
-        ikf_copy.start()
-        start_all(ikf_rows)
+
+    k_copy = rdma(own.at[6:9, 8:16], own_opp.at[6:9], 8, 16, (opp, gy, gx))
+
+    @pl.when(is_c)
+    def _():
+        for c in range(3):
+            own[6 + c, 8:16] = cstiff[CH[c], 0] * 0.25
 
     with jax.named_scope("wait_part"):
         for there, g in sides:
@@ -532,18 +579,73 @@
         def _(g=g):
             unpack_wide_columns(g, PAD, g.y)
             interface_step(g)
-            first = g.near + g.slabs[0]
-            for side, row in enumerate((0, g.y - 2)):
-                for i in range(2):
-                    for c in range(3):
-                        g.np_s[side, i, c] = g.out[c, first : first + 2, row + i : row + i + 1, :]
-            start_all(part_rows(g))
+
+    @pl.when(is_f)
+    def _():
+        first = fine.near + fine.slabs[0]
+
+        def two_rows(side, c):
+            row = (0, yf - 2)[side]
+            return fout[c, first : first + 2, row : row + 1, :] + fout[c, first : first + 2, row + 1 : row + 2, :]
+
+        tiles[0] = squeeze_rows(two_rows)
+        for side in range(2):
+            for k in range(6):
+                npf_s[side, k] = tiles[0, side * 6 + k : side * 6 + k + 1]
+            npf_s[side, 6:18] = own[6:18, (8, yc + 7)[side] : (9, yc + 8)[side], :]
+        start_all(part_rows(fine))
+        ikf_copy.start()
+
+    @pl.when(is_c)
+    def _():
+        for side in range(2):
+            for i in range(2):
+                row = (i, yc - 1 - i)[side]
+                for c in range(3):
+                    start, below = cout[c, 0, row : row + 1, :], cout[c, 1, row : row + 1, :]
+                    npc_s[side, 6 * i + c] = own[6 + c, 8 + row : 9 + row] * (below - start)
+                    npc_s[side, 6 * i + 3 + c] = below - 0.5 * start
+        start_all(part_rows(coarse))
+        k_copy.start()
+
+    def stretch_of(z):
+        return jnp.where(gz * zf + z < n_z * zf // 2, metric[z : z + 1], 1.0)
+
+    zb = min(4, zc)
+
+    def stress_all():
+        for z in range(zf):
+            stress_block(u, stiff, s, z, 1, yf, xf, 0.5, stretch_of(z))
+        for z in range(0, zc, zb):
+            stress_block(uc, cstiff, sc, z, zb, yc, xc, 0.25, 1.0)
+
+    with jax.named_scope("wait_near"):
+        end_round(0, (4, 5, 0, 1))
+    with jax.named_scope("part_stress"):
+        unpack_columns(0, (u, uc), (0, 1, 2))
+        if SPLIT:
+            stress_all()
+            pack_rows(1, (s, sc), FACE_Y)
+            start_round(1, (2, 3))
+            start_all(stiff_rows)
+
+    with jax.named_scope("wait_rows"):
+        end_round(0, (2, 3))
+        unpack_rows(0, fine, u, (0, 1, 2))
+        unpack_rows(0, coarse, uc, (0, 1, 2))
+
+    with jax.named_scope("stress"):
+        stress_all()
+        if not SPLIT:
+            pack_rows(1, (s, sc), FACE_Y)
+            start_round(1, (2, 3))
+        pack_columns(1, (s, sc), FACE_X)
+        start_round(1, (4, 5, 0, 1))
 
     with jax.named_scope("wait_wide"):
         for there, g in sides:
             @pl.when(there)
             def _(g=g):
-                end_round(0, (2, 3))
                 receive_all(wide_rows(g))
                 receive_all(wide_columns(g, (-1, 1)))
 
@@ -551,18 +653,15 @@
         @pl.when(there)
         def _(g=g):
             unpack_wide_rows(g)
-            unpack_wide_columns(g, 0, PAD)
-            unpack_wide_columns(g, PAD + g.y, PAD)
+            unpack_wide_columns(g, 0, 2 * PAD + g.y)
             interface_step(g)
 
     @pl.when(is_c)
     def _():
         for c in range(3):
             start, below = cout[c, 0], cout[c, 1]
-            k = cstiff[CH[c], 0] * 0.25
-            own[c, 8:16] = k * (below - start)
+            own[c, 8:16] = own[6 + c, 8:16] * (below - start)
             own[3 + c, 8:16] = below - 0.5 * start
-            own[6 + c, 8:16] = k
 
     @pl.when(is_f)
     def _():
@@ -576,16 +675,6 @@
                     pairs.append(pair + pltpu.roll(pair, LANES - 1, 1))
                 own[3 * i + c, 8:16] = squeeze(pairs[0], pairs[1], 0) * 0.25
 
-    with jax.named_scope("wait_beyond"):
-        for there, g in sides:
-            @pl.when(there)
-            def _(g=g):
-                receive_all(part_rows(g))
-
-        @pl.when(is_f)
-        def _():
-            receive_all(ikf_rows)
-
     @pl.when(is_c)
     def _():
         for side, rows in enumerate(beyond_edges(coarse)):
@@ -600,25 +689,15 @@
 
     @pl.when(is_f)
     def _():
-        for side, rows in enumerate(beyond_edges(fine)):
-            for c in range(3):
-                both = rows[0][c] + rows[1][c]
-                for i in range(2):
-                    k = side * 6 + 3 * i + c
-                    for t in range(2):
-                        sums[t, k : k + 1] = both[i, :, t * LANES : (t + 1) * LANES]
-        pairs = [sums[t] + pltpu.roll(sums[t], LANES - 1, 1) for t in range(2)]
-        lane16 = lanes_of(16)
-        index = (2 * lane16) % LANES
-        tiles[0] = jnp.where(lane16 < LANES // 2, pick(pairs[0], index), pick(pairs[1], index)) * 0.25
+        beyond = beyond_edges(fine)
+        tiles[0] = squeeze_rows(lambda side, c: beyond[side][0][c] + beyond[side][1][c])
         for side, place in enumerate((7, 16)):
             for k in range(6):
                 own[k, place : place + 1] = tiles[0, side * 6 + k : side * 6 + k + 1]
-            own[6:18, place : place + 1] = yi_r[side]
 
     fields = 18
     strips = [
-        (active, active, rdma(own.at[0:9, 8:16], own_opp, 13, 29, (opp, gy, gx))),
+        (active, active, rdma(own.at[0:6, 8:16], own_opp.at[0:6], 13, 29, (opp, gy, gx))),
         (active, active, rdma(ys3, yo3, 14, 30, (opp, gy, gx))),
     ]
     for level, tile_to, out, into in ((opp, xo3, 15, 33), (gz, xr3, 17, 31)):
@@ -646,37 +725,22 @@
 
     start_all(strips)
 
-    def stretch_of(z):
-        return jnp.where(gz * zf + z < n_z * zf // 2, metric[z : z + 1], 1.0)
-
-    zb = min(4, zc)
-
-    with jax.named_scope("wait_0"):
-        @pl.when(jnp.logical_not(active))
-        def _():
-            end_round(0, (2, 3))
-
-        end_round(0, (0, 1, 4, 5))
-    with jax.named_scope("stress"):
-        unpack(0, (u, uc), (0, 1, 2), (0, 1, 2))
-        for z in range(zf):
-            stress_block(u, stiff, s, z, 1, yf, xf, 0.5, stretch_of(z))
-        for z in range(0, zc, zb):
-            stress_block(uc, cstiff, sc, z, zb, yc, xc, 0.25, 1.0)
-    with jax.named_scope("pack_1"):
-        pack_rows(1, (s, sc), FACE_Y)
-        for d in range(6):
-            @pl.when(has[d])
-            def _(d=d):
-                for copy in round_copies(0, d):
-                    copy.wait_send()
-        start_round(1, (2, 3))
-        pack_columns(1, (s, sc), FACE_X)
-        start_round(1, (4, 5, 0, 1))
+    with jax.named_scope("wait_parts"):
+        for there, g in sides:
+            @pl.when(there)
+            def _(g=g):
+                receive_all(part_rows(g))
+                passed_parts(g).start()
+
     with jax.named_scope("wait_1"):
         end_round(1, (0, 1, 4, 5, 2, 3))
+        if SPLIT:
+            receive_all(stiff_rows)
+            complete_rows()
     with jax.named_scope("step"):
-        unpack(1, (s, sc), FACE_X, FACE_Y)
+        unpack_rows(1, fine, s, FACE_Y)
+        unpack_rows(1, coarse, sc, FACE_Y)
+        unpack_columns(1, (s, sc), FACE_X)
         for z in range(zf):
             step_block(u, s, fprev, dens, fout, z, 1, yf, xf, 0.5, stretch_of(z))
         for z in range(0, zc, zb):
@@ -729,11 +793,34 @@
     with jax.named_scope("wait_opp"):
         receive_all(opp_strips)
 
+    with jax.named_scope("wait_passed"):
+        for there, g in sides:
+            @pl.when(there)
+            def _(g=g):
+                passed_parts(coarse if g is fine else fine).wait_recv()
+
+    def part_of(parts, side, field):
+        edges = jnp.where(lanes_of(1) < LANES // 2, parts[side, 2, field], parts[side, 0, field])
+        return jnp.concatenate([parts[side, 1, field], edges], 1)
+
+    def add_part(k, parts, side, field, place):
+        ext[k, place : place + 1] += part_of(parts, side, field)
+
+    def set_part(k, parts, side, field, place):
+        ext[k, place : place + 1] = part_of(parts, side, field)
+
+    @pl.when(is_f)
+    def _():
+        k_copy.wait_recv()
+
     @pl.when(is_c)
     def _():
         edges = jnp.where(lane24 % 4 < 2, xo3[0], xo3[1])
         for c in range(3):
             extend(9 + c, 3 + c, own_opp[3 + c], yo3, 3 + c, edges)
+            for side, place in enumerate((7, 16)):
+                add_part(9 + c, npc_o, side, 3 + c, place)
+                add_part(3 + c, npc_l, side, 3 + c, place)
             t1 = clamp(ext[6 + c] * (ext[3 + c] - 0.5 * ext[9 + c]))
             total = jnp.zeros((yc, LANES), F32)
             for py, part in enumerate(along_y(t1)):
@@ -748,6 +835,13 @@
         for c in range(3):
             for k in (c, 3 + c, 6 + c):
                 extend(k, k, own_opp[k], yo3, k, edges)
+            for side, (place, after) in enumerate(((7, 6), (16, 17))):
+                add_part(c, npf_o, side, c, place)
+                add_part(c, npf_o, side, 6 + c, after)
+                add_part(3 + c, npf_o, side, 3 + c, place)
+                add_part(9 + c, npf_l, side, c, place)
+                for k in range(4 * c, 4 * c + 4):
+                    set_part(12 + k, npf_l, side, 6 + k, place)
             total = jnp.zeros((24, 2 * LANES), F32)
             for py, part in enumerate(along_y(clamp(ext[c]))):
                 for px, full in enumerate(along_x(part)):
@@ -771,17 +865,39 @@
             def _(d=d):
                 for copy in round_copies(1, d):
                     copy.wait_send()
+        for d in range(6):
+            @pl.when(has[d])
+            def _(d=d):
+                for copy in round_copies(0, d):
+                    copy.wait_send()
+        if SPLIT:
+            sent_all(stiff_rows)
         sent_all(strips)
         for there, g in sides:
             @pl.when(there)
             def _(g=g):
                 sent_all(wide_rows(g))
                 sent_all(part_rows(g))
+                passed_parts(g).wait_send()
 
         @pl.when(is_f)
         def _():
             ikf_copy.wait_send()
-            sent_all(ikf_rows)
+
+        @pl.when(is_c)
+        def _():
+            k_copy.wait_send()
+
+
+def write_out(fine, coarse, fine_out, coarse_out, sem):
+    copies = [
+        pltpu.make_async_copy(fine, fine_out, sem.at[0]),
+        pltpu.make_async_copy(coarse, coarse_out, sem.at[1]),
+    ]
+    for copy in copies:
+        copy.start()
+    for copy in copies:
+        copy.wait()
 
 
 def per_device(counts, *args):
@@ -791,7 +907,7 @@
     vmem = lambda *shape: pltpu.VMEM(shape, F32)
     anywhere = pl.BlockSpec(memory_space=pl.ANY)
     in_vmem = pl.BlockSpec(memory_space=pltpu.VMEM)
-    return pl.pallas_call(
+    made = pl.pallas_call(
         functools.partial(kernel, counts),
         out_shape=(pltpu.VMEM(fine, F32), pltpu.VMEM(coarse, F32)),
         in_specs=[anywhere] * 9,
@@ -806,23 +922,33 @@
             vmem(2, yf + yc, LANES), vmem(2, 2, yf + yc, LANES),
             vmem(2, 2, 3, zf + zc // 2, 1, xf), vmem(2, 2, 3, zf + zc // 2, 1, xf),
             vmem(9, 3, yf + 2 * PAD, xf + LANES), vmem(9, 3, yc + 2 * PAD, xc + LANES),
-            vmem(2, 31, 1, xf), vmem(2, 31, 1, xf), vmem(2, 31, 1, xc), vmem(2, 31, 1, xc),
+            vmem(2, 25, 1, xf), vmem(2, 25, 1, xf), vmem(2, 31, 1, xc), vmem(2, 31, 1, xc),
             vmem(yf, LANES), vmem(2, yf + 2 * PAD, LANES), vmem(yc, LANES), vmem(2, yc + 2 * PAD, LANES),
-            vmem(2, 2, 3, 2, 1, xf), vmem(2, 2, 3, 2, 1, xf), vmem(2, 2, 3, 2, 1, xc), vmem(2, 2, 3, 2, 1, xc),
+            vmem(2, 18, 1, LANES), vmem(2, 3, 18, 1, LANES), vmem(2, 3, 12, 1, LANES),
+            vmem(2, 12, 1, LANES), vmem(2, 3, 12, 1, LANES), vmem(2, 3, 6, 1, LANES),
+            vmem(2, 3, zf + zc // 2, 1, xf), vmem(2, 3, zf + zc // 2, 1, xf),
             vmem(2, yf, LANES), vmem(2, yf, LANES), vmem(18, 24, LANES), vmem(9, yc, LANES), vmem(12, yc, LANES),
-            vmem(2, 12, 1, LANES), vmem(2, 12, 1, LANES),
             vmem(2, 9, 2, LANES), vmem(2, 9, 2, LANES),
             vmem(24, LANES), vmem(2, 24, LANES), vmem(2, 24, LANES),
             vmem(24, 24, 2 * LANES),
             pltpu.SemaphoreType.DMA((10,)),
-            pltpu.SemaphoreType.DMA((21,)),
-            pltpu.SemaphoreType.DMA((35,)),
+            pltpu.SemaphoreType.DMA((37,)),
+            pltpu.SemaphoreType.DMA((43,)),
         ],
         compiler_params=pltpu.CompilerParams(
             collective_id=0, has_side_effects=True, vmem_limit_bytes=56 * 1024 * 1024
         ),
         name="elastic_step",
     )(*args)
+    made = [pltpu.with_memory_space_constraint(part, pltpu.VMEM) for part in made]
+    return pl.pallas_call(
+        write_out,
+        out_shape=(jax.ShapeDtypeStruct(fine, F32), jax.ShapeDtypeStruct(coarse, F32)),
+        in_specs=[in_vmem, in_vmem],
+        out_specs=(anywhere, anywhere),
+        scratch_shapes=[pltpu.SemaphoreType.DMA((2,))],
+        name="write_out",
+    )(*made)
 
 
 def solution(mesh):

time: 29.6 us -> 25.5 us (0.86)
  the two profiles are of different devices: /device:TPU:122 before, /device:TPU:25 now
where the time goes in v4:
time: 25.5 us; the launch traced here: 25 us
  Pallas kernels  24.4 us (96%)
  between operations  0.64 us (3%)
    pallas_call x1, Pallas kernels, per_device(): pl.pallas_call(functools.partial(kernel, counts), out_shape=(pltpu.VMEM(f...  23.7 us
    pallas_call x1, Pallas kernels, per_device(): pl.pallas_call(write_out, out_shape=(jax.ShapeDtypeStruct(fine, F32), jax...  0.72 us

profile of v4, /device:TPU:25, one launch (start us, length us, event | category | flops | bytes accessed | tf_op | source)
XLA Modules:
  0.0 25.0 jit_solution(60533190436496607)
XLA Ops:
  0.6 23.7 %elastic_step.1 = (f32[3,4,16,256]{3,2,1,0:T(8,128)S(1)}, f32[3,8,8,128]{3,2,1,0:T(8,128)S(1)}) custom-call(f32[3,4,16,256]{3,2,1,0:T(8,128)} %fn.1, f32[3,4,16,256]{3,2,1,0:T(8,128)} %fp.1, f32[9,4,16,256]{3,2,1,0:T(8,128)} %st.1, f32[4,16,256]{2,1,0:T(8,128)} %me.1, f32[4,16,256]{2,1,0:T(8,128)} %de.1, f32[3,8,8,128]{3,2,1,0:T(8,128)} %cn.1, ...), custom_call_target="tpu_custom_call" | custom-call | tf_op jit(solution)/shard_map/elastic_step/pallas_call | solution.py:910
  24.3 0.7 %write_out.1 = (f32[3,4,16,256]{3,2,1,0:T(8,128)}, f32[3,8,8,128]{3,2,1,0:T(8,128)}) custom-call(f32[3,4,16,256]{3,2,1,0:T(8,128)S(1)} %get-tuple-element.4.fine, f32[3,8,8,128]{3,2,1,0:T(8,128)S(1)} %get-tuple-element.5.coarse), custom_call_target="tpu_custom_call" | custom-call | tf_op jit(solution)/shard_map/write_out/pallas_call | solution.py:944

commit v5 on v4

--- a/solution.py
+++ b/solution.py
@@ -9,7 +9,6 @@
 
 TIME_STEP = 0.2
 ITERS = 3
-SPLIT = False
 F32 = jnp.float32
 XX, XY, YY, XZ, YZ, ZZ = range(6)
 FACE_X = (XX, XY, XZ)
@@ -143,7 +142,7 @@
     u, uc, s, sc, fprev, stiff, metric, dens, cprev, cstiff, cdens,
     xs, xr, ys, yr,
     fwide, cwide, yef_s, yef_r, yec_s, yec_r, xef_s, xef_r, xec_s, xec_r,
-    npf_s, npf_l, npf_o, npc_s, npc_l, npc_o, cs, cr,
+    npf_s, npf_l, npf_o, npc_s, npc_l, npc_o, pe_s, pe_l, pe_o, cs, xd_s, xd_r,
     tiles, sums, own, own_opp, ikf_opp, ys3, yo3, xs3, xr3, xo3, ext,
     load_sem, send_sem, recv_sem,
 ):
@@ -239,16 +238,17 @@
             elif d < 4:
                 for r in range(2):
                     clear(yr.at[r, side])
-                clear(cr.at[side])
                 for g in (fine, coarse):
                     clear(g.ye_r.at[side])
-                    for b in range(2):
-                        clear(g.xe_r.at[b, pl.ds(0 if side == 0 else PAD + g.y, PAD)])
+                for b in range(2):
+                    clear(xd_r.at[b, side])
             else:
                 for r in range(2):
                     clear(xr.at[r, side])
                 for g in (fine, coarse):
                     clear(g.xe_r.at[side])
+                for b in range(2):
+                    clear(xd_r.at[side, b])
 
     def rdma(src, dst, out, into, device):
         return pltpu.make_async_remote_copy(
@@ -311,10 +311,6 @@
         xs[r, 0:yf] = pack_x(refs[0], face_x, zf, yf, xf)
         xs[r, yf : yf + yc] = pack_x(refs[1], face_x, zc, yc, xc)
 
-    stiff_rows = [
-        (has_y[a], has_y[-a], rdma(cs.at[i], cr.at[1 - i], 23 + i, 35 + i, (gz, gy + a, gx))) for i, a in enumerate((-1, 1))
-    ]
-
     def pack_stiff_rows():
         half = zc // 2
         for i, c in enumerate(EDGE_Y):
@@ -328,9 +324,9 @@
                     ]
 
     def complete_rows():
-        for side, sign in enumerate((1.0, -1.0)):
+        for side, sign in enumerate((-1.0, 1.0)):
             for g, part in ((fine, slice(0, zf)), (coarse, slice(zf, zf + zc // 2))):
-                yr[1, side, :, part] = yr[1, side, :, part] + cr[side, :, part] * ys[0, side, :, part] * (sign * g.inv)
+                ys[1, side, :, part] = ys[1, side, :, part] + cs[side, :, part] * yr[0, side, :, part] * (sign * g.inv)
 
     def unpack_rows(r, g, ref, face_y):
         for side, row in enumerate((PAD - 1, PAD + g.y)):
@@ -366,6 +362,8 @@
                 tile = jnp.where(lane >= LANES // 2, last, tile)
             packed = jnp.where(lane // 4 == k, pltpu.roll(tile, 4 * k + 2, 1), packed)
         g.xe_s[...] = packed
+        xd_s[0] = packed[0:1]
+        xd_s[1] = packed[g.y - 1 : g.y]
 
     def wide_blocks(g):
         blocks = [(g.u, (c, g.near + l + 1)) for c in range(3) for l in range(3)]
@@ -381,17 +379,13 @@
         made = []
         for i, b in enumerate((-1, 1)):
             for a in ups:
-                src, dst = {
-                    -1: (slice(0, PAD), slice(PAD + g.y, 2 * PAD + g.y)),
-                    0: (slice(0, g.y), slice(PAD, PAD + g.y)),
-                    1: (slice(g.y - PAD, g.y), slice(0, PAD)),
-                }[a]
+                if a == 0:
+                    src, dst = g.xe_s, g.xe_r.at[1 - i]
+                else:
+                    src, dst = xd_s.at[(a + 1) // 2], xd_r.at[1 - i, (1 - a) // 2]
                 made.append((
                     jnp.logical_and(has_y[a], has_x[b]), jnp.logical_and(has_y[-a], has_x[-b]),
-                    rdma(
-                        g.xe_s.at[src], g.xe_r.at[1 - i, dst], 13 + i * 3 + (a + 1), 21 + i * 3 + (a + 1),
-                        (gz, gy + a, gx + b),
-                    ),
+                    rdma(src, dst, 13 + i * 3 + (a + 1), 21 + i * 3 + (a + 1), (gz, gy + a, gx + b)),
                 ))
         return made
 
@@ -400,15 +394,27 @@
         for i, a in enumerate((-1, 1)):
             for b in (-1, 0, 1):
                 k = 3 * i + b + 1
+                if b == 0:
+                    src, dst = g.np_s.at[i], g.np_l.at[1 - i]
+                else:
+                    src, dst = pe_s.at[i], pe_l.at[1 - i, (1 - b) // 2]
                 made.append((
                     jnp.logical_and(has_y[a], has_x[b]), jnp.logical_and(has_y[-a], has_x[-b]),
-                    rdma(g.np_s.at[i], g.np_l.at[1 - i, 1 - b], 25 + k, 37 + k, (gz, gy + a, gx + b)),
+                    rdma(src, dst, 25 + k, 35 + k, (gz, gy + a, gx + b)),
                 ))
         return made
 
+    def pack_parts(g, count):
+        lane1 = lanes_of(1)
+        for side in range(2):
+            packed = jnp.zeros((1, LANES), F32)
+            for k in range(count):
+                packed = jnp.where(lane1 // 4 == k, pltpu.roll(g.np_s[side, k], 4 * k + 2, 1), packed)
+            pe_s[side] = packed
+
     def passed_parts(g):
-        source, target = (npf_l.at[:, :, 0:6], npc_o) if g is fine else (npc_l, npf_o)
-        return rdma(source, target, 9, 17, (opp, gy, gx))
+        source, target = (npf_l.at[:, 0:6], npc_o) if g is fine else (npc_l, npf_o)
+        return [(active, active, rdma(source, target, 9, 17, (opp, gy, gx))), (active, active, rdma(pe_l, pe_o, 10, 18, (opp, gy, gx)))]
 
     def squeeze_rows(row_of):
         for side in range(2):
@@ -432,11 +438,15 @@
             for i, c in enumerate(WIDE_Y):
                 g.wide[c, :, edge : edge + 1, 0 : g.x] = landed[6 + 3 * i : 9 + 3 * i]
 
-    def unpack_wide_columns(g, row, count):
-        rows = slice(row, row + count)
-        both = jnp.where(lanes_of(count) % 4 < 2, g.xe_r[0, rows], g.xe_r[1, rows])
+    def unpack_wide_columns(g, corners):
+        own_rows = (slice(PAD, PAD + g.y), jnp.where(lanes_of(g.y) % 4 < 2, g.xe_r[0], g.xe_r[1]))
+        rows = [own_rows]
+        if corners:
+            for side, row in enumerate((PAD - 1, PAD + g.y)):
+                rows.append((slice(row, row + 1), jnp.where(lanes_of(1) % 4 < 2, xd_r[0, side], xd_r[1, side])))
         for k, (ref, index) in enumerate(wide_blocks(g)):
-            ref[index + (rows, slice(g.x, g.x + LANES))] = pltpu.roll(both, LANES - (4 * k + 2), 1)
+            for where, both in rows:
+                ref[index + (where, slice(g.x, g.x + LANES))] = pltpu.roll(both, LANES - (4 * k + 2), 1)
 
     def interface_step(g):
         stress_block(g.u, g.stiff, g.s, g.near + g.third, 1, g.y, g.x, g.inv, 1.0)
@@ -539,8 +549,7 @@
         start_round(0, (4, 5, 0, 1))
         for load in loads[4:]:
             load.wait()
-        if SPLIT:
-            pack_stiff_rows()
+        pack_stiff_rows()
 
     lane = lanes_of(yc)
     even = (2 * lane) % LANES
@@ -548,25 +557,36 @@
     def squeeze(left, right, odd):
         return jnp.where(lane < LANES // 2, pick(left, even + odd), pick(right, even + odd))
 
-    ikf_copy = rdma(own.at[6:18, 8:16], ikf_opp, 8, 16, (opp, gy, gx))
+    ikf_copy = rdma(own.at[6:18, 0:8], ikf_opp, 8, 16, (opp, gy, gx))
     @pl.when(is_f)
     def _():
         for c in range(3):
             inverse = 1.0 / stiff[CH[c], zf - 1]
             for t in range(2):
-                tiles[t] = inverse[:, t * LANES : (t + 1) * LANES]
+                tiles[c, t] = inverse[:, t * LANES : (t + 1) * LANES]
             for py in range(2):
                 rows = pl.ds(py, yc, stride=2)
-                left, right = tiles[0, rows, :], tiles[1, rows, :]
+                left, right = tiles[c, 0, rows, :], tiles[c, 1, rows, :]
                 for px in range(2):
-                    own[6 + c * 4 + py * 2 + px, 8:16] = squeeze(left, right, px)
-
-    k_copy = rdma(own.at[6:9, 8:16], own_opp.at[6:9], 8, 16, (opp, gy, gx))
+                    own[6 + c * 4 + py * 2 + px, 0:8] = squeeze(left, right, px)
+
+    k_copy = rdma(own.at[6:9, 0:8], own_opp.at[6:9], 8, 16, (opp, gy, gx))
 
     @pl.when(is_c)
     def _():
         for c in range(3):
-            own[6 + c, 8:16] = cstiff[CH[c], 0] * 0.25
+            own[6 + c, 0:8] = cstiff[CH[c], 0] * 0.25
+
+    def pack_own(first, last):
+        lane4 = lanes_of(16) // 4
+        packed = xs3[...]
+        for k in range(first, last):
+            packed = jnp.where(lane4 == k, pltpu.roll(own[k], 4 * k + 2, 1), packed)
+        xs3[...] = packed
+
+    @pl.when(is_f)
+    def _():
+        pack_own(6, 18)
 
     with jax.named_scope("wait_part"):
         for there, g in sides:
@@ -577,7 +597,7 @@
     for there, g in sides:
         @pl.when(there)
         def _(g=g):
-            unpack_wide_columns(g, PAD, g.y)
+            unpack_wide_columns(g, False)
             interface_step(g)
 
     @pl.when(is_f)
@@ -588,11 +608,12 @@
             row = (0, yf - 2)[side]
             return fout[c, first : first + 2, row : row + 1, :] + fout[c, first : first + 2, row + 1 : row + 2, :]
 
-        tiles[0] = squeeze_rows(two_rows)
+        squeezed = squeeze_rows(two_rows)
         for side in range(2):
             for k in range(6):
-                npf_s[side, k] = tiles[0, side * 6 + k : side * 6 + k + 1]
-            npf_s[side, 6:18] = own[6:18, (8, yc + 7)[side] : (9, yc + 8)[side], :]
+                npf_s[side, k] = squeezed[side * 6 + k : side * 6 + k + 1]
+            npf_s[side, 6:18] = own[6:18, (0, yc - 1)[side] : (1, yc)[side], :]
+        pack_parts(fine, 18)
         start_all(part_rows(fine))
         ikf_copy.start()
 
@@ -603,8 +624,9 @@
                 row = (i, yc - 1 - i)[side]
                 for c in range(3):
                     start, below = cout[c, 0, row : row + 1, :], cout[c, 1, row : row + 1, :]
-                    npc_s[side, 6 * i + c] = own[6 + c, 8 + row : 9 + row] * (below - start)
+                    npc_s[side, 6 * i + c] = own[6 + c, row : row + 1] * (below - start)
                     npc_s[side, 6 * i + 3 + c] = below - 0.5 * start
+        pack_parts(coarse, 12)
         start_all(part_rows(coarse))
         k_copy.start()
 
@@ -623,22 +645,18 @@
         end_round(0, (4, 5, 0, 1))
     with jax.named_scope("part_stress"):
         unpack_columns(0, (u, uc), (0, 1, 2))
-        if SPLIT:
-            stress_all()
-            pack_rows(1, (s, sc), FACE_Y)
-            start_round(1, (2, 3))
-            start_all(stiff_rows)
+        stress_all()
+        pack_rows(1, (s, sc), FACE_Y)
 
     with jax.named_scope("wait_rows"):
         end_round(0, (2, 3))
+        complete_rows()
+        start_round(1, (2, 3))
         unpack_rows(0, fine, u, (0, 1, 2))
         unpack_rows(0, coarse, uc, (0, 1, 2))
 
     with jax.named_scope("stress"):
         stress_all()
-        if not SPLIT:
-            pack_rows(1, (s, sc), FACE_Y)
-            start_round(1, (2, 3))
         pack_columns(1, (s, sc), FACE_X)
         start_round(1, (4, 5, 0, 1))
 
@@ -653,15 +671,15 @@
         @pl.when(there)
         def _(g=g):
             unpack_wide_rows(g)
-            unpack_wide_columns(g, 0, 2 * PAD + g.y)
+            unpack_wide_columns(g, True)
             interface_step(g)
 
     @pl.when(is_c)
     def _():
         for c in range(3):
             start, below = cout[c, 0], cout[c, 1]
-            own[c, 8:16] = own[6 + c, 8:16] * (below - start)
-            own[3 + c, 8:16] = below - 0.5 * start
+            own[c, 0:8] = own[6 + c, 0:8] * (below - start)
+            own[3 + c, 0:8] = below - 0.5 * start
 
     @pl.when(is_f)
     def _():
@@ -669,17 +687,18 @@
             for i, z in enumerate((zf - 2, zf - 1)):
                 plane = fout[c, z]
                 pairs = []
+                k = 3 * i + c
                 for t in range(2):
-                    tiles[t] = plane[:, t * LANES : (t + 1) * LANES]
-                    pair = tiles[t, pl.ds(0, yc, stride=2), :] + tiles[t, pl.ds(1, yc, stride=2), :]
+                    tiles[k, t] = plane[:, t * LANES : (t + 1) * LANES]
+                    pair = tiles[k, t, pl.ds(0, yc, stride=2), :] + tiles[k, t, pl.ds(1, yc, stride=2), :]
                     pairs.append(pair + pltpu.roll(pair, LANES - 1, 1))
-                own[3 * i + c, 8:16] = squeeze(pairs[0], pairs[1], 0) * 0.25
+                own[3 * i + c, 0:8] = squeeze(pairs[0], pairs[1], 0) * 0.25
 
     @pl.when(is_c)
     def _():
         for side, rows in enumerate(beyond_edges(coarse)):
             for i in range(2):
-                place = (7 - i) if side == 0 else (16 + i)
+                place = (15 - i) if side == 0 else (8 + i)
                 for c in range(3):
                     start, below = rows[i][c][0], rows[i][c][1]
                     k = yec_r[side, 25 + 3 * i + c] * 0.25
@@ -690,15 +709,15 @@
     @pl.when(is_f)
     def _():
         beyond = beyond_edges(fine)
-        tiles[0] = squeeze_rows(lambda side, c: beyond[side][0][c] + beyond[side][1][c])
-        for side, place in enumerate((7, 16)):
+        squeezed = squeeze_rows(lambda side, c: beyond[side][0][c] + beyond[side][1][c])
+        for side, place in enumerate((15, 8)):
             for k in range(6):
-                own[k, place : place + 1] = tiles[0, side * 6 + k : side * 6 + k + 1]
-
-    fields = 18
+                own[k, place : place + 1] = squeezed[side * 6 + k : side * 6 + k + 1]
+
     strips = [
-        (active, active, rdma(own.at[0:6, 8:16], own_opp.at[0:6], 13, 29, (opp, gy, gx))),
-        (active, active, rdma(ys3, yo3, 14, 30, (opp, gy, gx))),
+        (active, active, rdma(own.at[0:6, 0:8], own_opp.at[0:6], 13, 29, (opp, gy, gx))),
+        (is_f, is_c, rdma(ys3.at[:, 3:6], yo3.at[:, 3:6], 14, 30, (opp, gy, gx))),
+        (is_c, is_f, rdma(ys3, yo3, 14, 30, (opp, gy, gx))),
     ]
     for level, tile_to, out, into in ((opp, xo3, 15, 33), (gz, xr3, 17, 31)):
         for i, b in enumerate((-1, 1)):
@@ -706,17 +725,17 @@
                 jnp.logical_and(active, has_x[b]), jnp.logical_and(active, has_x[-b]),
                 rdma(xs3, tile_to.at[1 - i], out + i, into + i, (level, gy, gx + b)),
             ))
-    opp_strips, level_strips = strips[:4], strips[4:]
+    opp_strips, level_strips = strips[:5], strips[5:]
+
+    for there, first, last in ((is_f, 0, 6), (is_c, 0, 9)):
+        @pl.when(there)
+        def _(first=first, last=last):
+            pack_own(first, last)
 
     @pl.when(active)
     def _():
-        ys3[0] = own[0:9, 6:8, :]
-        ys3[1] = own[0:9, 16:18, :]
-        packed = jnp.zeros((24, LANES), F32)
-        lane4 = lanes_of(24) // 4
-        for k in range(fields):
-            packed = jnp.where(lane4 == k, pltpu.roll(own[k], 4 * k + 2, 1), packed)
-        xs3[...] = packed
+        ys3[0] = own[0:9, 14:16, :]
+        ys3[1] = own[0:9, 8:10, :]
 
     for there, g in sides:
         @pl.when(there)
@@ -730,40 +749,53 @@
             @pl.when(there)
             def _(g=g):
                 receive_all(part_rows(g))
-                passed_parts(g).start()
+                start_all(passed_parts(g))
 
     with jax.named_scope("wait_1"):
-        end_round(1, (0, 1, 4, 5, 2, 3))
-        if SPLIT:
-            receive_all(stiff_rows)
-            complete_rows()
+        end_round(1, (4, 5, 0, 1))
     with jax.named_scope("step"):
-        unpack_rows(1, fine, s, FACE_Y)
-        unpack_rows(1, coarse, sc, FACE_Y)
+        for g in (fine, coarse):
+            for row in (PAD - 1, PAD + g.y):
+                for c in FACE_Y:
+                    clear(g.s.at[c, 1 : g.z + 1, row : row + 1, 0 : g.x])
         unpack_columns(1, (s, sc), FACE_X)
         for z in range(zf):
             step_block(u, s, fprev, dens, fout, z, 1, yf, xf, 0.5, stretch_of(z))
         for z in range(0, zc, zb):
             step_block(uc, sc, cprev, cdens, cout, z, zb, yc, xc, 0.25, 1.0)
-
-    lane24 = lax.broadcasted_iota(jnp.int32, (24, LANES), 1)
-    wide_row = lax.broadcasted_iota(jnp.int32, (24, 2 * LANES), 0)
-    wide_lane = lax.broadcasted_iota(jnp.int32, (24, 2 * LANES), 1)
+    with jax.named_scope("wait_rows_1"):
+        end_round(1, (2, 3))
+        half = zc // 2
+        for side, sign in enumerate((-1.0, 1.0)):
+            row = (0, yf - 1)[side]
+            gain = (sign * 0.5 * TIME_STEP * TIME_STEP) / dens[:, row : row + 1, :]
+            for c in range(3):
+                fout[c, :, row : row + 1, :] += gain * yr[1, side, c, 0:zf]
+            row = (0, yc - 1)[side]
+            gain = (sign * 0.25 * TIME_STEP * TIME_STEP) / cdens[:, row : row + 1, :]
+            for j in range(2):
+                part, cols = slice(j * half, (j + 1) * half), slice(j * xc, (j + 1) * xc)
+                for c in range(3):
+                    cout[c, part, row : row + 1, :] += gain[part] * yr[1, side, c, zf : zf + half, :, cols]
+
+    lane16 = lanes_of(16)
+    wide_row = lax.broadcasted_iota(jnp.int32, (16, 2 * LANES), 0)
+    wide_lane = lax.broadcasted_iota(jnp.int32, (16, 2 * LANES), 1)
 
     def extend(k, field, centre, rims, row, edges):
-        ext[k, 8:16, 0:LANES] = centre
-        ext[k, 6:8, 0:LANES] = rims[0, row]
-        ext[k, 16:18, 0:LANES] = rims[1, row]
+        ext[k, 0:8, 0:LANES] = centre
+        ext[k, 14:16, 0:LANES] = rims[0, row]
+        ext[k, 8:10, 0:LANES] = rims[1, row]
         ext[k, :, LANES : 2 * LANES] = pltpu.roll(edges, LANES - (4 * field + 2), 1)
 
     def clamp(t):
-        t = jnp.where(jnp.logical_and(wide_row == 7, gy == 0), pltpu.roll(t, 23, 0), t)
-        t = jnp.where(jnp.logical_and(wide_row == 16, gy == n_y - 1), pltpu.roll(t, 1, 0), t)
+        t = jnp.where(jnp.logical_and(wide_row == 15, gy == 0), pltpu.roll(t, 15, 0), t)
+        t = jnp.where(jnp.logical_and(wide_row == 8, gy == n_y - 1), pltpu.roll(t, 1, 0), t)
         t = jnp.where(jnp.logical_and(wide_lane == 2 * LANES - 1, gx == 0), pltpu.roll(t, 2 * LANES - 1, 1), t)
         return jnp.where(jnp.logical_and(wide_lane == LANES, gx == n_x - 1), pltpu.roll(t, 1, 1), t)
 
     def along_y(t):
-        return (0.75 * t + 0.25 * pltpu.roll(t, 1, 0), 0.75 * t + 0.25 * pltpu.roll(t, 23, 0))
+        return (0.75 * t + 0.25 * pltpu.roll(t, 1, 0), 0.75 * t + 0.25 * pltpu.roll(t, 15, 0))
 
     def along_x(t):
         return (0.75 * t + 0.25 * pltpu.roll(t, 1, 1), 0.75 * t + 0.25 * pltpu.roll(t, 2 * LANES - 1, 1))
@@ -777,14 +809,14 @@
 
     @pl.when(is_c)
     def _():
-        edges = jnp.where(lane24 % 4 < 2, xr3[0], xr3[1])
+        edges = jnp.where(lane16 % 4 < 2, xr3[0], xr3[1])
         for k in range(3, 9):
             extend_own(k, k, edges)
         ikf_copy.wait_recv()
 
     @pl.when(is_f)
     def _():
-        edges = jnp.where(lane24 % 4 < 2, xr3[0], xr3[1])
+        edges = jnp.where(lane16 % 4 < 2, xr3[0], xr3[1])
         for k in range(3):
             extend_own(9 + k, k, edges)
         for k in range(12):
@@ -797,17 +829,17 @@
         for there, g in sides:
             @pl.when(there)
             def _(g=g):
-                passed_parts(coarse if g is fine else fine).wait_recv()
-
-    def part_of(parts, side, field):
-        edges = jnp.where(lanes_of(1) < LANES // 2, parts[side, 2, field], parts[side, 0, field])
-        return jnp.concatenate([parts[side, 1, field], edges], 1)
-
-    def add_part(k, parts, side, field, place):
-        ext[k, place : place + 1] += part_of(parts, side, field)
-
-    def set_part(k, parts, side, field, place):
-        ext[k, place : place + 1] = part_of(parts, side, field)
+                receive_all(passed_parts(coarse if g is fine else fine))
+
+    def part_of(parts, rims, side, field):
+        edges = jnp.where(lanes_of(1) % 4 < 2, rims[side, 0], rims[side, 1])
+        return jnp.concatenate([parts[side, field], pltpu.roll(edges, LANES - (4 * field + 2), 1)], 1)
+
+    def add_part(k, parts, rims, side, field, place):
+        ext[k, place : place + 1] += part_of(parts, rims, side, field)
+
+    def set_part(k, parts, rims, side, field, place):
+        ext[k, place : place + 1] = part_of(parts, rims, side, field)
 
     @pl.when(is_f)
     def _():
@@ -815,49 +847,49 @@
 
     @pl.when(is_c)
     def _():
-        edges = jnp.where(lane24 % 4 < 2, xo3[0], xo3[1])
+        edges = jnp.where(lane16 % 4 < 2, xo3[0], xo3[1])
         for c in range(3):
             extend(9 + c, 3 + c, own_opp[3 + c], yo3, 3 + c, edges)
-            for side, place in enumerate((7, 16)):
-                add_part(9 + c, npc_o, side, 3 + c, place)
-                add_part(3 + c, npc_l, side, 3 + c, place)
+            for side, place in enumerate((15, 8)):
+                add_part(9 + c, npc_o, pe_o, side, 3 + c, place)
+                add_part(3 + c, npc_l, pe_l, side, 3 + c, place)
             t1 = clamp(ext[6 + c] * (ext[3 + c] - 0.5 * ext[9 + c]))
             total = jnp.zeros((yc, LANES), F32)
             for py, part in enumerate(along_y(t1)):
-                for px, full in enumerate(along_x(part[8:16])):
+                for px, full in enumerate(along_x(part[0:8])):
                     total += full[:, 0:LANES] * ikf_opp[c * 4 + py * 2 + px]
             cout[c, 0] = 0.5 * (cout[c, 0] + own_opp[c] + 0.25 * total)
 
     @pl.when(is_f)
     def _():
-        edges = jnp.where(lane24 % 4 < 2, xo3[0], xo3[1])
+        edges = jnp.where(lane16 % 4 < 2, xo3[0], xo3[1])
         half = lane // 2
         for c in range(3):
             for k in (c, 3 + c, 6 + c):
                 extend(k, k, own_opp[k], yo3, k, edges)
-            for side, (place, after) in enumerate(((7, 6), (16, 17))):
-                add_part(c, npf_o, side, c, place)
-                add_part(c, npf_o, side, 6 + c, after)
-                add_part(3 + c, npf_o, side, 3 + c, place)
-                add_part(9 + c, npf_l, side, c, place)
+            for side, (place, after) in enumerate(((15, 14), (8, 9))):
+                add_part(c, npf_o, pe_o, side, c, place)
+                add_part(c, npf_o, pe_o, side, 6 + c, after)
+                add_part(3 + c, npf_o, pe_o, side, 3 + c, place)
+                add_part(9 + c, npf_l, pe_l, side, c, place)
                 for k in range(4 * c, 4 * c + 4):
-                    set_part(12 + k, npf_l, side, 6 + k, place)
-            total = jnp.zeros((24, 2 * LANES), F32)
+                    set_part(12 + k, npf_l, pe_l, side, 6 + k, place)
+            total = jnp.zeros((16, 2 * LANES), F32)
             for py, part in enumerate(along_y(clamp(ext[c]))):
                 for px, full in enumerate(along_x(part)):
                     total += full * ext[12 + c * 4 + py * 2 + px]
             t2 = clamp(ext[6 + c] * (ext[3 + c] - 0.5 * (ext[9 + c] + 0.25 * total)))
             for py, part in enumerate(along_y(t2)):
-                evens, odds = along_x(part[8:16])
+                evens, odds = along_x(part[0:8])
                 evens, odds = evens[:, 0:LANES], odds[:, 0:LANES]
                 for t in range(2):
                     index = half + t * (LANES // 2)
-                    tiles[t, pl.ds(py, yc, stride=2), :] = jnp.where(
+                    tiles[c, t, pl.ds(py, yc, stride=2), :] = jnp.where(
                         lane % 2 == 0, pick(evens, index), pick(odds, index)
                     )
             for t in range(2):
                 cols = slice(t * LANES, (t + 1) * LANES)
-                fout[c, zf - 1, :, cols] = fout[c, zf - 2, :, cols] + tiles[t] / stiff[CH[c], zf - 1, :, cols]
+                fout[c, zf - 1, :, cols] = fout[c, zf - 2, :, cols] + tiles[c, t] / stiff[CH[c], zf - 1, :, cols]
 
     with jax.named_scope("drain"):
         for d in range(6):
@@ -870,15 +902,13 @@
             def _(d=d):
                 for copy in round_copies(0, d):
                     copy.wait_send()
-        if SPLIT:
-            sent_all(stiff_rows)
         sent_all(strips)
         for there, g in sides:
             @pl.when(there)
             def _(g=g):
                 sent_all(wide_rows(g))
                 sent_all(part_rows(g))
-                passed_parts(g).wait_send()
+                sent_all(passed_parts(g))
 
         @pl.when(is_f)
         def _():
@@ -923,17 +953,18 @@
             vmem(2, 2, 3, zf + zc // 2, 1, xf), vmem(2, 2, 3, zf + zc // 2, 1, xf),
             vmem(9, 3, yf + 2 * PAD, xf + LANES), vmem(9, 3, yc + 2 * PAD, xc + LANES),
             vmem(2, 25, 1, xf), vmem(2, 25, 1, xf), vmem(2, 31, 1, xc), vmem(2, 31, 1, xc),
-            vmem(yf, LANES), vmem(2, yf + 2 * PAD, LANES), vmem(yc, LANES), vmem(2, yc + 2 * PAD, LANES),
-            vmem(2, 18, 1, LANES), vmem(2, 3, 18, 1, LANES), vmem(2, 3, 12, 1, LANES),
-            vmem(2, 12, 1, LANES), vmem(2, 3, 12, 1, LANES), vmem(2, 3, 6, 1, LANES),
-            vmem(2, 3, zf + zc // 2, 1, xf), vmem(2, 3, zf + zc // 2, 1, xf),
-            vmem(2, yf, LANES), vmem(2, yf, LANES), vmem(18, 24, LANES), vmem(9, yc, LANES), vmem(12, yc, LANES),
+            vmem(yf, LANES), vmem(2, yf, LANES), vmem(yc, LANES), vmem(2, yc, LANES),
+            vmem(2, 18, 1, LANES), vmem(2, 18, 1, LANES), vmem(2, 12, 1, LANES),
+            vmem(2, 12, 1, LANES), vmem(2, 12, 1, LANES), vmem(2, 6, 1, LANES),
+            vmem(2, 1, LANES), vmem(2, 2, 1, LANES), vmem(2, 2, 1, LANES),
+            vmem(2, 3, zf + zc // 2, 1, xf), vmem(2, 1, LANES), vmem(2, 2, 1, LANES),
+            vmem(6, 2, yf, LANES), vmem(2, 16, LANES), vmem(18, 16, LANES), vmem(9, yc, LANES), vmem(12, yc, LANES),
             vmem(2, 9, 2, LANES), vmem(2, 9, 2, LANES),
-            vmem(24, LANES), vmem(2, 24, LANES), vmem(2, 24, LANES),
-            vmem(24, 24, 2 * LANES),
+            vmem(16, LANES), vmem(2, 16, LANES), vmem(2, 16, LANES),
+            vmem(24, 16, 2 * LANES),
             pltpu.SemaphoreType.DMA((10,)),
             pltpu.SemaphoreType.DMA((37,)),
-            pltpu.SemaphoreType.DMA((43,)),
+            pltpu.SemaphoreType.DMA((41,)),
         ],
         compiler_params=pltpu.CompilerParams(
             collective_id=0, has_side_effects=True, vmem_limit_bytes=56 * 1024 * 1024

time: 25.5 us -> 24.4 us (0.957)
  Pallas kernels: 24.4 us -> 23.4 us
    pallas_call x1, Pallas kernels: 23.7 us -> 22.7 us  [per_device(): pl.pallas_call(functools.partial(kernel, counts), out_shape=(pltpu.VMEM(f...]
where the time goes in v5:
time: 24.4 us; the launch traced here: 24.1 us
  Pallas kernels  23.4 us (96%)
  between operations  0.64 us (3%)
    pallas_call x1, Pallas kernels, per_device(): pl.pallas_call(functools.partial(kernel, counts), out_shape=(pltpu.VMEM(f...  22.7 us
    pallas_call x1, Pallas kernels, per_device(): pl.pallas_call(write_out, out_shape=(jax.ShapeDtypeStruct(fine, F32), jax...  0.72 us

profile of v5, /device:TPU:25, one launch (start us, length us, event | category | flops | bytes accessed | tf_op | source)
XLA Modules:
  0.0 24.1 jit_solution(3608573012797377835)
XLA Ops:
  0.6 22.7 %elastic_step.1 = (f32[3,4,16,256]{3,2,1,0:T(8,128)S(1)}, f32[3,8,8,128]{3,2,1,0:T(8,128)S(1)}) custom-call(f32[3,4,16,256]{3,2,1,0:T(8,128)} %fn.1, f32[3,4,16,256]{3,2,1,0:T(8,128)} %fp.1, f32[9,4,16,256]{3,2,1,0:T(8,128)} %st.1, f32[4,16,256]{2,1,0:T(8,128)} %me.1, f32[4,16,256]{2,1,0:T(8,128)} %de.1, f32[3,8,8,128]{3,2,1,0:T(8,128)} %cn.1, ...), custom_call_target="tpu_custom_call" | custom-call | tf_op jit(solution)/shard_map/elastic_step/pallas_call | solution.py:940
  23.4 0.7 %write_out.1 = (f32[3,4,16,256]{3,2,1,0:T(8,128)}, f32[3,8,8,128]{3,2,1,0:T(8,128)}) custom-call(f32[3,4,16,256]{3,2,1,0:T(8,128)S(1)} %get-tuple-element.4.fine, f32[3,8,8,128]{3,2,1,0:T(8,128)S(1)} %get-tuple-element.5.coarse), custom_call_target="tpu_custom_call" | custom-call | tf_op jit(solution)/shard_map/write_out/pallas_call | solution.py:975

commit v6 on v5

--- a/solution.py
+++ b/solution.py
@@ -267,12 +267,12 @@
                 sent, landed = (1, g.z + 1) if side == 0 else (g.z, 0)
                 made.append(rdma(
                     ref.at[comps, sent, g.own[1], g.own[2]], ref.at[comps, landed, g.own[1], g.own[2]],
-                    (0, 31)[r] + 2 * d + i, 8 * r + 2 * d + i, near[d],
+                    (0, 29)[r] + 2 * d + i, 8 * r + 2 * d + i, near[d],
                 ))
             return made
         if d < 4:
             return [rdma(ys.at[r, side], yr.at[r, arrival], (d + 2, d + 19)[r], 8 * r + d + 2, near[d])]
-        return [rdma(xs.at[r], xr.at[r, arrival], (d + 2, d + 31)[r], 8 * r + d + 2, near[d])]
+        return [rdma(xs.at[r], xr.at[r, arrival], (d + 2, d + 29)[r], 8 * r + d + 2, near[d])]
 
     def start_round(r, directions):
         for d in directions:
@@ -400,7 +400,7 @@
                     src, dst = pe_s.at[i], pe_l.at[1 - i, (1 - b) // 2]
                 made.append((
                     jnp.logical_and(has_y[a], has_x[b]), jnp.logical_and(has_y[-a], has_x[-b]),
-                    rdma(src, dst, 25 + k, 35 + k, (gz, gy + a, gx + b)),
+                    rdma(src, dst, 23 + k, 33 + k, (gz, gy + a, gx + b)),
                 ))
         return made
 
@@ -448,8 +448,9 @@
             for where, both in rows:
                 ref[index + (where, slice(g.x, g.x + LANES))] = pltpu.roll(both, LANES - (4 * k + 2), 1)
 
-    def interface_step(g):
-        stress_block(g.u, g.stiff, g.s, g.near + g.third, 1, g.y, g.x, g.inv, 1.0)
+    def interface_step(g, whole):
+        if whole:
+            stress_block(g.u, g.stiff, g.s, g.near + g.third, 1, g.y, g.x, g.inv, 1.0)
         for l in g.slabs:
             stress_ext(g.u, g.wide, g.s, g.near + l, l, g.y, g.x, g.inv)
         for l in g.slabs:
@@ -594,14 +595,10 @@
             def _(g=g):
                 receive_all(wide_columns(g, (0,)))
 
-    for there, g in sides:
-        @pl.when(there)
-        def _(g=g):
-            unpack_wide_columns(g, False)
-            interface_step(g)
-
     @pl.when(is_f)
     def _():
+        unpack_wide_columns(fine, False)
+        interface_step(fine, True)
         first = fine.near + fine.slabs[0]
 
         def two_rows(side, c):
@@ -619,6 +616,8 @@
 
     @pl.when(is_c)
     def _():
+        unpack_wide_columns(coarse, False)
+        interface_step(coarse, True)
         for side in range(2):
             for i in range(2):
                 row = (i, yc - 1 - i)[side]
@@ -641,6 +640,15 @@
         for z in range(0, zc, zb):
             stress_block(uc, cstiff, sc, z, zb, yc, xc, 0.25, 1.0)
 
+    def complete_stress():
+        for g in (fine, coarse):
+            for row, beyond, sign in ((0, PAD - 1, -1.0), (g.y - 1, PAD + g.y, 1.0)):
+                d = [g.u[c, 1 : g.z + 1, beyond : beyond + 1, 0 : g.x] * (sign * g.inv) for c in range(3)]
+                for component, channel, c in ((XX, 6, 1), (YY, 1, 1), (ZZ, 8, 1), (YZ, 3, 2), (XY, 5, 0)):
+                    g.s[component, 1 : g.z + 1, PAD + row : PAD + row + 1, 0 : g.x] += (
+                        g.stiff[channel, :, row : row + 1, :] * d[c]
+                    )
+
     with jax.named_scope("wait_near"):
         end_round(0, (4, 5, 0, 1))
     with jax.named_scope("part_stress"):
@@ -656,7 +664,7 @@
         unpack_rows(0, coarse, uc, (0, 1, 2))
 
     with jax.named_scope("stress"):
-        stress_all()
+        complete_stress()
         pack_columns(1, (s, sc), FACE_X)
         start_round(1, (4, 5, 0, 1))
 
@@ -667,35 +675,20 @@
                 receive_all(wide_rows(g))
                 receive_all(wide_columns(g, (-1, 1)))
 
-    for there, g in sides:
-        @pl.when(there)
-        def _(g=g):
-            unpack_wide_rows(g)
-            unpack_wide_columns(g, True)
-            interface_step(g)
+    def pack_strips(first, last):
+        pack_own(first, last)
+        ys3[0] = own[0:9, 14:16, :]
+        ys3[1] = own[0:9, 8:10, :]
 
     @pl.when(is_c)
     def _():
+        unpack_wide_rows(coarse)
+        unpack_wide_columns(coarse, True)
+        interface_step(coarse, False)
         for c in range(3):
             start, below = cout[c, 0], cout[c, 1]
             own[c, 0:8] = own[6 + c, 0:8] * (below - start)
             own[3 + c, 0:8] = below - 0.5 * start
-
-    @pl.when(is_f)
-    def _():
-        for c in range(3):
-            for i, z in enumerate((zf - 2, zf - 1)):
-                plane = fout[c, z]
-                pairs = []
-                k = 3 * i + c
-                for t in range(2):
-                    tiles[k, t] = plane[:, t * LANES : (t + 1) * LANES]
-                    pair = tiles[k, t, pl.ds(0, yc, stride=2), :] + tiles[k, t, pl.ds(1, yc, stride=2), :]
-                    pairs.append(pair + pltpu.roll(pair, LANES - 1, 1))
-                own[3 * i + c, 0:8] = squeeze(pairs[0], pairs[1], 0) * 0.25
-
-    @pl.when(is_c)
-    def _():
         for side, rows in enumerate(beyond_edges(coarse)):
             for i in range(2):
                 place = (15 - i) if side == 0 else (8 + i)
@@ -705,37 +698,41 @@
                     own[c, place : place + 1] = k * (below - start)
                     own[3 + c, place : place + 1] = below - 0.5 * start
                     own[6 + c, place : place + 1] = k
+        pack_strips(0, 9)
 
     @pl.when(is_f)
     def _():
+        unpack_wide_rows(fine)
+        unpack_wide_columns(fine, True)
+        interface_step(fine, False)
         beyond = beyond_edges(fine)
         squeezed = squeeze_rows(lambda side, c: beyond[side][0][c] + beyond[side][1][c])
+        for c in range(3):
+            for i, z in enumerate((zf - 2, zf - 1)):
+                pairs = []
+                k = 3 * i + c
+                for t in range(2):
+                    tiles[k, t] = fout[c, z, :, t * LANES : (t + 1) * LANES]
+                    pair = tiles[k, t, pl.ds(0, yc, stride=2), :] + tiles[k, t, pl.ds(1, yc, stride=2), :]
+                    pairs.append(pair + pltpu.roll(pair, LANES - 1, 1))
+                own[k, 0:8] = squeeze(pairs[0], pairs[1], 0) * 0.25
         for side, place in enumerate((15, 8)):
             for k in range(6):
                 own[k, place : place + 1] = squeezed[side * 6 + k : side * 6 + k + 1]
+        pack_strips(0, 6)
 
     strips = [
-        (active, active, rdma(own.at[0:6, 0:8], own_opp.at[0:6], 13, 29, (opp, gy, gx))),
-        (is_f, is_c, rdma(ys3.at[:, 3:6], yo3.at[:, 3:6], 14, 30, (opp, gy, gx))),
-        (is_c, is_f, rdma(ys3, yo3, 14, 30, (opp, gy, gx))),
+        (active, active, rdma(own.at[0:6, 0:8], own_opp.at[0:6], 13, 27, (opp, gy, gx))),
+        (is_f, is_c, rdma(ys3.at[:, 3:6], yo3.at[:, 3:6], 14, 28, (opp, gy, gx))),
+        (is_c, is_f, rdma(ys3, yo3, 14, 28, (opp, gy, gx))),
     ]
-    for level, tile_to, out, into in ((opp, xo3, 15, 33), (gz, xr3, 17, 31)):
+    for level, tile_to, out, into in ((opp, xo3, 15, 31), (gz, xr3, 17, 29)):
         for i, b in enumerate((-1, 1)):
             strips.append((
                 jnp.logical_and(active, has_x[b]), jnp.logical_and(active, has_x[-b]),
                 rdma(xs3, tile_to.at[1 - i], out + i, into + i, (level, gy, gx + b)),
             ))
     opp_strips, level_strips = strips[:5], strips[5:]
-
-    for there, first, last in ((is_f, 0, 6), (is_c, 0, 9)):
-        @pl.when(there)
-        def _(first=first, last=last):
-            pack_own(first, last)
-
-    @pl.when(active)
-    def _():
-        ys3[0] = own[0:9, 14:16, :]
-        ys3[1] = own[0:9, 8:10, :]
 
     for there, g in sides:
         @pl.when(there)
@@ -963,8 +960,8 @@
             vmem(16, LANES), vmem(2, 16, LANES), vmem(2, 16, LANES),
             vmem(24, 16, 2 * LANES),
             pltpu.SemaphoreType.DMA((10,)),
-            pltpu.SemaphoreType.DMA((37,)),
-            pltpu.SemaphoreType.DMA((41,)),
+            pltpu.SemaphoreType.DMA((35,)),
+            pltpu.SemaphoreType.DMA((39,)),
         ],
         compiler_params=pltpu.CompilerParams(
             collective_id=0, has_side_effects=True, vmem_limit_bytes=56 * 1024 * 1024

time: 24.4 us -> 24.4 us (level)
  no operation moved by 1% of the time
where the time goes in v6:
time: 24.4 us; the launch traced here: 24 us
  Pallas kernels  23.4 us (96%)
  between operations  0.64 us (3%)
    pallas_call x1, Pallas kernels, per_device(): pl.pallas_call(functools.partial(kernel, counts), out_shape=(pltpu.VMEM(f...  22.7 us
    pallas_call x1, Pallas kernels, per_device(): pl.pallas_call(write_out, out_shape=(jax.ShapeDtypeStruct(fine, F32), jax...  0.72 us

profile of v6, /device:TPU:25, one launch (start us, length us, event | category | flops | bytes accessed | tf_op | source)
XLA Modules:
  0.0 24.0 jit_solution(15995066730520504131)
XLA Ops:
  0.6 22.7 %elastic_step.1 = (f32[3,4,16,256]{3,2,1,0:T(8,128)S(1)}, f32[3,8,8,128]{3,2,1,0:T(8,128)S(1)}) custom-call(f32[3,4,16,256]{3,2,1,0:T(8,128)} %fn.1, f32[3,4,16,256]{3,2,1,0:T(8,128)} %fp.1, f32[9,4,16,256]{3,2,1,0:T(8,128)} %st.1, f32[4,16,256]{2,1,0:T(8,128)} %me.1, f32[4,16,256]{2,1,0:T(8,128)} %de.1, f32[3,8,8,128]{3,2,1,0:T(8,128)} %cn.1, ...), custom_call_target="tpu_custom_call" | custom-call | tf_op jit(solution)/shard_map/elastic_step/pallas_call | solution.py:937
  23.3 0.7 %write_out.1 = (f32[3,4,16,256]{3,2,1,0:T(8,128)}, f32[3,8,8,128]{3,2,1,0:T(8,128)}) custom-call(f32[3,4,16,256]{3,2,1,0:T(8,128)S(1)} %get-tuple-element.4.fine, f32[3,8,8,128]{3,2,1,0:T(8,128)S(1)} %get-tuple-element.5.coarse), custom_call_target="tpu_custom_call" | custom-call | tf_op jit(solution)/shard_map/write_out/pallas_call | solution.py:972

commit v7 on v6

--- a/solution.py
+++ b/solution.py
@@ -392,7 +392,7 @@
     def part_rows(g):
         made = []
         for i, a in enumerate((-1, 1)):
-            for b in (-1, 0, 1):
+            for b in (-1, 1, 0):
                 k = 3 * i + b + 1
                 if b == 0:
                     src, dst = g.np_s.at[i], g.np_l.at[1 - i]
@@ -541,12 +541,12 @@
             @pl.when(there)
             def _(g=g):
                 start_all(wide_columns(g, (0,)))
+                start_all(wide_columns(g, (-1, 1)))
         start_round(0, (2, 3))
         for there, g in sides:
             @pl.when(there)
             def _(g=g):
                 start_all(wide_rows(g))
-                start_all(wide_columns(g, (-1, 1)))
         start_round(0, (4, 5, 0, 1))
         for load in loads[4:]:
             load.wait()

time: 24.4 us -> 24.4 us (level)
  no operation moved by 1% of the time
where the time goes in v7:
time: 24.4 us; the launch traced here: 24 us
  Pallas kernels  23.4 us (96%)
  between operations  0.64 us (3%)
    pallas_call x1, Pallas kernels, per_device(): pl.pallas_call(functools.partial(kernel, counts), out_shape=(pltpu.VMEM(f...  22.7 us
    pallas_call x1, Pallas kernels, per_device(): pl.pallas_call(write_out, out_shape=(jax.ShapeDtypeStruct(fine, F32), jax...  0.72 us

profile of v7, /device:TPU:25, one launch (start us, length us, event | category | flops | bytes accessed | tf_op | source)
XLA Modules:
  0.0 24.0 jit_solution(12084768614484941874)
XLA Ops:
  0.6 22.7 %elastic_step.1 = (f32[3,4,16,256]{3,2,1,0:T(8,128)S(1)}, f32[3,8,8,128]{3,2,1,0:T(8,128)S(1)}) custom-call(f32[3,4,16,256]{3,2,1,0:T(8,128)} %fn.1, f32[3,4,16,256]{3,2,1,0:T(8,128)} %fp.1, f32[9,4,16,256]{3,2,1,0:T(8,128)} %st.1, f32[4,16,256]{2,1,0:T(8,128)} %me.1, f32[4,16,256]{2,1,0:T(8,128)} %de.1, f32[3,8,8,128]{3,2,1,0:T(8,128)} %cn.1, ...), custom_call_target="tpu_custom_call" | custom-call | tf_op jit(solution)/shard_map/elastic_step/pallas_call | solution.py:937
  23.3 0.7 %write_out.1 = (f32[3,4,16,256]{3,2,1,0:T(8,128)}, f32[3,8,8,128]{3,2,1,0:T(8,128)}) custom-call(f32[3,4,16,256]{3,2,1,0:T(8,128)S(1)} %get-tuple-element.4.fine, f32[3,8,8,128]{3,2,1,0:T(8,128)S(1)} %get-tuple-element.5.coarse), custom_call_target="tpu_custom_call" | custom-call | tf_op jit(solution)/shard_map/write_out/pallas_call | solution.py:972
